TPU v7x, 32 devices: a whole 2x2x4 slice. The times are simulated.
32 devices in a mesh: gx: 2 (over y), gy: 4 (over x, core), gz: 4 (over z).
Axes of the slice: x: 2, y: 2, z: 4, core: 2. Of those that a mesh axis runs over, the one named last changes fastest.
Arguments:
- density: float32 [32, 64, 4096], P('gx', 'gy', 'gz'), may hold values from -19 to 19
Outputs:
- potential: float32 [32, 64, 4096], P('gx', 'gy', 'gz')
- coulomb: float32 [64, 64], replicated
All inputs are finite; a program needn't handle non-finite values.
Results may differ from a plain program's by a relative error of at most 0.000057.
Values sent between devices are 32-bit elements; how exact they have to be, the bound alone decides.
No kernel may reach another device: no remote copies, remote signals or barrier semaphores. Data moves between devices by JAX's collectives and lax.ppermute only.
A program may use at most 64 MiB of HBM per device.

v0:
```python
import jax
import jax.numpy as jnp
from jax import lax
from jax.sharding import PartitionSpec as P

PAIRS = 64
LEVELS = 6
COARSE_SWEEPS = 8


OMEGA = 2.0 / 3.0


def extended_2(x, sides, width):
    for axis, dim in sides:
        size, length = (lax.axis_size(axis), x.shape[dim])
        up = [(i, (i + 1) % size) for i in range(size - 1)]
        down = [(j, i) for i, j in up]
        last = lax.slice_in_dim(x, length - width, length, axis=dim)
        initial = lax.slice_in_dim(x, 0, width, axis=dim)
        before = lax.ppermute(last, axis, up)
        after = lax.ppermute(initial, axis, down)
        x = jnp.concatenate([before, x, after], axis=dim)
    return x


def neighbours(padded):
    total = padded[2:, 1:-1, 1:-1] + padded[:-2, 1:-1, 1:-1]
    total = total + padded[1:-1, 2:, 1:-1] + padded[1:-1, :-2, 1:-1]
    return total + padded[1:-1, 1:-1, 2:] + padded[1:-1, 1:-1, :-2]


def apply_inner(padded, factor):
    return factor * (6.0 * padded[1:-1, 1:-1, 1:-1] - neighbours(padded))


def sweep_inner(padded, source, factor):
    return padded[1:-1, 1:-1, 1:-1] + OMEGA * (source - apply_inner(padded, factor)) / (
        6.0 * factor
    )


def zero_rim(current):
    return jnp.pad(current, ((1, 1), (1, 1), (1, 1), (0, 0)))


def restrict(residual):
    size_x, size_y, size_z, count = residual.shape
    grouped = residual.reshape(size_x // 2, 2, size_y // 2, 2, size_z // 2, 2, count)
    return jnp.mean(grouped, axis=(1, 3, 5))


def prolong(correction):
    return jnp.repeat(jnp.repeat(jnp.repeat(correction, 2, axis=0), 2, axis=1), 2, axis=2)


def global_cycle(source, grid_level):
    factor = 0.25 ** (grid_level - 1)
    current = OMEGA * source / (6.0 * factor)
    if grid_level == LEVELS:
        for repeat_no in range(COARSE_SWEEPS - 1):
            current = sweep_inner(zero_rim(current), source, factor)
        return current
    current = sweep_inner(zero_rim(current), source, factor)
    residual = source - apply_inner(zero_rim(current), factor)
    current = current + prolong(global_cycle(restrict(residual), grid_level + 1))
    for repeat_no in range(2):
        current = sweep_inner(zero_rim(current), source, factor)
    return current


def arrange(stacked, block_shape):
    size_x, size_y, size_z, count = block_shape
    devs_x, devs_y, devs_z = (lax.axis_size("gx"), lax.axis_size("gy"), lax.axis_size("gz"))
    grouped = stacked.reshape(devs_x, devs_y, devs_z, size_x, size_y, size_z, count)
    grouped = grouped.transpose(0, 3, 1, 4, 2, 5, 6)
    return grouped.reshape(devs_x * size_x, devs_y * size_y, devs_z * size_z, count)


def own_block(gathered, block_shape):
    size_x, size_y, size_z, count = block_shape
    starts = (
        lax.axis_index("gx") * size_x,
        lax.axis_index("gy") * size_y,
        lax.axis_index("gz") * size_z,
        jnp.int32(0),
    )
    return lax.dynamic_slice(gathered, starts, block_shape)


def edge_mask(length, where, devices):
    position = jnp.arange(length + 2, dtype=jnp.int32) - 1 + where * length
    return (position >= 0) & (position < length * devices)


def inside_mask(block_shape):
    mask_x = edge_mask(block_shape[0], lax.axis_index("gx"), lax.axis_size("gx"))
    mask_y = edge_mask(block_shape[1], lax.axis_index("gy"), lax.axis_size("gy"))
    mask_z = edge_mask(block_shape[2], lax.axis_index("gz"), lax.axis_size("gz"))
    joined = mask_x[:, None, None] & mask_y[None, :, None] & mask_z[None, None, :]
    return joined[..., None].astype(jnp.float32)


def double_sweep(current, source, factor):
    count = current.shape[3]
    extended = extended_2(
        jnp.concatenate([current, source], axis=3), (("gx", 0), ("gy", 1), ("gz", 2)), 2
    )
    source_wide = extended[1:-1, 1:-1, 1:-1, count:]
    swept = sweep_inner(extended[..., :count], source_wide, factor) * inside_mask(current.shape)
    return swept


def distributed(source, grid_level):
    factor = 0.25 ** (grid_level - 1)
    if grid_level == LEVELS - 1:
        stacked = lax.all_gather(source[None], ("gx", "gy", "gz"), axis=0, tiled=True)
        return own_block(global_cycle(arrange(stacked, source.shape), grid_level), source.shape)
    current = OMEGA * source / (6.0 * factor)
    swept = double_sweep(current, source, factor)
    residual = source - apply_inner(swept, factor)
    current = swept[1:-1, 1:-1, 1:-1]
    current = current + prolong(distributed(restrict(residual), grid_level + 1))
    current = sweep_inner(double_sweep(current, source, factor), source, factor)
    return current


def local(density):
    cells_x, cells_y, merged = density.shape
    cells_z = merged // PAIRS
    cells = density.reshape(cells_x, cells_y, cells_z, PAIRS)
    solved = distributed(cells, 1)
    partial_block = jnp.dot(
        cells.reshape(-1, PAIRS).T,
        solved.reshape(-1, PAIRS),
        precision=lax.Precision.HIGHEST,
        preferred_element_type=jnp.float32,
    )
    summed = lax.psum(partial_block, ("gx", "gy", "gz"))
    total_cells = (
        cells_x
        * cells_y
        * cells_z
        * lax.axis_size("gx")
        * lax.axis_size("gy")
        * lax.axis_size("gz")
    )
    coulomb = summed * (4.0 / total_cells)
    return (solved.reshape(cells_x, cells_y, merged), coulomb)


def solution(mesh):
    return jax.shard_map(
        local,
        mesh=mesh,
        in_specs=(P("gx", "gy", "gz"),),
        out_specs=(P("gx", "gy", "gz"), P()),
        check_vma=False,
    )
```

profile of v0, /device:TPU:1, one launch (start us, length us, event | category | flops | bytes accessed | tf_op | source)
XLA Modules:
  0.0 360.6 jit_solution(3952595412670936373)
XLA Ops:
  4.8 4.0 %collective-permute-start = (f32[2,16,16,128]{3,2,1,0:T(8,128)S(1)}, f32[2,16,16,128]{3,2,1,0:T(8,128)S(1)}, u32[]{:S(2)}, u32[]{:S(2)}) collective-permute-start(f32[2,16,16,128]{3,2,1,0:T(8,128)S(1)} %get-tuple-element.22), channel_id=1, source_target_pairs={{0,16},{1,17},{2,18},{3,19},{4,20},{5,21},{6,22},{7,23},{8,24},{9,... | collective-permute-start | bytes 786440 | tf_op jit(solution)/shard_map/ppermute | solution.py:21
  13.7 3.8 %collective-permute-done.1 = f32[2,16,16,128]{3,2,1,0:T(8,128)S(1)} collective-permute-done((f32[2,16,16,128]{3,2,1,0:T(8,128)S(1)}, f32[2,16,16,128]{3,2,1,0:T(8,128)S(1)}, u32[]{:S(2)}, u32[]{:S(2)}) %collective-permute-start.1) | collective-permute-done | bytes 262176 | tf_op jit(solution)/shard_map/ppermute | solution.py:22
  19.8 4.8 %collective-permute-start.2 = (f32[20,2,16,128]{3,2,1,0:T(8,128)S(1)}, f32[20,2,16,128]{3,2,1,0:T(8,128)S(1)}, u32[]{:S(2)}, u32[]{:S(2)}) collective-permute-start(f32[20,2,16,128]{3,2,1,0:T(8,128)S(1)} %get-tuple-element.18), channel_id=1, source_target_pairs={{0,4},{4,8},{8,12},{1,5},{5,9},{9,13},{2,6},{6,10},{10,14},{3,7},{... | collective-permute-start | bytes 983048 | tf_op jit(solution)/shard_map/ppermute | solution.py:21
  28.7 4.4 %collective-permute-done.3 = f32[20,2,16,128]{3,2,1,0:T(8,128)S(1)} collective-permute-done((f32[20,2,16,128]{3,2,1,0:T(8,128)S(1)}, f32[20,2,16,128]{3,2,1,0:T(8,128)S(1)}, u32[]{:S(2)}, u32[]{:S(2)}) %collective-permute-start.3) | collective-permute-done | bytes 327712 | tf_op jit(solution)/shard_map/ppermute | solution.py:22
  42.1 4.1 %collective-permute-done.5 = f32[20,20,2,128]{3,2,1,0:T(2,128)S(1)} collective-permute-done((f32[20,20,2,128]{3,2,1,0:T(2,128)S(1)}, f32[20,20,2,128]{3,2,1,0:T(2,128)S(1)}, u32[]{:S(2)}, u32[]{:S(2)}) %collective-permute-start.5) | collective-permute-done | bytes 409632 | tf_op jit(solution)/shard_map/ppermute | solution.py:22
  49.5 8.6 %fusion.23 = f32[18,18,18,64]{3,2,1,0:T(8,128)S(1)} fusion(f32[16,16,16,64]{3,2,1,0:T(8,128)S(1)} %reshape.351, f32[20,20,2,128]{3,2,1,0:T(2,128)S(1)} %collective-permute-done.4, f32[20,2,16,128]{3,2,1,0:T(8,128)S(1)} %collective-permute-done.3, f32[20,2,16,128]{3,2,1,0:T(8,128)S(1)} %collective-permute-done.2, ...), kind=kLoop, calls=%fused_computation.29 | loop fusion | flops 8584704 | bytes 14570272 | tf_op jit(solution)/shard_map/mul | solution.py:110
  71.0 4.2 %collective-permute-start.8 = (f32[12,2,8,128]{3,2,1,0:T(8,128)S(1)}, f32[12,2,8,128]{3,2,1,0:T(8,128)S(1)}, u32[]{:S(2)}, u32[]{:S(2)}) collective-permute-start(f32[12,2,8,128]{3,2,1,0:T(8,128)S(1)} %get-tuple-element.29), channel_id=1, source_target_pairs={{0,4},{4,8},{8,12},{1,5},{5,9},{9,13},{2,6},{6,10},{10,14},{3,7},{... | collective-permute-start | bytes 294920 | tf_op jit(solution)/shard_map/ppermute | solution.py:21
  77.1 4.0 %collective-permute-done.9 = f32[12,2,8,128]{3,2,1,0:T(8,128)S(1)} collective-permute-done((f32[12,2,8,128]{3,2,1,0:T(8,128)S(1)}, f32[12,2,8,128]{3,2,1,0:T(8,128)S(1)}, u32[]{:S(2)}, u32[]{:S(2)}) %collective-permute-start.9) | collective-permute-done | bytes 98336 | tf_op jit(solution)/shard_map/ppermute | solution.py:22
  98.9 4.7 %collective-permute-start.14 = (f32[8,2,4,128]{3,2,1,0:T(4,128)S(1)}, f32[8,2,4,128]{3,2,1,0:T(4,128)S(1)}, u32[]{:S(2)}, u32[]{:S(2)}) collective-permute-start(f32[8,2,4,128]{3,2,1,0:T(4,128)S(1)} %get-tuple-element.44), channel_id=1, source_target_pairs={{0,4},{4,8},{8,12},{1,5},{5,9},{9,13},{2,6},{6,10},{10,14},{3,7},{... | collective-permute-start | bytes 98312 | tf_op jit(solution)/shard_map/ppermute | solution.py:21
  123.4 4.8 %collective-permute-start.20 = (f32[6,2,2,128]{3,2,1,0:T(2,128)S(1)}, f32[6,2,2,128]{3,2,1,0:T(2,128)S(1)}, u32[]{:S(2)}, u32[]{:S(2)}) collective-permute-start(f32[6,2,2,128]{3,2,1,0:T(2,128)S(1)} %fusion.281), channel_id=1, source_target_pairs={{0,4},{4,8},{8,12},{1,5},{5,9},{9,13},{2,6},{6,10},{10,14},{3,7},{... | collective-permute-start | bytes 36872 | tf_op jit(solution)/shard_map/ppermute | solution.py:21
  143.0 36.2 %all-reduce.11 = f32[2048]{0:T(1024)S(1)} all-reduce(f32[2048]{0:T(1024)S(1)} %multiply_dynamic-update-slice_fusion), channel_id=2, replica_groups=mesh['gx'=2,'gy'=4,'gz'=4] {'gx','gy','gz'}, use_global_device_ids=true, to_apply=%add.11 | all-reduce | flops 2048 | bytes 16384
  180.4 4.3 %collective-permute-start.24 = (f32[2,2,2,128]{3,2,1,0:T(2,128)S(1)}, f32[2,2,2,128]{3,2,1,0:T(2,128)S(1)}, u32[]{:S(2)}, u32[]{:S(2)}) collective-permute-start(f32[2,2,2,128]{3,2,1,0:T(2,128)S(1)} %pad_maximum_fusion.47), channel_id=1, source_target_pairs={{0,16},{1,17},{2,18},{3,19},{4,20},{5,21},{6,22},{7,23},{8,24},{9,... | collective-permute-start | bytes 12296 | tf_op jit(solution)/shard_map/ppermute | solution.py:21
  189.2 5.9 %collective-permute-start.26 = (f32[6,2,2,128]{3,2,1,0:T(2,128)S(1)}, f32[6,2,2,128]{3,2,1,0:T(2,128)S(1)}, u32[]{:S(2)}, u32[]{:S(2)}) collective-permute-start(f32[6,2,2,128]{3,2,1,0:T(2,128)S(1)} %fusion.283), channel_id=1, source_target_pairs={{0,4},{4,8},{8,12},{1,5},{5,9},{9,13},{2,6},{6,10},{10,14},{3,7},{... | collective-permute-start | bytes 36872 | tf_op jit(solution)/shard_map/ppermute | solution.py:21
  214.9 4.8 %collective-permute-start.32 = (f32[8,2,4,128]{3,2,1,0:T(4,128)S(1)}, f32[8,2,4,128]{3,2,1,0:T(4,128)S(1)}, u32[]{:S(2)}, u32[]{:S(2)}) collective-permute-start(f32[8,2,4,128]{3,2,1,0:T(4,128)S(1)} %get-tuple-element.40), channel_id=1, source_target_pairs={{0,4},{4,8},{8,12},{1,5},{5,9},{9,13},{2,6},{6,10},{10,14},{3,7},{... | collective-permute-start | bytes 98312 | tf_op jit(solution)/shard_map/ppermute | solution.py:21
  236.8 4.3 %collective-permute-done.37 = f32[2,8,8,128]{3,2,1,0:T(8,128)S(1)} collective-permute-done((f32[2,8,8,128]{3,2,1,0:T(8,128)S(1)}, f32[2,8,8,128]{3,2,1,0:T(8,128)S(1)}, u32[]{:S(2)}, u32[]{:S(2)}) %collective-permute-start.37) | collective-permute-done | bytes 65568 | tf_op jit(solution)/shard_map/ppermute | solution.py:22
  247.0 4.0 %collective-permute-done.39 = f32[12,2,8,128]{3,2,1,0:T(8,128)S(1)} collective-permute-done((f32[12,2,8,128]{3,2,1,0:T(8,128)S(1)}, f32[12,2,8,128]{3,2,1,0:T(8,128)S(1)}, u32[]{:S(2)}, u32[]{:S(2)}) %collective-permute-start.39) | collective-permute-done | bytes 98336 | tf_op jit(solution)/shard_map/ppermute | solution.py:22
  266.1 4.0 %collective-permute-done.42 = f32[2,16,16,128]{3,2,1,0:T(8,128)S(1)} collective-permute-done((f32[2,16,16,128]{3,2,1,0:T(8,128)S(1)}, f32[2,16,16,128]{3,2,1,0:T(8,128)S(1)}, u32[]{:S(2)}, u32[]{:S(2)}) %collective-permute-start.42) | collective-permute-done | bytes 262176 | tf_op jit(solution)/shard_map/ppermute | solution.py:21
  270.1 4.1 %collective-permute-done.43 = f32[2,16,16,128]{3,2,1,0:T(8,128)S(1)} collective-permute-done((f32[2,16,16,128]{3,2,1,0:T(8,128)S(1)}, f32[2,16,16,128]{3,2,1,0:T(8,128)S(1)}, u32[]{:S(2)}, u32[]{:S(2)}) %collective-permute-start.43) | collective-permute-done | bytes 262176 | tf_op jit(solution)/shard_map/ppermute | solution.py:22
  281.3 4.4 %collective-permute-done.45 = f32[20,2,16,128]{3,2,1,0:T(8,128)S(1)} collective-permute-done((f32[20,2,16,128]{3,2,1,0:T(8,128)S(1)}, f32[20,2,16,128]{3,2,1,0:T(8,128)S(1)}, u32[]{:S(2)}, u32[]{:S(2)}) %collective-permute-start.45) | collective-permute-done | bytes 327712 | tf_op jit(solution)/shard_map/ppermute | solution.py:22
  294.4 4.8 %collective-permute-done.47 = f32[20,20,2,128]{3,2,1,0:T(2,128)} collective-permute-done((f32[20,20,2,128]{3,2,1,0:T(2,128)}, f32[20,20,2,128]{3,2,1,0:T(2,128)}, u32[]{:S(2)}, u32[]{:S(2)}) %collective-permute-start.47) | collective-permute-done | bytes 409632 | tf_op jit(solution)/shard_map/ppermute | solution.py:22
  299.2 4.6 %fusion.11 = f32[20,20,20,128]{3,2,1,0:T(8,128)S(1)} fusion(f32[16,16,16,64]{3,2,1,0:T(8,128)S(1)} %reshape.351, f32[20,20,2,128]{3,2,1,0:T(2,128)} %collective-permute-done.47, f32[20,2,16,128]{3,2,1,0:T(8,128)S(1)} %collective-permute-done.45, f32[2,16,16,128]{3,2,1,0:T(8,128)S(1)} %collective-permute-done.43, f32[16,16,16,64]{3,2,1,0:T(8,128)} %copy-done.4, ...), kind=kLoop, calls=%fused_computation.13 | loop fusion | flops 7168000 | bytes 8192000 | tf_op jit(solution)/shard_map/concatenate | solution.py:23
  303.8 9.5 %fusion.35 = f32[18,18,18,64]{3,2,1,0:T(8,128)S(1)} fusion(f32[16,16,16,64]{3,2,1,0:T(8,128)S(1)} %reshape.351, f32[20,20,2,128]{3,2,1,0:T(2,128)} %collective-permute-done.46, f32[20,2,16,128]{3,2,1,0:T(8,128)S(1)} %collective-permute-done.45, f32[20,2,16,128]{3,2,1,0:T(8,128)S(1)} %collective-permute-done.44, ...), kind=kLoop, calls=%fused_computation.41 | loop fusion | flops 8584704 | bytes 14570272 | tf_op jit(solution)/shard_map/mul | solution.py:110
  319.3 5.2 %convolution_bitcast_fusion = f32[64,64]{0,1:T(8,128)S(1)} fusion(f32[4096,64]{1,0:T(8,128)S(1)} %bitcast.73, f32[4096,64]{1,0:T(8,128)} %reshape_reshape.3), kind=kOutput, calls=%fused_computation.108 | convolution fusion | flops 201326592 | bytes 2113536 | tf_op jit(solution)/shard_map/dot_general | solution.py:133
  324.5 35.4 %psum.7 = f32[64,64]{0,1:T(8,128)S(1)} all-reduce(f32[64,64]{0,1:T(8,128)S(1)} %convolution_bitcast_fusion), channel_id=1, replica_groups=mesh['gx'=2,'gy'=4,'gz'=4] {'gx','gy','gz'}, use_global_device_ids=true, to_apply=%region_6.7 | all-reduce | flops 4096 | bytes 32768 | tf_op jit(solution)/shard_map/psum | solution.py:139
  (235 shorter events, 180.0 us)
Async XLA Ops:
  4.8 8.9 %collective-permute-start = (f32[2,16,16,128]{3,2,1,0:T(8,128)S(1)}, f32[2,16,16,128]{3,2,1,0:T(8,128)S(1)}, u32[]{:S(2)}, u32[]{:S(2)}) collective-permute-start(f32[2,16,16,128]{3,2,1,0:T(8,128)S(1)} %get-tuple-element.22), channel_id=1, source_target_pairs={{0,16},{1,17},{2,18},{3,19},{4,20},{5,21},{6,22},{7,23},{8,24},{9,... | collective-permute-start | bytes 786440 | tf_op jit(solution)/shard_map/ppermute | solution.py:21
  8.8 8.8 %collective-permute-start.1 = (f32[2,16,16,128]{3,2,1,0:T(8,128)S(1)}, f32[2,16,16,128]{3,2,1,0:T(8,128)S(1)}, u32[]{:S(2)}, u32[]{:S(2)}) collective-permute-start(f32[2,16,16,128]{3,2,1,0:T(8,128)S(1)} %get-tuple-element.10), channel_id=1, source_target_pairs={{16,0},{17,1},{18,2},{19,3},{20,4},{21,5},{22,6},{23,7},{24,8},{25... | collective-permute-start | bytes 786440 | tf_op jit(solution)/shard_map/ppermute | solution.py:22
  19.8 8.8 %collective-permute-start.2 = (f32[20,2,16,128]{3,2,1,0:T(8,128)S(1)}, f32[20,2,16,128]{3,2,1,0:T(8,128)S(1)}, u32[]{:S(2)}, u32[]{:S(2)}) collective-permute-start(f32[20,2,16,128]{3,2,1,0:T(8,128)S(1)} %get-tuple-element.18), channel_id=1, source_target_pairs={{0,4},{4,8},{8,12},{1,5},{5,9},{9,13},{2,6},{6,10},{10,14},{3,7},{... | collective-permute-start | bytes 983048 | tf_op jit(solution)/shard_map/ppermute | solution.py:21
  24.7 8.4 %collective-permute-start.3 = (f32[20,2,16,128]{3,2,1,0:T(8,128)S(1)}, f32[20,2,16,128]{3,2,1,0:T(8,128)S(1)}, u32[]{:S(2)}, u32[]{:S(2)}) collective-permute-start(f32[20,2,16,128]{3,2,1,0:T(8,128)S(1)} %get-tuple-element.19), channel_id=1, source_target_pairs={{4,0},{8,4},{12,8},{5,1},{9,5},{13,9},{6,2},{10,6},{14,10},{7,3},{... | collective-permute-start | bytes 983048 | tf_op jit(solution)/shard_map/ppermute | solution.py:22
  34.0 8.1 %collective-permute-start.4 = (f32[20,20,2,128]{3,2,1,0:T(2,128)S(1)}, f32[20,20,2,128]{3,2,1,0:T(2,128)S(1)}, u32[]{:S(2)}, u32[]{:S(2)}) collective-permute-start(f32[20,20,2,128]{3,2,1,0:T(2,128)S(1)} %get-tuple-element.15), channel_id=1, source_target_pairs={{0,1},{1,2},{2,3},{4,5},{5,6},{6,7},{8,9},{9,10},{10,11},{12,13},{... | collective-permute-start | bytes 1228808 | tf_op jit(solution)/shard_map/ppermute | solution.py:21
  37.3 9.0 %collective-permute-start.5 = (f32[20,20,2,128]{3,2,1,0:T(2,128)S(1)}, f32[20,20,2,128]{3,2,1,0:T(2,128)S(1)}, u32[]{:S(2)}, u32[]{:S(2)}) collective-permute-start(f32[20,20,2,128]{3,2,1,0:T(2,128)S(1)} %get-tuple-element.14), channel_id=1, source_target_pairs={{1,0},{2,1},{3,2},{5,4},{6,5},{7,6},{9,8},{10,9},{11,10},{13,12},{... | collective-permute-start | bytes 1228808 | tf_op jit(solution)/shard_map/ppermute | solution.py:22
  71.0 6.2 %collective-permute-start.8 = (f32[12,2,8,128]{3,2,1,0:T(8,128)S(1)}, f32[12,2,8,128]{3,2,1,0:T(8,128)S(1)}, u32[]{:S(2)}, u32[]{:S(2)}) collective-permute-start(f32[12,2,8,128]{3,2,1,0:T(8,128)S(1)} %get-tuple-element.29), channel_id=1, source_target_pairs={{0,4},{4,8},{8,12},{1,5},{5,9},{9,13},{2,6},{6,10},{10,14},{3,7},{... | collective-permute-start | bytes 294920 | tf_op jit(solution)/shard_map/ppermute | solution.py:21
  75.2 5.9 %collective-permute-start.9 = (f32[12,2,8,128]{3,2,1,0:T(8,128)S(1)}, f32[12,2,8,128]{3,2,1,0:T(8,128)S(1)}, u32[]{:S(2)}, u32[]{:S(2)}) collective-permute-start(f32[12,2,8,128]{3,2,1,0:T(8,128)S(1)} %get-tuple-element.30), channel_id=1, source_target_pairs={{4,0},{8,4},{12,8},{5,1},{9,5},{13,9},{6,2},{10,6},{14,10},{7,3},{... | collective-permute-start | bytes 294920 | tf_op jit(solution)/shard_map/ppermute | solution.py:22
  84.6 5.9 %collective-permute-start.11 = (f32[12,12,2,128]{3,2,1,0:T(2,128)S(1)}, f32[12,12,2,128]{3,2,1,0:T(2,128)S(1)}, u32[]{:S(2)}, u32[]{:S(2)}) collective-permute-start(f32[12,12,2,128]{3,2,1,0:T(2,128)S(1)} %get-tuple-element.25), channel_id=1, source_target_pairs={{1,0},{2,1},{3,2},{5,4},{6,5},{7,6},{9,8},{10,9},{11,10},{13,12},{... | collective-permute-start | bytes 442376 | tf_op jit(solution)/shard_map/ppermute | solution.py:22
  98.9 6.7 %collective-permute-start.14 = (f32[8,2,4,128]{3,2,1,0:T(4,128)S(1)}, f32[8,2,4,128]{3,2,1,0:T(4,128)S(1)}, u32[]{:S(2)}, u32[]{:S(2)}) collective-permute-start(f32[8,2,4,128]{3,2,1,0:T(4,128)S(1)} %get-tuple-element.44), channel_id=1, source_target_pairs={{0,4},{4,8},{8,12},{1,5},{5,9},{9,13},{2,6},{6,10},{10,14},{3,7},{... | collective-permute-start | bytes 98312 | tf_op jit(solution)/shard_map/ppermute | solution.py:21
  123.4 6.7 %collective-permute-start.20 = (f32[6,2,2,128]{3,2,1,0:T(2,128)S(1)}, f32[6,2,2,128]{3,2,1,0:T(2,128)S(1)}, u32[]{:S(2)}, u32[]{:S(2)}) collective-permute-start(f32[6,2,2,128]{3,2,1,0:T(2,128)S(1)} %fusion.281), channel_id=1, source_target_pairs={{0,4},{4,8},{8,12},{1,5},{5,9},{9,13},{2,6},{6,10},{10,14},{3,7},{... | collective-permute-start | bytes 36872 | tf_op jit(solution)/shard_map/ppermute | solution.py:21
  180.4 5.6 %collective-permute-start.24 = (f32[2,2,2,128]{3,2,1,0:T(2,128)S(1)}, f32[2,2,2,128]{3,2,1,0:T(2,128)S(1)}, u32[]{:S(2)}, u32[]{:S(2)}) collective-permute-start(f32[2,2,2,128]{3,2,1,0:T(2,128)S(1)} %pad_maximum_fusion.47), channel_id=1, source_target_pairs={{0,16},{1,17},{2,18},{3,19},{4,20},{5,21},{6,22},{7,23},{8,24},{9,... | collective-permute-start | bytes 12296 | tf_op jit(solution)/shard_map/ppermute | solution.py:21
  189.2 7.8 %collective-permute-start.26 = (f32[6,2,2,128]{3,2,1,0:T(2,128)S(1)}, f32[6,2,2,128]{3,2,1,0:T(2,128)S(1)}, u32[]{:S(2)}, u32[]{:S(2)}) collective-permute-start(f32[6,2,2,128]{3,2,1,0:T(2,128)S(1)} %fusion.283), channel_id=1, source_target_pairs={{0,4},{4,8},{8,12},{1,5},{5,9},{9,13},{2,6},{6,10},{10,14},{3,7},{... | collective-permute-start | bytes 36872 | tf_op jit(solution)/shard_map/ppermute | solution.py:21
  214.9 6.7 %collective-permute-start.32 = (f32[8,2,4,128]{3,2,1,0:T(4,128)S(1)}, f32[8,2,4,128]{3,2,1,0:T(4,128)S(1)}, u32[]{:S(2)}, u32[]{:S(2)}) collective-permute-start(f32[8,2,4,128]{3,2,1,0:T(4,128)S(1)} %get-tuple-element.40), channel_id=1, source_target_pairs={{0,4},{4,8},{8,12},{1,5},{5,9},{9,13},{2,6},{6,10},{10,14},{3,7},{... | collective-permute-start | bytes 98312 | tf_op jit(solution)/shard_map/ppermute | solution.py:21
  235.1 6.0 %collective-permute-start.37 = (f32[2,8,8,128]{3,2,1,0:T(8,128)S(1)}, f32[2,8,8,128]{3,2,1,0:T(8,128)S(1)}, u32[]{:S(2)}, u32[]{:S(2)}) collective-permute-start(f32[2,8,8,128]{3,2,1,0:T(8,128)S(1)} %get-tuple-element.32), channel_id=1, source_target_pairs={{16,0},{17,1},{18,2},{19,3},{20,4},{21,5},{22,6},{23,7},{24,8},{25... | collective-permute-start | bytes 196616 | tf_op jit(solution)/shard_map/ppermute | solution.py:22
  241.2 5.8 %collective-permute-start.38 = (f32[12,2,8,128]{3,2,1,0:T(8,128)S(1)}, f32[12,2,8,128]{3,2,1,0:T(8,128)S(1)}, u32[]{:S(2)}, u32[]{:S(2)}) collective-permute-start(f32[12,2,8,128]{3,2,1,0:T(8,128)S(1)} %get-tuple-element.27), channel_id=1, source_target_pairs={{0,4},{4,8},{8,12},{1,5},{5,9},{9,13},{2,6},{6,10},{10,14},{3,7},{... | collective-permute-start | bytes 294920 | tf_op jit(solution)/shard_map/ppermute | solution.py:21
  245.1 5.9 %collective-permute-start.39 = (f32[12,2,8,128]{3,2,1,0:T(8,128)S(1)}, f32[12,2,8,128]{3,2,1,0:T(8,128)S(1)}, u32[]{:S(2)}, u32[]{:S(2)}) collective-permute-start(f32[12,2,8,128]{3,2,1,0:T(8,128)S(1)} %get-tuple-element.28), channel_id=1, source_target_pairs={{4,0},{8,4},{12,8},{5,1},{9,5},{13,9},{6,2},{10,6},{14,10},{7,3},{... | collective-permute-start | bytes 294920 | tf_op jit(solution)/shard_map/ppermute | solution.py:22
  252.9 5.9 %collective-permute-start.41 = (f32[12,12,2,128]{3,2,1,0:T(2,128)S(1)}, f32[12,12,2,128]{3,2,1,0:T(2,128)S(1)}, u32[]{:S(2)}, u32[]{:S(2)}) collective-permute-start(f32[12,12,2,128]{3,2,1,0:T(2,128)S(1)} %get-tuple-element.23), channel_id=1, source_target_pairs={{1,0},{2,1},{3,2},{5,4},{6,5},{7,6},{9,8},{10,9},{11,10},{13,12},{... | collective-permute-start | bytes 442376 | tf_op jit(solution)/shard_map/ppermute | solution.py:22
  263.5 6.6 %collective-permute-start.42 = (f32[2,16,16,128]{3,2,1,0:T(8,128)S(1)}, f32[2,16,16,128]{3,2,1,0:T(8,128)S(1)}, u32[]{:S(2)}, u32[]{:S(2)}) collective-permute-start(f32[2,16,16,128]{3,2,1,0:T(8,128)S(1)} %get-tuple-element.20), channel_id=1, source_target_pairs={{0,16},{1,17},{2,18},{3,19},{4,20},{5,21},{6,22},{7,23},{8,24},{9,... | collective-permute-start | bytes 786440 | tf_op jit(solution)/shard_map/ppermute | solution.py:21
  264.8 9.4 %collective-permute-start.43 = (f32[2,16,16,128]{3,2,1,0:T(8,128)S(1)}, f32[2,16,16,128]{3,2,1,0:T(8,128)S(1)}, u32[]{:S(2)}, u32[]{:S(2)}) collective-permute-start(f32[2,16,16,128]{3,2,1,0:T(8,128)S(1)} %get-tuple-element.21), channel_id=1, source_target_pairs={{16,0},{17,1},{18,2},{19,3},{20,4},{21,5},{22,6},{23,7},{24,8},{25... | collective-permute-start | bytes 786440 | tf_op jit(solution)/shard_map/ppermute | solution.py:22
  274.9 6.4 %collective-permute-start.44 = (f32[20,2,16,128]{3,2,1,0:T(8,128)S(1)}, f32[20,2,16,128]{3,2,1,0:T(8,128)S(1)}, u32[]{:S(2)}, u32[]{:S(2)}) collective-permute-start(f32[20,2,16,128]{3,2,1,0:T(8,128)S(1)} %get-tuple-element.16), channel_id=1, source_target_pairs={{0,4},{4,8},{8,12},{1,5},{5,9},{9,13},{2,6},{6,10},{10,14},{3,7},{... | collective-permute-start | bytes 983048 | tf_op jit(solution)/shard_map/ppermute | solution.py:21
  277.3 8.4 %collective-permute-start.45 = (f32[20,2,16,128]{3,2,1,0:T(8,128)S(1)}, f32[20,2,16,128]{3,2,1,0:T(8,128)S(1)}, u32[]{:S(2)}, u32[]{:S(2)}) collective-permute-start(f32[20,2,16,128]{3,2,1,0:T(8,128)S(1)} %get-tuple-element.17), channel_id=1, source_target_pairs={{4,0},{8,4},{12,8},{5,1},{9,5},{13,9},{6,2},{10,6},{14,10},{7,3},{... | collective-permute-start | bytes 983048 | tf_op jit(solution)/shard_map/ppermute | solution.py:22
  287.6 6.8 %collective-permute-start.46 = (f32[20,20,2,128]{3,2,1,0:T(2,128)}, f32[20,20,2,128]{3,2,1,0:T(2,128)}, u32[]{:S(2)}, u32[]{:S(2)}) collective-permute-start(f32[20,20,2,128]{3,2,1,0:T(2,128)} %get-tuple-element.13), channel_id=1, source_target_pairs={{0,1},{1,2},{2,3},{4,5},{5,6},{6,7},{8,9},{9,10},{10,11},{12,13},{... | collective-permute-start | bytes 1228808 | tf_op jit(solution)/shard_map/ppermute | solution.py:21
  290.0 9.3 %collective-permute-start.47 = (f32[20,20,2,128]{3,2,1,0:T(2,128)}, f32[20,20,2,128]{3,2,1,0:T(2,128)}, u32[]{:S(2)}, u32[]{:S(2)}) collective-permute-start(f32[20,20,2,128]{3,2,1,0:T(2,128)} %get-tuple-element.12), channel_id=1, source_target_pairs={{1,0},{2,1},{3,2},{5,4},{6,5},{7,6},{9,8},{10,9},{11,10},{13,12},{... | collective-permute-start | bytes 1228808 | tf_op jit(solution)/shard_map/ppermute | solution.py:22
  (43 other events, 416.1 us)
where the time goes:
time: 365 us; the launch traced here: 361 us
  starting transfers between devices  109 us (30%)
  waiting for transfers between devices  103 us (28%)
  blocking collectives  71.6 us (20%)
  other arithmetic  54.9 us (15%)
  local copies, waits for them, and re-layouts  14.3 us (4%)
  matrix products  5.15 us (1%)
    ppermute x24, waiting for transfers between devices, extended_2(): after = lax.ppermute(initial, axis, down)  86.6 us
    ppermute x24, starting transfers between devices, extended_2(): before = lax.ppermute(last, axis, up)  72.9 us
    ppermute x24, starting transfers between devices, extended_2(): after = lax.ppermute(initial, axis, down)  36.4 us
    unnamed x1, blocking collectives  36.2 us
    psum x1, blocking collectives, local(): summed = lax.psum(partial_block, ('gx', 'gy', 'gz'))  35.4 us
    mul x8, other arithmetic, double_sweep(): sweep_inner(extended[..., :count], source_wide, factor)  23.4 us
    ppermute x24, waiting for transfers between devices, extended_2(): before = lax.ppermute(last, axis, up)  16.9 us
    concatenate x24, other arithmetic, extended_2(): x = jnp.concatenate([before, x, after], axis=dim)  15.6 us
  transfers between devices with their start and end apart: 48, of which 33 were waited for; matrix products, arithmetic and copies ran while one was open for 2% of the time, Pallas kernels for 0%

commit v1 on v0

--- a/solution.py
+++ b/solution.py
@@ -1,6 +1,11 @@
+import functools
+
 import jax
 import jax.numpy as jnp
+import numpy as np
 from jax import lax
+from jax.experimental import pallas as pl
+from jax.experimental.pallas import tpu as pltpu
 from jax.sharding import PartitionSpec as P
 
 PAIRS = 64
@@ -9,6 +14,712 @@
 
 
 OMEGA = 2.0 / 3.0
+AXES = ("gx", "gy", "gz")
+LANES = 128
+KEEP = 1.0 - OMEGA
+SIDE = OMEGA / 6.0
+PITCH = 24
+
+
+def half_select(first, second):
+    low = lax.broadcasted_iota(jnp.int32, first.shape, 1) < PAIRS
+    return jnp.where(low, first, second)
+
+
+def swap(value):
+    return pltpu.roll(value, PAIRS, 1)
+
+
+def pack_tiles(tiles):
+    half = len(tiles)
+    mid = half // 2
+    packed = []
+    for j in range(half):
+        first, second = tiles[j // 2], tiles[j // 2 + mid]
+        if j % 2 == 0:
+            packed.append(half_select(first, swap(second)))
+        else:
+            packed.append(half_select(swap(first), second))
+    return packed
+
+
+def unpack_slots(slots):
+    half = len(slots)
+    tiles = []
+    for k in range(half // 2):
+        tiles.append(half_select(slots[2 * k], swap(slots[2 * k + 1])))
+    for k in range(half // 2):
+        tiles.append(half_select(swap(slots[2 * k]), slots[2 * k + 1]))
+    return tiles
+
+
+def device_flags():
+    flags = []
+    for axis in AXES:
+        where = lax.axis_index(axis)
+        flags.append((where > 0).astype(jnp.float32))
+        flags.append((where < lax.axis_size(axis) - 1).astype(jnp.float32))
+    return flags
+
+
+def row_mask(offset, reach, length, low_flag, high_flag):
+    cell = lax.broadcasted_iota(jnp.int32, (8, LANES), 0) + offset
+    low = jnp.where(cell < 0, low_flag, 1.0)
+    both = jnp.where(cell >= length, high_flag, low)
+    return jnp.where((cell < -reach) | (cell >= length + reach), 0.0, both)
+
+
+def share_kernel(rho_ref, out_ref, r_ref, t_ref, q_ref, a_ref, c_ref):
+    size_x, size_y, merged = rho_ref.shape
+    tiles = merged // LANES
+    half = tiles
+    slots = half + 4
+    inner = half + 2
+    flags = device_flags()
+    zeros = jnp.zeros((8, LANES), jnp.float32)
+
+    def r_row(x, j, y):
+        return ((x + 2) * slots + (j + 2)) * PITCH + (y + 2)
+
+    def t_row(x, j, y):
+        return ((x + 3) * inner + (j + 1)) * PITCH + (y + 3)
+
+    for first, count in ((0, 2), (size_x + 2, 2)):
+        base = first * slots * PITCH
+
+        def clear(i, carry, base=base):
+            r_ref[pl.ds(base + i * PITCH, PITCH), :] = jnp.zeros((PITCH, LANES), jnp.float32)
+            return carry
+
+        lax.fori_loop(0, count * slots, clear, 0)
+    r_ref[pl.ds((size_x + 4) * slots * PITCH, 8), :] = zeros
+    for x in (-3, size_x + 1):
+        base = (x + 3) * inner * PITCH
+
+        def clear_t(i, carry, base=base):
+            t_ref[pl.ds(base + i * PITCH, PITCH), :] = jnp.zeros((PITCH, LANES), jnp.float32)
+            return carry
+
+        lax.fori_loop(0, 2 * inner, clear_t, 0)
+    t_ref[pl.ds(t_row(-1, -1, -3), 8), :] = zeros
+    t_ref[pl.ds((size_x + 6) * inner * PITCH, 8), :] = zeros
+
+    def pack(x, carry):
+        for i in range(size_y // 8):
+            natural = [rho_ref[x, pl.ds(8 * i, 8), pl.ds(LANES * k, LANES)] for k in range(tiles)]
+            packed = pack_tiles(natural)
+            for j in range(half):
+                r_ref[pl.ds(r_row(x, j, 8 * i), 8), :] = packed[j]
+            for j in (-2, -1):
+                r_ref[pl.ds(r_row(x, j, 8 * i), 8), :] = half_select(zeros, swap(packed[half + j]))
+            for j in (half, half + 1):
+                r_ref[pl.ds(r_row(x, j, 8 * i), 8), :] = half_select(swap(packed[j - half]), zeros)
+        r_ref[pl.ds(r_row(x, -2, -2), 2), :] = zeros[:2]
+        for j in range(-2, half + 2):
+            r_ref[pl.ds(r_row(x, j, size_y), 8), :] = zeros
+        return carry
+
+    lax.fori_loop(0, size_x, pack, 0)
+
+    masks = [row_mask(-1 + 8 * i, 1, size_y, flags[2], flags[3]) for i in range(3)]
+    low = lax.broadcasted_iota(jnp.int32, (8, LANES), 1) < PAIRS
+    z_first = jnp.where(low, flags[4], 1.0)
+    z_last = jnp.where(low, 1.0, flags[5])
+
+    def smooth(step, carry):
+        x = step - 1
+        scale = jnp.where(x < 0, flags[0], jnp.where(x >= size_x, flags[1], 1.0))
+        for i in range(3):
+            y = -1 + 8 * i
+            centre = [r_ref[pl.ds(r_row(x, j, y), 8), :] for j in range(-2, half + 2)]
+            for j in range(-1, half + 1):
+                around = centre[j + 1] + centre[j + 3]
+                around = around + r_ref[pl.ds(r_row(x, j, y - 1), 8), :] + r_ref[pl.ds(r_row(x, j, y + 1), 8), :]
+                around = around + r_ref[pl.ds(r_row(x - 1, j, y), 8), :] + r_ref[pl.ds(r_row(x + 1, j, y), 8), :]
+                value = (KEEP * centre[j + 2] + SIDE * around) * (masks[i] * scale)
+                if j == -1:
+                    value = value * z_first
+                if j == half:
+                    value = value * z_last
+                t_ref[pl.ds(t_row(x, j, y), 8), :] = value
+        return carry
+
+    lax.fori_loop(0, size_x + 2, smooth, 0)
+
+    coarse_y = size_y // 2 + 2
+    coarse_k = half // 2 + 1
+
+    def coarsen(step, carry):
+        x = 2 * (step - 1)
+        for i in range(3):
+            y = -3 + 8 * i
+            inside, outside = {}, {}
+            for j in range(-1, half + 1):
+                line = [t_ref[pl.ds(t_row(x + d, j, y), 8), :] for d in (-1, 0, 1, 2)]
+                inside[j] = line[1] + line[2]
+                outside[j] = line[0] + line[3]
+
+            def get(table, j):
+                return table.get(j, zeros)
+
+            whole, faces = [], []
+            for jc in range(-1, half // 2 + 1):
+                j = 2 * jc
+                whole.append(get(inside, j) + get(inside, j + 1))
+                faces.append(
+                    get(inside, j - 1) + get(inside, j + 2) + get(outside, j) + get(outside, j + 1)
+                )
+            for k in range(coarse_k):
+                w = half_select(whole[k], whole[k + 1])
+                f = half_select(faces[k], faces[k + 1])
+                a_ref[pl.ds(k * PITCH + 8 * i, 8), :] = w * (SIDE / 8.0)
+                q_ref[pl.ds(k * PITCH + 8 * i, 8), :] = w * ((KEEP + 3.0 * SIDE) / 8.0) + f * (SIDE / 8.0)
+        for k in range(coarse_k):
+            for start, count in ((0, 8), (8, coarse_y - 8)):
+                base = k * PITCH + 2 * start
+                value = q_ref[pl.ds(base + 1, count, stride=2), :] + q_ref[pl.ds(base + 2, count, stride=2), :]
+                value = value + a_ref[pl.ds(base, count, stride=2), :] + a_ref[pl.ds(base + 3, count, stride=2), :]
+                c_ref[pl.ds((step * coarse_k + k) * coarse_y + start, count), :] = value
+        return carry
+
+    lax.fori_loop(0, size_x // 2 + 2, coarsen, 0)
+    used = (size_x // 2 + 2) * coarse_k * coarse_y
+    c_ref[pl.ds(used, c_ref.shape[0] - used), :] = jnp.zeros((c_ref.shape[0] - used, LANES), jnp.float32)
+    to_messages(c_ref, out_ref)
+
+
+def to_messages(c_ref, out_ref):
+    chunks = c_ref.shape[0] // LANES
+    for c in range(chunks):
+        turned = c_ref[pl.ds(c * LANES, LANES), :].T
+        out_ref[pl.ds(c, PAIRS, stride=2 * chunks), :] = turned[:PAIRS]
+        out_ref[pl.ds(chunks + c, PAIRS, stride=2 * chunks), :] = turned[PAIRS:]
+
+
+def from_messages(in_ref, c_ref):
+    chunks = c_ref.shape[0] // LANES
+    for c in range(chunks):
+        low = in_ref[pl.ds(c, PAIRS, stride=2 * chunks), :]
+        high = in_ref[pl.ds(chunks + c, PAIRS, stride=2 * chunks), :]
+        c_ref[pl.ds(c * LANES, LANES), :] = jnp.concatenate([low, high], axis=0).T
+
+
+def message_rows(block):
+    cells = (block[0] // 2 + 2) * (block[1] // 2 + 2) * (block[2] // 4 + 1)
+    return -(-cells // LANES) * LANES
+
+
+def share(density):
+    size_x, size_y, merged = density.shape
+    half = merged // LANES
+    rows = message_rows((size_x, size_y, merged // PAIRS))
+    vmem = lambda n: pltpu.VMEM((n, LANES), jnp.float32)
+    return pl.pallas_call(
+        share_kernel,
+        out_shape=jax.ShapeDtypeStruct((rows, LANES), jnp.float32),
+        in_specs=[pl.BlockSpec(memory_space=pltpu.VMEM)],
+        out_specs=pl.BlockSpec(memory_space=pltpu.VMEM),
+        scratch_shapes=[
+            vmem((size_x + 4) * (half + 4) * PITCH + 8),
+            vmem((size_x + 6) * (half + 2) * PITCH + 8),
+            vmem((half // 2 + 1) * PITCH + 8),
+            vmem((half // 2 + 1) * PITCH + 8),
+            vmem(rows),
+        ],
+        compiler_params=pltpu.CompilerParams(vmem_limit_bytes=40 << 20),
+        name="share",
+    )(density)
+
+
+def neighbour_sum(field):
+    padded = np.pad(field, ((1, 1), (1, 1), (1, 1), (0, 0)))
+    total = padded[2:, 1:-1, 1:-1] + padded[:-2, 1:-1, 1:-1]
+    total = total + padded[1:-1, 2:, 1:-1] + padded[1:-1, :-2, 1:-1]
+    return total + padded[1:-1, 1:-1, 2:] + padded[1:-1, 1:-1, :-2]
+
+
+def unit_cycle(source, levels):
+    step = lambda v: KEEP * v + SIDE * neighbour_sum(v)
+    if levels == 1:
+        current = SIDE * source
+        for _ in range(COARSE_SWEEPS - 1):
+            current = step(current) + SIDE * source
+        return current
+    once = step(source)
+    residual = step(once)
+    size_x, size_y, size_z, count = residual.shape
+    grouped = residual.reshape(size_x // 2, 2, size_y // 2, 2, size_z // 2, 2, count)
+    fine = 4.0 * unit_cycle(grouped.mean(axis=(1, 3, 5)), levels - 1)
+    for axis in range(3):
+        fine = np.repeat(fine, 2, axis=axis)
+    current = SIDE * (source + once) + fine
+    for _ in range(2):
+        current = step(current) + SIDE * source
+    return current
+
+
+def dense_operator(devices, own, levels):
+    devs_x, devs_y, devs_z = devices
+    size = (2 * devs_x, 2 * devs_y, 2 * devs_z)
+    cells = size[0] * size[1] * size[2]
+    basis = np.eye(cells).reshape(size + (cells,))
+    matrix = 4.0 * unit_cycle(basis, levels).reshape(cells, cells)
+    grid = np.arange(cells).reshape(devs_x, 2, devs_y, 2, devs_z, 2)
+    order = grid.transpose(1, 3, 5, 0, 2, 4).reshape(-1)
+    matrix = matrix[order][:, order].T
+    wide = np.kron(matrix, np.eye(own))
+    return wide.astype(np.float32)
+
+
+def make_lane_roll(shift):
+    return lambda value: pltpu.roll(value, shift % LANES, 1)
+
+
+def solve_kernel(devices, own, block, levels_below, in_ref, dense_ref, out_ref, c_ref, *scratch):
+    devs_x, devs_y, devs_z = devices
+    step_z = own
+    step_y = step_z * devs_z
+    step_x = step_y * devs_y
+    lane = lax.broadcasted_iota(jnp.int32, (1, LANES), 1)
+    device = lane % PAIRS
+    at_z = (device // step_z) % devs_z
+    at_y = (device // step_y) % devs_y
+    at_x = device // step_x
+    low = lane < PAIRS
+    as_f = lambda cond: jnp.where(cond, 1.0, 0.0)
+    has_before_x, has_after_x = as_f(at_x > 0), as_f(at_x < devs_x - 1)
+    has_before_y, has_after_y = as_f(at_y > 0), as_f(at_y < devs_y - 1)
+    low_before_z = as_f(low & (at_z > 0))
+    high_after_z = as_f((~low) & (at_z < devs_z - 1))
+    low_f, high_f = as_f(low), as_f(~low)
+    from_before_x, from_after_x = make_lane_roll(step_x), make_lane_roll(-step_x)
+    from_before_y, from_after_y = make_lane_roll(step_y), make_lane_roll(-step_y)
+    low_from_before = make_lane_roll(PAIRS + step_z)
+    high_from_after = make_lane_roll(PAIRS - step_z)
+
+    def choose(first, second):
+        return jnp.where(jnp.broadcast_to(low, first.shape), first, second)
+
+    class Field:
+        def __init__(self, ref, size):
+            self.ref, self.size = ref, size
+            self.half = size // 2
+            self.pitch = 16 if size > 6 else 8
+            self.slots = self.half + 2
+
+        def row(self, x, k, y):
+            return ((x + 1) * self.slots + (k + 1)) * self.pitch + (y + 1)
+
+        def get(self, x, k, y=0, count=8):
+            return self.ref[pl.ds(self.row(x, k, y), count), :]
+
+        def put(self, x, k, value, y=0):
+            self.ref[pl.ds(self.row(x, k, y), value.shape[0]), :] = value
+
+        def fill(self, corners=False):
+            size, half = self.size, self.half
+            for k in range(half):
+                self.put(-1, k, from_before_x(self.get(size - 1, k, 0, size)) * has_before_x)
+                self.put(size, k, from_after_x(self.get(0, k, 0, size)) * has_after_x)
+            first = -1 if corners else 0
+            count = (size + (2 if corners else 0)) * self.slots
+
+            def line(y):
+                return pl.ds(self.row(first, -1, y), count, stride=self.pitch)
+
+            self.ref[line(-1), :] = from_before_y(self.ref[line(size - 1), :]) * has_before_y
+            self.ref[line(size), :] = from_after_y(self.ref[line(0), :]) * has_after_y
+            y, rows = (-1, size + 2) if corners else (0, size)
+            for x in range(first, size - first):
+                last = self.get(x, half - 1, y, rows)
+                self.put(x, -1, low_from_before(last) * low_before_z + swap(last) * high_f, y)
+                begin = self.get(x, 0, y, rows)
+                self.put(x, half, high_from_after(begin) * high_after_z + swap(begin) * low_f, y)
+
+        def smooth(self, x, k):
+            around = self.get(x - 1, k) + self.get(x + 1, k)
+            around = around + self.get(x, k - 1) + self.get(x, k + 1)
+            around = around + self.get(x, k, -1) + self.get(x, k, 1)
+            return KEEP * self.get(x, k) + SIDE * around
+
+        def cells(self):
+            return [(x, k) for x in range(self.size) for k in range(self.half)]
+
+    sizes = []
+    size = block[0]
+    while size > 2:
+        sizes.append(size)
+        size //= 2
+    f_refs, t_refs, v_refs, u_refs = (scratch[i * len(sizes) : (i + 1) * len(sizes)] for i in range(4))
+    tmp_ref, small_ref = scratch[4 * len(sizes) :]
+    for ref in scratch:
+        ref[...] = jnp.zeros(ref.shape, jnp.float32)
+    sources = [Field(ref, s) for ref, s in zip(f_refs, sizes)]
+    onces = [Field(ref, s) for ref, s in zip(t_refs, sizes)]
+    values = [Field(ref, s) for ref, s in zip(v_refs, sizes)]
+    others = [Field(ref, s) for ref, s in zip(u_refs, sizes)]
+
+    size = sizes[0]
+    slots, wide = size // 2 + 1, size + 2
+    plane = slots * wide
+    from_messages(in_ref, c_ref)
+    rows = lambda x: pl.ds((x + 1) * plane, plane)
+    c_ref[rows(size - 1), :] += from_after_x(c_ref[rows(-1), :]) * has_after_x
+    c_ref[rows(0), :] += from_before_x(c_ref[rows(size), :]) * has_before_x
+    line = lambda y: pl.ds(plane + y + 1, size * slots, stride=wide)
+    c_ref[line(size - 1), :] += from_after_y(c_ref[line(-1), :]) * has_after_y
+    c_ref[line(0), :] += from_before_y(c_ref[line(size), :]) * has_before_y
+    source = sources[0]
+    for x in range(size):
+        part = [c_ref[pl.ds((x + 1) * plane + k * wide + 1, size), :] for k in range(slots)]
+        for k in range(source.half):
+            value = choose(part[k + 1], part[k])
+            if k == 0:
+                value = value + low_from_before(part[slots - 1]) * low_before_z
+            if k == source.half - 1:
+                value = value + high_from_after(part[0]) * high_after_z
+            source.put(x, k, value)
+
+    for number, size in enumerate(sizes):
+        source, once = sources[number], onces[number]
+        source.fill()
+        for x, k in source.cells():
+            once.put(x, k, source.smooth(x, k)[:size])
+        once.fill()
+        half = size // 2
+        quarter = max(half // 2, 1)
+        for x in range(half):
+            for k in range(quarter):
+                total = None
+                for d in range(2):
+                    for e in range(2):
+                        value = once.smooth(2 * x + d, 2 * k + e)
+                        total = value if total is None else total + value
+                tmp_ref[pl.ds((x * quarter + k) * size, size), :] = total[:size] * 0.125
+        count = half * quarter * half
+        coarse = tmp_ref[pl.ds(0, count, stride=2), :] + tmp_ref[pl.ds(1, count, stride=2), :]
+        if half > 2:
+            for x in range(half):
+                for k in range(quarter):
+                    at = (x * quarter + k) * half
+                    sources[number + 1].put(x, k, coarse[at : at + half])
+        else:
+            small_ref[pl.ds(0, count), :] = coarse
+
+    row = jnp.concatenate([small_ref[pl.ds(i, 1), :] for i in range(4)], axis=1)
+    row = jnp.broadcast_to(row, (8, 4 * LANES))
+    solved = jnp.dot(row, dense_ref[...], precision=lax.Precision.HIGHEST, preferred_element_type=jnp.float32)
+    for i in range(4):
+        small_ref[pl.ds(i, 1), :] = solved[0:1, i * LANES : (i + 1) * LANES]
+    correction = small_ref[pl.ds(0, 4), :]
+
+    for number in reversed(range(len(sizes))):
+        size = sizes[number]
+        source, once, value, other = (each[number] for each in (sources, onces, values, others))
+        half = size // 2
+        quarter = max(half // 2, 1)
+        count = half * quarter * half
+        tmp_ref[pl.ds(0, count, stride=2), :] = correction
+        tmp_ref[pl.ds(1, count, stride=2), :] = correction
+        for x, k in source.cells():
+            at = ((x // 2) * quarter + k // 2) * size
+            begin = SIDE * (source.get(x, k, 0, size) + once.get(x, k, 0, size))
+            value.put(x, k, begin + tmp_ref[pl.ds(at, size), :])
+        value.fill()
+        for x, k in source.cells():
+            other.put(x, k, value.smooth(x, k)[:size] + SIDE * source.get(x, k, 0, size))
+        other.fill()
+        for x, k in source.cells():
+            final = 4.0 * (other.smooth(x, k)[:size] + SIDE * source.get(x, k, 0, size))
+            if number:
+                small_ref[pl.ds((x * source.half + k) * size, size), :] = final
+            else:
+                value.put(x, k, final)
+        if number:
+            correction = small_ref[pl.ds(0, size * source.half * size), :]
+
+    result = values[0]
+    size = sizes[0]
+    result.fill(corners=True)
+    for x in range(-1, size + 1):
+        part = [result.get(x, k, -1, wide) for k in range(-1, source.half + 1)]
+        for k in range(slots):
+            c_ref[pl.ds((x + 1) * plane + k * wide, wide), :] = choose(part[k], part[k + 1])
+    to_messages(c_ref, out_ref)
+
+
+def solve(received, devices, block, levels_below):
+    own = PAIRS // (devices[0] * devices[1] * devices[2])
+    rows = received.shape[0]
+    sizes = []
+    size = block[0]
+    while size > 2:
+        sizes.append(size)
+        size //= 2
+    dense = dense_operator(devices, own, levels_below - len(sizes))
+    vmem = lambda n: pltpu.VMEM((n, LANES), jnp.float32)
+    fields = []
+    for _ in range(4):
+        for size in sizes:
+            fields.append(vmem((size + 2) * (size // 2 + 2) * (16 if size > 6 else 8) + 8))
+    return pl.pallas_call(
+        functools.partial(solve_kernel, devices, own, block, levels_below),
+        out_shape=jax.ShapeDtypeStruct((rows, LANES), jnp.float32),
+        in_specs=[pl.BlockSpec(memory_space=pltpu.VMEM)] * 2,
+        out_specs=pl.BlockSpec(memory_space=pltpu.VMEM),
+        scratch_shapes=[vmem(rows)] + fields + [vmem(512), vmem(256)],
+        compiler_params=pltpu.CompilerParams(vmem_limit_bytes=40 << 20),
+        name="solve",
+    )(received, dense)
+
+
+def finish_kernel(
+    copies, rho_ref, xlo_ref, xhi_ref, ylo_ref, yhi_ref, zlo_ref, zhi_ref, in_ref, out_ref, block_ref,
+    r_ref, v_ref, p_ref, e_ref, c_ref
+):
+    size_x, size_y, merged = rho_ref.shape
+    tiles = merged // LANES
+    half = tiles
+    r_slots, v_slots, p_slots = half + 6, half + 4, half + 2
+    flags = device_flags()
+
+    def r_row(x, j, y):
+        return ((x + 3) * r_slots + (j + 3)) * PITCH + (y + 3)
+
+    def v_row(x, j, y):
+        return ((x + 2) * v_slots + (j + 2)) * PITCH + (y + 2)
+
+    def p_row(x, j, y):
+        return ((x + 1) * p_slots + (j + 1)) * PITCH + (y + 1)
+
+    def pack_rows(natural, before, after, x, y, count):
+        packed = pack_tiles(natural)
+        slots = {j: packed[j] for j in range(half)}
+        outer = {-1: swap(before[1]), -2: before[1], -3: swap(before[0])}
+        for j in (-3, -2, -1):
+            slots[j] = half_select(outer[j], swap(packed[half + j]))
+        outer = {0: swap(after[0]), 1: after[0], 2: swap(after[1])}
+        for j in range(3):
+            slots[half + j] = half_select(swap(packed[j]), outer[j])
+        for j, value in slots.items():
+            r_ref[pl.ds(r_row(x, j, y), count), :] = value
+
+    def pack_plane(source_ref, index, x):
+        def lanes(ref, at, rows):
+            return [ref[at, rows, pl.ds(LANES * k, LANES)] for k in range(ref.shape[2] // LANES)]
+
+        for i in range(size_y // 8):
+            rows = pl.ds(8 * i, 8)
+            outer = pl.ds(8 * i + 3, 8)
+            pack_rows(lanes(source_ref, index, rows), lanes(zlo_ref, x + 3, outer), lanes(zhi_ref, x + 3, outer), x, 8 * i, 8)
+        for ref, y in ((ylo_ref, -3), (yhi_ref, size_y)):
+            outer = pl.ds(y + 3, 3)
+            pack_rows(lanes(ref, x + 3, pl.ds(0, 3)), lanes(zlo_ref, x + 3, outer), lanes(zhi_ref, x + 3, outer), x, y, 3)
+
+    def loop(count, body):
+        def step(i, carry):
+            body(i)
+            return carry
+
+        lax.fori_loop(0, count, step, 0)
+
+    loop(3, lambda i: pack_plane(xlo_ref, i, i - 3))
+    loop(size_x, lambda i: pack_plane(rho_ref, i, i))
+    loop(3, lambda i: pack_plane(xhi_ref, i, i + size_x))
+
+    from_messages(in_ref, c_ref)
+    coarse_y = size_y // 2 + 2
+    coarse_k = half // 2 + 1
+    e_slots = coarse_k + 1
+
+    def spread(i):
+        part = [c_ref[pl.ds((i * coarse_k + k) * coarse_y, coarse_y), :] for k in range(coarse_k)]
+        last = coarse_k - 1
+        slots = [half_select(part[0], swap(part[last]))]
+        for k in range(coarse_k - 1):
+            slots.append(half_select(part[k + 1], part[k]))
+        slots.append(half_select(swap(part[0]), part[last]))
+        for k in range(e_slots):
+            base = (i * e_slots + k) * PITCH
+            e_ref[pl.ds(base, coarse_y, stride=2), :] = slots[k]
+            e_ref[pl.ds(base + 1, coarse_y, stride=2), :] = slots[k]
+
+    loop(size_x // 2 + 2, spread)
+
+    low = lax.broadcasted_iota(jnp.int32, (8, LANES), 1) < PAIRS
+    z_first = jnp.where(low, flags[4], 1.0)
+    z_last = jnp.where(low, 1.0, flags[5])
+
+    def x_scale(x):
+        return jnp.where(x < 0, flags[0], jnp.where(x >= size_x, flags[1], 1.0))
+
+    def smooth(ref, row, x, j, y, centre):
+        around = centre[j - 1] + centre[j + 1]
+        around = around + ref[pl.ds(row(x, j, y - 1), 8), :] + ref[pl.ds(row(x, j, y + 1), 8), :]
+        around = around + ref[pl.ds(row(x - 1, j, y), 8), :] + ref[pl.ds(row(x + 1, j, y), 8), :]
+        return KEEP * centre[j] + SIDE * around
+
+    def column(ref, row, x, y, first, last):
+        return {j: ref[pl.ds(row(x, j, y), 8), :] for j in range(first, last)}
+
+    masks = [row_mask(-2 + 8 * i, 2, size_y, flags[2], flags[3]) for i in range(3)]
+
+    def correct(i):
+        x = i - 2
+        scale = x_scale(x)
+        for n in range(3):
+            y = -2 + 8 * n
+            centre = column(r_ref, r_row, x, y, -3, half + 3)
+            mask = masks[n] * scale
+            for j in range(-2, half + 2):
+                value = smooth(r_ref, r_row, x, j, y, centre) * mask
+                if j < 0:
+                    value = value * z_first
+                if j >= half:
+                    value = value * z_last
+                e_slot = (lax.div(i, 2) * e_slots + (j + 2) // 2) * PITCH + 8 * n
+                v_ref[pl.ds(v_row(x, j, y), 8), :] = SIDE * (centre[j] + value) + e_ref[pl.ds(e_slot, 8), :]
+
+    loop(size_x + 4, correct)
+
+    masks_1 = [row_mask(-1 + 8 * i, 1, size_y, flags[2], flags[3]) for i in range(3)]
+
+    def sweep(i):
+        x = i - 1
+        scale = x_scale(x)
+        for n in range(3):
+            y = -1 + 8 * n
+            centre = column(v_ref, v_row, x, y, -2, half + 2)
+            mask = masks_1[n] * scale
+            for j in range(-1, half + 1):
+                value = smooth(v_ref, v_row, x, j, y, centre) + SIDE * r_ref[pl.ds(r_row(x, j, y), 8), :]
+                value = value * mask
+                if j < 0:
+                    value = value * z_first
+                if j >= half:
+                    value = value * z_last
+                p_ref[pl.ds(p_row(x, j, y), 8), :] = value
+
+    loop(size_x + 2, sweep)
+
+    def last_sweep(x):
+        for n in range(size_y // 8):
+            y = 8 * n
+            centre = column(p_ref, p_row, x, y, -1, half + 1)
+            slots = []
+            for j in range(half):
+                slots.append(smooth(p_ref, p_row, x, j, y, centre) + SIDE * r_ref[pl.ds(r_row(x, j, y), 8), :])
+            for k, value in enumerate(unpack_slots(slots)):
+                out_ref[x, pl.ds(y, 8), pl.ds(LANES * k, LANES)] = value
+
+    loop(size_x, last_sweep)
+
+    both = jnp.zeros((LANES, LANES), jnp.float32)
+    for k in range(tiles):
+        lanes = pl.ds(LANES * k, LANES)
+        left = rho_ref[:, :, lanes].reshape(size_x * size_y, LANES)
+        right = out_ref[:, :, lanes].reshape(size_x * size_y, LANES)
+        both = both + lax.dot_general(
+            left, right, (((0,), (0,)), ((), ())),
+            precision=lax.Precision.HIGHEST, preferred_element_type=jnp.float32,
+        )
+    whole = both[:PAIRS] + swap(both[PAIRS:])
+    flat = half_select(whole[: PAIRS // 2], swap(whole[PAIRS // 2 :]))
+    for i in range(copies):
+        block_ref[i] = flat
+
+
+def finish(density, halos, received, copies):
+    size_x, size_y, merged = density.shape
+    half = merged // LANES
+    rows = received.shape[0]
+    vmem = lambda n: pltpu.VMEM((n, LANES), jnp.float32)
+    return pl.pallas_call(
+        functools.partial(finish_kernel, copies),
+        out_shape=(
+            jax.ShapeDtypeStruct(density.shape, jnp.float32),
+            jax.ShapeDtypeStruct((copies, PAIRS // 2, LANES), jnp.float32),
+        ),
+        in_specs=[pl.BlockSpec(memory_space=pltpu.VMEM)] * 8,
+        out_specs=(pl.BlockSpec(memory_space=pltpu.VMEM),) * 2,
+        scratch_shapes=[
+            vmem((size_x + 6) * (half + 6) * PITCH + 8),
+            vmem((size_x + 4) * (half + 4) * PITCH + 8),
+            vmem((size_x + 2) * (half + 2) * PITCH + 8),
+            vmem((size_x // 2 + 2) * (half // 2 + 2) * PITCH + 8),
+            vmem(rows),
+        ],
+        compiler_params=pltpu.CompilerParams(vmem_limit_bytes=56 << 20),
+        name="finish",
+    )(density, *halos, received)
+
+
+def total_kernel(scale, in_ref, out_ref):
+    total = in_ref[0]
+    for i in range(1, in_ref.shape[0]):
+        total = total + in_ref[i]
+    total = total * scale
+    half = PAIRS // 2
+    out_ref[pl.ds(0, half), :] = total[:, :PAIRS]
+    out_ref[pl.ds(half, half), :] = swap(total)[:, :PAIRS]
+
+
+def total(parts, scale):
+    return pl.pallas_call(
+        functools.partial(total_kernel, scale),
+        out_shape=jax.ShapeDtypeStruct((PAIRS, PAIRS), jnp.float32),
+        in_specs=[pl.BlockSpec(memory_space=pltpu.VMEM)],
+        out_specs=pl.BlockSpec(memory_space=pltpu.VMEM),
+        name="total",
+    )(parts)
+
+
+def shifted(first, last, axis):
+    size = lax.axis_size(axis)
+    where = lax.axis_index(axis)
+    if size == 2:
+        got = lax.ppermute(jnp.where(where == 0, last, first), axis, [(0, 1), (1, 0)])
+        return jnp.where(where == 0, 0.0, got), jnp.where(where == 0, got, 0.0)
+    up = [(i, i + 1) for i in range(size - 1)]
+    down = [(j, i) for i, j in up]
+    return lax.ppermute(last, axis, up), lax.ppermute(first, axis, down)
+
+
+def exchanged(messages, axes=AXES):
+    devices = 1
+    for axis in axes:
+        devices *= lax.axis_size(axis)
+    rows = messages.shape[0] // devices
+    shaped = messages.reshape(devices, rows, LANES)
+    return lax.all_to_all(shaped, axes, 0, 0, tiled=True).reshape(messages.shape)
+
+
+def fast_local(density):
+    size_x, size_y, merged = density.shape
+    devices = tuple(lax.axis_size(axis) for axis in AXES)
+    count = devices[0] * devices[1] * devices[2]
+    block = (size_x // 2, size_y // 2, merged // PAIRS // 2)
+
+    xlo, xhi = shifted(density[:3], density[-3:], "gx")
+    messages = share(density)
+
+    def wide_x(part):
+        return jnp.concatenate([part(xlo), part(density), part(xhi)], axis=0)
+
+    ylo, yhi = shifted(wide_x(lambda a: a[:, :3]), wide_x(lambda a: a[:, -3:]), "gy")
+
+    def wide_xy(part):
+        return jnp.concatenate([part(ylo), wide_x(part), part(yhi)], axis=1)
+
+    received = exchanged(messages)
+    deep = 4 * PAIRS
+    zlo, zhi = shifted(wide_xy(lambda a: a[..., :deep]), wide_xy(lambda a: a[..., -deep:]), "gz")
+    answers = solve(received, devices, block, LEVELS - 1)
+    correction = exchanged(answers)
+    potential, parts = finish(density, (xlo, xhi, ylo, yhi, zlo, zhi), correction, count)
+    parts = lax.all_to_all(parts, AXES, 0, 0, tiled=True)
+    cells = size_x * size_y * (merged // PAIRS) * count
+    return potential, total(parts, 4.0 / cells)
 
 
 def extended_2(x, sides, width):
@@ -125,7 +836,7 @@
     return current
 
 
-def local(density):
+def general_local(density):
     cells_x, cells_y, merged = density.shape
     cells_z = merged // PAIRS
     cells = density.reshape(cells_x, cells_y, cells_z, PAIRS)
@@ -149,6 +860,30 @@
     return (solved.reshape(cells_x, cells_y, merged), coulomb)
 
 
+def suits(shape, count):
+    size_x, size_y, merged = shape
+    size_z = merged // PAIRS
+    equal = size_x == size_y == size_z
+    return (
+        2 * PAIRS == LANES
+        and PAIRS % count == 0
+        and equal
+        and size_x % 8 == 0
+        and size_x & (size_x - 1) == 0
+        and size_y + 8 <= PITCH
+        and size_x // 2 ** (LEVELS - 2) == 1
+    )
+
+
+def local(density):
+    count = 1
+    for axis in AXES:
+        count *= lax.axis_size(axis)
+    if suits(density.shape, count):
+        return fast_local(density)
+    return general_local(density)
+
+
 def solution(mesh):
     return jax.shard_map(
         local,

time: 365 us -> 94.1 us (0.26); the launches traced: 361 us -> 93.6 us
  starting transfers between devices: 109 us -> 21 us
  waiting for transfers between devices: 103 us -> 23.9 us
  other arithmetic: 54.9 us -> 1.42 us
  blocking collectives: 71.6 us -> 20.8 us
  Pallas kernels: 0 us -> 22.6 us
  local copies, waits for them, and re-layouts: 14.3 us -> 3.03 us
  matrix products: 5.15 us -> 0 us
    ppermute x48 -> x5, starting transfers between devices: 109 us -> 12.6 us  [the longest x4 10.5 us: shifted(): return (lax.ppermute(last, axis, up), lax.ppermute(first, axis, down))]
    ppermute x48 -> x5, waiting for transfers between devices: 103 us -> 23.8 us  [the longest x4 23.8 us: shifted(): return (lax.ppermute(last, axis, up), lax.ppermute(first, axis, down))]
    unnamed x1 -> x0, blocking collectives: 36.2 us -> none
    psum x1 -> x0, blocking collectives: 35.4 us -> none  [local(): summed = lax.psum(partial_block, ('gx', 'gy', 'gz'))]
    mul x9 -> x0, other arithmetic: 23.4 us -> none  [the longest x8 23.4 us: double_sweep(): sweep_inner(extended[..., :count], source_wide, factor)]
    pallas_call x0 -> x4, Pallas kernels: none -> 22.6 us  [the longest x1 12.7 us: finish(): pl.pallas_call(functools.partial(finish_kernel, copies), out_shape=(jax.S...]
    all_to_all x0 -> x1, blocking collectives: none -> 20.8 us  [fast_local(): parts = lax.all_to_all(parts, AXES, 0, 0, tiled=True)]
    concatenate x32 -> x4, other arithmetic: 17.8 us -> 0.35 us  [the longest x2 0.18 us: wide_x(): return jnp.concatenate([part(xlo), part(density), part(xhi)], axis=0)]
  transfers between devices with their start and end apart: 48 -> 7, of which waited for: 33 -> 3; matrix products, arithmetic and copies ran while one was open for 2% -> 1% of each run, Pallas kernels for 0% -> 9%
where the time goes in v1:
time: 94.1 us; the launch traced here: 93.6 us
  waiting for transfers between devices  23.9 us (25%)
  Pallas kernels  22.6 us (24%)
  starting transfers between devices  21 us (22%)
  blocking collectives  20.8 us (22%)
  local copies, waits for them, and re-layouts  3.03 us (3%)
  other arithmetic  1.42 us (2%)
    ppermute x4, waiting for transfers between devices, shifted(): return (lax.ppermute(last, axis, up), lax.ppermute(first, axis, down))  23.8 us
    all_to_all x1, blocking collectives, fast_local(): parts = lax.all_to_all(parts, AXES, 0, 0, tiled=True)  20.8 us
    pallas_call x1, Pallas kernels, finish(): pl.pallas_call(functools.partial(finish_kernel, copies), out_shape=(jax.S...  12.7 us
    ppermute x4, starting transfers between devices, shifted(): return (lax.ppermute(last, axis, up), lax.ppermute(first, axis, down))  10.5 us
    all_to_all x2, starting transfers between devices, exchanged(): lax.all_to_all(shaped, axes, 0, 0, tiled=True).reshape(messages.shape)  8.39 us
    pallas_call x1, Pallas kernels, share(): pl.pallas_call(share_kernel, out_shape=jax.ShapeDtypeStruct((rows, LANES)...  4.96 us
    pallas_call x1, Pallas kernels, solve(): pl.pallas_call(functools.partial(solve_kernel, devices, own, block, level...  3.21 us
    unnamed x18, local copies, waits for them, and re-layouts  2.75 us
  transfers between devices with their start and end apart: 7, of which 3 were waited for; matrix products, arithmetic and copies ran while one was open for 1% of the time, Pallas kernels for 9%

profile of v1, /device:TPU:1, one launch (start us, length us, event | category | flops | bytes accessed | tf_op | source)
XLA Modules:
  0.0 93.6 jit_solution(15458569997371841826)
XLA Ops:
  0.6 1.0 %slice_select_fusion = f32[3,16,1024]{2,1,0:T(8,128)S(1)} fusion(f32[16,16,1024]{2,1,0:T(8,128)} %rho_ref.3, pred[]{:T(512)S(6)} %eq.2), kind=kLoop, calls=%fused_computation.4 | loop fusion | flops 49152 | bytes 589825 | tf_op jit(solution)/shard_map/jit(_where)/select_n | solution.py:681
  1.7 2.1 %collective-permute-start = (f32[3,16,1024]{2,1,0:T(8,128)S(1)}, f32[3,16,1024]{2,1,0:T(8,128)S(1)}, u32[]{:S(2)}, u32[]{:S(2)}) collective-permute-start(f32[3,16,1024]{2,1,0:T(8,128)S(1)} %slice_select_fusion), channel_id=1, source_target_pairs={{0,16},{16,0},{1,17},{17,1},{2,18},{18,2},{3,19},{19,3},{4,20},{20... | collective-permute-start | bytes 589832 | tf_op jit(solution)/shard_map/ppermute | solution.py:681
  3.8 1.2 %copy-done = f32[16,16,1024]{2,1,0:T(8,128)S(1)} copy-done((f32[16,16,1024]{2,1,0:T(8,128)S(1)}, f32[16,16,1024]{2,1,0:T(8,128)}, u32[]{:S(2)}) %copy-start) | copy-done | bytes 1048600
  5.0 5.0 %share.1 = f32[512,128]{1,0:T(8,128)} custom-call(f32[16,16,1024]{2,1,0:T(8,128)S(1)} %copy-done), custom_call_target="tpu_custom_call" | custom-call | tf_op jit(solution)/shard_map/share/pallas_call | solution.py:217
  10.0 5.6 %all-to-all-start = ((f32[32,16,128]{2,1,0:T(8,128)}), f32[32,16,128]{2,1,0:T(8,128)S(1)}, u32[]{:S(2)}, u32[]{:S(2)}) async-start(f32[32,16,128]{2,1,0:T(8,128)} %bitcast), calls=%async_computation | async-start | bytes 524288 | tf_op jit(solution)/shard_map/all_to_all | solution.py:694
  15.6 0.1 fusion.1
  15.9 0.1 pad_maximum_fusion.2
  16.0 3.5 %collective-permute-start.1 = (f32[22,3,1024]{2,1,0:T(4,128)S(1)}, f32[22,3,1024]{2,1,0:T(4,128)S(1)}, u32[]{:S(2)}, u32[]{:S(2)}) collective-permute-start(f32[22,3,1024]{2,1,0:T(4,128)S(1)} %pad_maximum_fusion.2), channel_id=1, source_target_pairs={{0,4},{4,8},{8,12},{1,5},{5,9},{9,13},{2,6},{6,10},{10,14},{3,7},{... | collective-permute-start | bytes 811016 | tf_op jit(solution)/shard_map/ppermute | solution.py:685
  19.5 0.1 pad_maximum_fusion.3
  19.6 2.1 %collective-permute-start.2 = (f32[22,3,1024]{2,1,0:T(4,128)S(1)}, f32[22,3,1024]{2,1,0:T(4,128)S(1)}, u32[]{:S(2)}, u32[]{:S(2)}) collective-permute-start(f32[22,3,1024]{2,1,0:T(4,128)S(1)} %pad_maximum_fusion.3), channel_id=1, source_target_pairs={{4,0},{8,4},{12,8},{5,1},{9,5},{13,9},{6,2},{10,6},{14,10},{7,3},{... | collective-permute-start | bytes 811016 | tf_op jit(solution)/shard_map/ppermute | solution.py:685
  21.8 3.1 %collective-permute-done.1.ylo_ref = f32[22,3,1024]{2,1,0:T(4,128)S(1)} collective-permute-done((f32[22,3,1024]{2,1,0:T(4,128)S(1)}, f32[22,3,1024]{2,1,0:T(4,128)S(1)}, u32[]{:S(2)}, u32[]{:S(2)}) %collective-permute-start.1) | collective-permute-done | bytes 270368 | tf_op jit(solution)/shard_map/ppermute | solution.py:685
  24.9 3.9 %collective-permute-done.2.yhi_ref = f32[22,3,1024]{2,1,0:T(4,128)S(1)} collective-permute-done((f32[22,3,1024]{2,1,0:T(4,128)S(1)}, f32[22,3,1024]{2,1,0:T(4,128)S(1)}, u32[]{:S(2)}, u32[]{:S(2)}) %collective-permute-start.2) | collective-permute-done | bytes 270368 | tf_op jit(solution)/shard_map/ppermute | solution.py:685
  28.8 0.1 pad_maximum_fusion
  28.9 0.6 copy-done.7
  29.5 3.6 %collective-permute-start.3 = (f32[22,22,256]{2,1,0:T(8,128)S(1)}, f32[22,22,256]{2,1,0:T(8,128)}, u32[]{:S(2)}, u32[]{:S(2)}) collective-permute-start(f32[22,22,256]{2,1,0:T(8,128)S(1)} %pad_maximum_fusion), channel_id=1, source_target_pairs={{0,1},{1,2},{2,3},{4,5},{5,6},{6,7},{8,9},{9,10},{10,11},{12,13},{... | collective-permute-start | bytes 1486856 | tf_op jit(solution)/shard_map/ppermute | solution.py:685
  33.2 3.2 %solve.1 = f32[512,128]{1,0:T(8,128)} custom-call(f32[512,128]{1,0:T(8,128)S(1)} %bitcast.4, f32[512,512]{1,0:T(8,128)S(1)} %copy-done.2), custom_call_target="tpu_custom_call" | custom-call | tf_op jit(solution)/shard_map/solve/pallas_call | solution.py:465
  36.4 2.8 %all-to-all-start.1 = ((f32[32,16,128]{2,1,0:T(8,128)}), f32[32,16,128]{2,1,0:T(8,128)S(1)}, u32[]{:S(2)}, u32[]{:S(2)}) async-start(f32[32,16,128]{2,1,0:T(8,128)} %bitcast.2), calls=%async_computation.1 | async-start | bytes 524288 | tf_op jit(solution)/shard_map/all_to_all | solution.py:694
  39.3 1.3 %collective-permute-start.4 = (f32[22,22,256]{2,1,0:T(8,128)S(1)}, f32[22,22,256]{2,1,0:T(8,128)S(1)}, u32[]{:S(2)}, u32[]{:S(2)}) collective-permute-start(f32[22,22,256]{2,1,0:T(8,128)S(1)} %pad_maximum_fusion.1), channel_id=1, source_target_pairs={{1,0},{2,1},{3,2},{5,4},{6,5},{7,6},{9,8},{10,9},{11,10},{13,12},{... | collective-permute-start | bytes 1486856 | tf_op jit(solution)/shard_map/ppermute | solution.py:685
  40.6 16.8 %collective-permute-done.4.zhi_ref = f32[22,22,256]{2,1,0:T(8,128)S(1)} collective-permute-done((f32[22,22,256]{2,1,0:T(8,128)S(1)}, f32[22,22,256]{2,1,0:T(8,128)S(1)}, u32[]{:S(2)}, u32[]{:S(2)}) %collective-permute-start.4) | collective-permute-done | bytes 495648 | tf_op jit(solution)/shard_map/ppermute | solution.py:685
  57.4 0.8 copy-done.8
  58.2 0.1 copy-done.5
  58.3 12.7 %finish.1 = (f32[16,16,1024]{2,1,0:T(8,128)}, f32[32,32,128]{2,1,0:T(8,128)}) custom-call(f32[16,16,1024]{2,1,0:T(8,128)} %rho_ref.3, f32[3,16,1024]{2,1,0:T(8,128)} %copy-done.4, f32[3,16,1024]{2,1,0:T(8,128)} %copy-done.3, f32[22,3,1024]{2,1,0:T(4,128)} %copy-done.6, f32[22,3,1024]{2,1,0:T(4,128)} %copy-done.7, ...), custom_call_target="tpu_custom_call" | custom-call | tf_op jit(solution)/shard_map/finish/pallas_call | solution.py:637
  71.0 20.8 %all_to_all.15.in_ref = f32[32,32,128]{2,1,0:T(8,128)} all-to-all(f32[32,32,128]{2,1,0:T(8,128)} %get-tuple-element.5), channel_id=1, replica_groups=mesh['gx'=2,'gy'=4,'gz'=4] {'gx','gy','gz'}, dimensions={0} | all-to-all | bytes 1048576 | tf_op jit(solution)/shard_map/all_to_all | solution.py:720
  91.9 1.8 %total.1 = f32[64,64]{1,0:T(8,128)} custom-call(f32[32,32,128]{2,1,0:T(8,128)} %all_to_all.15.in_ref), custom_call_target="tpu_custom_call" | custom-call | tf_op jit(solution)/shard_map/total/pallas_call | solution.py:668
  (25 shorter events, 0.3 us)
Async XLA Ops:
  1.7 14.1 %collective-permute-start = (f32[3,16,1024]{2,1,0:T(8,128)S(1)}, f32[3,16,1024]{2,1,0:T(8,128)S(1)}, u32[]{:S(2)}, u32[]{:S(2)}) collective-permute-start(f32[3,16,1024]{2,1,0:T(8,128)S(1)} %slice_select_fusion), channel_id=1, source_target_pairs={{0,16},{16,0},{1,17},{17,1},{2,18},{18,2},{3,19},{19,3},{4,20},{20... | collective-permute-start | bytes 589832 | tf_op jit(solution)/shard_map/ppermute | solution.py:681
  3.8 1.2 %copy-start = (f32[16,16,1024]{2,1,0:T(8,128)S(1)}, f32[16,16,1024]{2,1,0:T(8,128)}, u32[]{:S(2)}) copy-start(f32[16,16,1024]{2,1,0:T(8,128)} %rho_ref.3) | copy-start | bytes 3145732
  5.0 10.6 %copy-start.1 = (f32[16,16,1024]{2,1,0:T(8,128)S(1)}, f32[16,16,1024]{2,1,0:T(8,128)}, u32[]{:S(2)}) copy-start(f32[16,16,1024]{2,1,0:T(8,128)} %rho_ref.3) | copy-start | bytes 3145732
  10.0 23.2 %all-to-all-start = ((f32[32,16,128]{2,1,0:T(8,128)}), f32[32,16,128]{2,1,0:T(8,128)S(1)}, u32[]{:S(2)}, u32[]{:S(2)}) async-start(f32[32,16,128]{2,1,0:T(8,128)} %bitcast), calls=%async_computation | async-start | bytes 524288 | tf_op jit(solution)/shard_map/all_to_all | solution.py:694
  15.8 5.9 %copy-start.3 = (f32[3,16,1024]{2,1,0:T(8,128)}, f32[3,16,1024]{2,1,0:T(8,128)S(1)}, u32[]{:S(2)}) copy-start(f32[3,16,1024]{2,1,0:T(8,128)S(1)} %get-tuple-element.22.xhi_ref) | copy-start | bytes 589828
  15.8 5.9 %copy-start.4 = (f32[3,16,1024]{2,1,0:T(8,128)}, f32[3,16,1024]{2,1,0:T(8,128)S(1)}, u32[]{:S(2)}) copy-start(f32[3,16,1024]{2,1,0:T(8,128)S(1)} %get-tuple-element.23.xlo_ref) | copy-start | bytes 589828
  16.0 8.9 %collective-permute-start.1 = (f32[22,3,1024]{2,1,0:T(4,128)S(1)}, f32[22,3,1024]{2,1,0:T(4,128)S(1)}, u32[]{:S(2)}, u32[]{:S(2)}) collective-permute-start(f32[22,3,1024]{2,1,0:T(4,128)S(1)} %pad_maximum_fusion.2), channel_id=1, source_target_pairs={{0,4},{4,8},{8,12},{1,5},{5,9},{9,13},{2,6},{6,10},{10,14},{3,7},{... | collective-permute-start | bytes 811016 | tf_op jit(solution)/shard_map/ppermute | solution.py:685
  19.6 13.5 %copy-start.2 = (f32[512,512]{1,0:T(8,128)S(1)}, f32[512,512]{1,0:T(8,128)}, u32[]{:S(2)}) copy-start(f32[512,512]{1,0:T(8,128)} %constant.12.clone.dense_ref) | copy-start | bytes 3145732
  19.6 9.1 %collective-permute-start.2 = (f32[22,3,1024]{2,1,0:T(4,128)S(1)}, f32[22,3,1024]{2,1,0:T(4,128)S(1)}, u32[]{:S(2)}, u32[]{:S(2)}) collective-permute-start(f32[22,3,1024]{2,1,0:T(4,128)S(1)} %pad_maximum_fusion.3), channel_id=1, source_target_pairs={{4,0},{8,4},{12,8},{5,1},{9,5},{13,9},{6,2},{10,6},{14,10},{7,3},{... | collective-permute-start | bytes 811016 | tf_op jit(solution)/shard_map/ppermute | solution.py:685
  24.9 4.0 %copy-start.6 = (f32[22,3,1024]{2,1,0:T(4,128)}, f32[22,3,1024]{2,1,0:T(4,128)S(1)}, u32[]{:S(2)}) copy-start(f32[22,3,1024]{2,1,0:T(4,128)S(1)} %collective-permute-done.1.ylo_ref) | copy-start | bytes 811012
  28.8 0.7 copy-start.7
  29.5 11.0 %collective-permute-start.3 = (f32[22,22,256]{2,1,0:T(8,128)S(1)}, f32[22,22,256]{2,1,0:T(8,128)}, u32[]{:S(2)}, u32[]{:S(2)}) collective-permute-start(f32[22,22,256]{2,1,0:T(8,128)S(1)} %pad_maximum_fusion), channel_id=1, source_target_pairs={{0,1},{1,2},{2,3},{4,5},{5,6},{6,7},{8,9},{9,10},{10,11},{12,13},{... | collective-permute-start | bytes 1486856 | tf_op jit(solution)/shard_map/ppermute | solution.py:685
  36.4 21.1 %all-to-all-start.1 = ((f32[32,16,128]{2,1,0:T(8,128)}), f32[32,16,128]{2,1,0:T(8,128)S(1)}, u32[]{:S(2)}, u32[]{:S(2)}) async-start(f32[32,16,128]{2,1,0:T(8,128)} %bitcast.2), calls=%async_computation.1 | async-start | bytes 524288 | tf_op jit(solution)/shard_map/all_to_all | solution.py:694
  39.3 18.2 %collective-permute-start.4 = (f32[22,22,256]{2,1,0:T(8,128)S(1)}, f32[22,22,256]{2,1,0:T(8,128)S(1)}, u32[]{:S(2)}, u32[]{:S(2)}) collective-permute-start(f32[22,22,256]{2,1,0:T(8,128)S(1)} %pad_maximum_fusion.1), channel_id=1, source_target_pairs={{1,0},{2,1},{3,2},{5,4},{6,5},{7,6},{9,8},{10,9},{11,10},{13,12},{... | collective-permute-start | bytes 1486856 | tf_op jit(solution)/shard_map/ppermute | solution.py:685
  57.4 0.8 copy-start.8
  57.4 0.9 copy-start.5

commit v2 on v1

--- a/solution.py
+++ b/solution.py
@@ -69,7 +69,7 @@
     return jnp.where((cell < -reach) | (cell >= length + reach), 0.0, both)
 
 
-def share_kernel(rho_ref, out_ref, r_ref, t_ref, q_ref, a_ref, c_ref):
+def share_kernel(rho_ref, out_ref, c_ref, r_ref, t_ref, q_ref, a_ref):
     size_x, size_y, merged = rho_ref.shape
     tiles = merged // LANES
     half = tiles
@@ -216,17 +216,17 @@
     vmem = lambda n: pltpu.VMEM((n, LANES), jnp.float32)
     return pl.pallas_call(
         share_kernel,
-        out_shape=jax.ShapeDtypeStruct((rows, LANES), jnp.float32),
+        out_shape=(jax.ShapeDtypeStruct((rows, LANES), jnp.float32),) * 2,
         in_specs=[pl.BlockSpec(memory_space=pltpu.VMEM)],
-        out_specs=pl.BlockSpec(memory_space=pltpu.VMEM),
+        out_specs=(pl.BlockSpec(memory_space=pltpu.VMEM),) * 2,
         scratch_shapes=[
             vmem((size_x + 4) * (half + 4) * PITCH + 8),
             vmem((size_x + 6) * (half + 2) * PITCH + 8),
             vmem((half // 2 + 1) * PITCH + 8),
             vmem((half // 2 + 1) * PITCH + 8),
-            vmem(rows),
         ],
         compiler_params=pltpu.CompilerParams(vmem_limit_bytes=40 << 20),
+        cost_estimate=pl.CostEstimate(flops=20_000_000, bytes_accessed=2_000_000, transcendentals=0),
         name="share",
     )(density)
 
@@ -469,13 +469,50 @@
         out_specs=pl.BlockSpec(memory_space=pltpu.VMEM),
         scratch_shapes=[vmem(rows)] + fields + [vmem(512), vmem(256)],
         compiler_params=pltpu.CompilerParams(vmem_limit_bytes=40 << 20),
+        cost_estimate=pl.CostEstimate(flops=20_000_000, bytes_accessed=2_000_000, transcendentals=0),
         name="solve",
     )(received, dense)
 
 
-def finish_kernel(
-    copies, rho_ref, xlo_ref, xhi_ref, ylo_ref, yhi_ref, zlo_ref, zhi_ref, in_ref, out_ref, block_ref,
-    r_ref, v_ref, p_ref, e_ref, c_ref
+def loop(count, body):
+    def step(i, carry):
+        body(i)
+        return carry
+
+    lax.fori_loop(0, count, step, 0)
+
+
+def smoothed(ref, row, x, j, y, centre):
+    around = centre[j - 1] + centre[j + 1]
+    around = around + ref[pl.ds(row(x, j, y - 1), 8), :] + ref[pl.ds(row(x, j, y + 1), 8), :]
+    around = around + ref[pl.ds(row(x - 1, j, y), 8), :] + ref[pl.ds(row(x + 1, j, y), 8), :]
+    return KEEP * centre[j] + SIDE * around
+
+
+def column(ref, row, x, y, first, last):
+    return {j: ref[pl.ds(row(x, j, y), 8), :] for j in range(first, last)}
+
+
+def edge_lanes(flags):
+    low = lax.broadcasted_iota(jnp.int32, (8, LANES), 1) < PAIRS
+    return jnp.where(low, flags[4], 1.0), jnp.where(low, 1.0, flags[5])
+
+
+def inside(value, mask, j, half, z_first, z_last):
+    value = value * mask
+    if j < 0:
+        value = value * z_first
+    if j >= half:
+        value = value * z_last
+    return value
+
+
+def plane_scale(flags, x, size_x):
+    return jnp.where(x < 0, flags[0], jnp.where(x >= size_x, flags[1], 1.0))
+
+
+def local_kernel(
+    rho_ref, zlo_ref, zhi_ref, ylo_ref, yhi_ref, xlo_ref, xhi_ref, psi_ref, both_ref, r_ref, v_ref, p_ref
 ):
     size_x, size_y, merged = rho_ref.shape
     tiles = merged // LANES
@@ -492,45 +529,158 @@
     def p_row(x, j, y):
         return ((x + 1) * p_slots + (j + 1)) * PITCH + (y + 1)
 
-    def pack_rows(natural, before, after, x, y, count):
-        packed = pack_tiles(natural)
-        slots = {j: packed[j] for j in range(half)}
-        outer = {-1: swap(before[1]), -2: before[1], -3: swap(before[0])}
-        for j in (-3, -2, -1):
-            slots[j] = half_select(outer[j], swap(packed[half + j]))
-        outer = {0: swap(after[0]), 1: after[0], 2: swap(after[1])}
-        for j in range(3):
-            slots[half + j] = half_select(swap(packed[j]), outer[j])
-        for j, value in slots.items():
-            r_ref[pl.ds(r_row(x, j, y), count), :] = value
-
-    def pack_plane(source_ref, index, x):
-        def lanes(ref, at, rows):
-            return [ref[at, rows, pl.ds(LANES * k, LANES)] for k in range(ref.shape[2] // LANES)]
-
+    def lanes(ref, at, rows):
+        return [ref[at, rows, pl.ds(LANES * k, LANES)] for k in range(ref.shape[2] // LANES)]
+
+    def pack_own(x):
         for i in range(size_y // 8):
             rows = pl.ds(8 * i, 8)
-            outer = pl.ds(8 * i + 3, 8)
-            pack_rows(lanes(source_ref, index, rows), lanes(zlo_ref, x + 3, outer), lanes(zhi_ref, x + 3, outer), x, 8 * i, 8)
-        for ref, y in ((ylo_ref, -3), (yhi_ref, size_y)):
-            outer = pl.ds(y + 3, 3)
-            pack_rows(lanes(ref, x + 3, pl.ds(0, 3)), lanes(zlo_ref, x + 3, outer), lanes(zhi_ref, x + 3, outer), x, y, 3)
-
-    def loop(count, body):
-        def step(i, carry):
-            body(i)
-            return carry
-
-        lax.fori_loop(0, count, step, 0)
-
-    loop(3, lambda i: pack_plane(xlo_ref, i, i - 3))
-    loop(size_x, lambda i: pack_plane(rho_ref, i, i))
-    loop(3, lambda i: pack_plane(xhi_ref, i, i + size_x))
-
+            packed = pack_tiles(lanes(rho_ref, x, rows))
+            slots = {j: packed[j] for j in range(half)}
+            before, after = lanes(zlo_ref, x, rows), lanes(zhi_ref, x, rows)
+            outer = {-1: swap(before[1]), -2: before[1], -3: swap(before[0])}
+            for j in (-3, -2, -1):
+                slots[j] = half_select(outer[j], swap(packed[half + j]))
+            outer = {0: swap(after[0]), 1: after[0], 2: swap(after[1])}
+            for j in range(3):
+                slots[half + j] = half_select(swap(packed[j]), outer[j])
+            for j, value in slots.items():
+                r_ref[pl.ds(r_row(x, j, 8 * i), 8), :] = value
+
+    def pack_wide(tile, x, y, count):
+        for j in range(-2, half + 2):
+            first, second = tile[(j + 2) // 2], tile[(j + 2) // 2 + half // 2]
+            if j % 2 == 0:
+                value = half_select(first, swap(second))
+            else:
+                value = half_select(swap(first), second)
+            r_ref[pl.ds(r_row(x, j, y), count), :] = value
+
+    def pack_plane(x):
+        pack_own(x)
+        pack_wide(lanes(ylo_ref, x, pl.ds(0, 3)), x, -3, 3)
+        pack_wide(lanes(yhi_ref, x, pl.ds(0, 3)), x, size_y, 3)
+
+    def pack_outer(i):
+        for ref, x in ((xlo_ref, i - 3), (xhi_ref, i + size_x)):
+            for start, count in ((0, 8), (8, 8), (16, 4)):
+                pack_wide(lanes(ref, i, pl.ds(start, count)), x, start - 2, count)
+
+    loop(size_x, pack_plane)
+    loop(3, pack_outer)
+
+    z_first, z_last = edge_lanes(flags)
+    masks = [row_mask(-2 + 8 * i, 2, size_y, flags[2], flags[3]) for i in range(3)]
+
+    def first_sweep(i):
+        x = i - 2
+        scale = plane_scale(flags, x, size_x)
+        for n in range(3):
+            y = -2 + 8 * n
+            centre = column(r_ref, r_row, x, y, -3, half + 3)
+            mask = masks[n] * scale
+            for j in range(-2, half + 2):
+                value = inside(smoothed(r_ref, r_row, x, j, y, centre), mask, j, half, z_first, z_last)
+                v_ref[pl.ds(v_row(x, j, y), 8), :] = SIDE * (centre[j] + value)
+
+    loop(size_x + 4, first_sweep)
+    masks_1 = [row_mask(-1 + 8 * i, 1, size_y, flags[2], flags[3]) for i in range(3)]
+
+    def second_sweep(i):
+        x = i - 1
+        scale = plane_scale(flags, x, size_x)
+        for n in range(3):
+            y = -1 + 8 * n
+            centre = column(v_ref, v_row, x, y, -2, half + 2)
+            mask = masks_1[n] * scale
+            for j in range(-1, half + 1):
+                value = smoothed(v_ref, v_row, x, j, y, centre) + SIDE * r_ref[pl.ds(r_row(x, j, y), 8), :]
+                p_ref[pl.ds(p_row(x, j, y), 8), :] = inside(value, mask, j, half, z_first, z_last)
+
+    loop(size_x + 2, second_sweep)
+    both_ref[...] = jnp.zeros_like(both_ref)
+
+    def third_sweep(x):
+        left, right = [], []
+        for n in range(size_y // 8):
+            y = 8 * n
+            centre = column(p_ref, p_row, x, y, -1, half + 1)
+            for j in range(half):
+                rho = r_ref[pl.ds(r_row(x, j, y), 8), :]
+                value = smoothed(p_ref, p_row, x, j, y, centre) + SIDE * rho
+                psi_ref[pl.ds((x * half + j) * size_y + y, 8), :] = value
+                left.append(rho)
+                right.append(value)
+        both_ref[...] += lax.dot_general(
+            jnp.concatenate(left, axis=0), jnp.concatenate(right, axis=0), (((0,), (0,)), ((), ())),
+            precision=lax.Precision.HIGHEST, preferred_element_type=jnp.float32,
+        )
+
+    loop(size_x, third_sweep)
+
+
+def local_part(density, halos):
+    size_x, size_y, merged = density.shape
+    half = merged // LANES
+    vmem = lambda n: pltpu.VMEM((n, LANES), jnp.float32)
+    return pl.pallas_call(
+        local_kernel,
+        out_shape=(
+            jax.ShapeDtypeStruct((size_x * half * size_y, LANES), jnp.float32),
+            jax.ShapeDtypeStruct((LANES, LANES), jnp.float32),
+        ),
+        in_specs=[pl.BlockSpec(memory_space=pltpu.VMEM)] * 7,
+        out_specs=(pl.BlockSpec(memory_space=pltpu.VMEM),) * 2,
+        scratch_shapes=[
+            vmem((size_x + 6) * (half + 6) * PITCH + 8),
+            vmem((size_x + 4) * (half + 4) * PITCH + 8),
+            vmem((size_x + 2) * (half + 2) * PITCH + 8),
+        ],
+        compiler_params=pltpu.CompilerParams(vmem_limit_bytes=40 << 20),
+        cost_estimate=pl.CostEstimate(flops=30_000_000, bytes_accessed=4_000_000, transcendentals=0),
+        name="local_part",
+    )(density, *halos)
+
+
+def gram_kernel(copies, in_ref, share_ref, both_ref, c_ref, block_ref):
     from_messages(in_ref, c_ref)
+    both = both_ref[...] + 8.0 * lax.dot_general(
+        share_ref[...], c_ref[...], (((0,), (0,)), ((), ())),
+        precision=lax.Precision.HIGHEST, preferred_element_type=jnp.float32,
+    )
+    whole = both[:PAIRS] + swap(both[PAIRS:])
+    flat = half_select(whole[: PAIRS // 2], swap(whole[PAIRS // 2 :]))
+    for i in range(copies):
+        block_ref[i] = flat
+
+
+def gram(received, shares, both, copies):
+    return pl.pallas_call(
+        functools.partial(gram_kernel, copies),
+        out_shape=(
+            jax.ShapeDtypeStruct(received.shape, jnp.float32),
+            jax.ShapeDtypeStruct((copies, PAIRS // 2, LANES), jnp.float32),
+        ),
+        in_specs=[pl.BlockSpec(memory_space=pltpu.VMEM)] * 3,
+        out_specs=(pl.BlockSpec(memory_space=pltpu.VMEM),) * 2,
+        compiler_params=pltpu.CompilerParams(vmem_limit_bytes=16 << 20),
+        name="gram",
+    )(received, shares, both)
+
+
+def correct_kernel(c_ref, psi_ref, out_ref, e_ref, u_ref):
+    size_x, size_y, merged = out_ref.shape
+    half = merged // LANES
+    flags = device_flags()
     coarse_y = size_y // 2 + 2
     coarse_k = half // 2 + 1
-    e_slots = coarse_k + 1
+    e_slots, u_slots = coarse_k + 1, half + 2
+
+    def e_row(xc, jc, y):
+        return ((xc + 1) * e_slots + (jc + 1)) * PITCH + (y + 2)
+
+    def u_row(x, j, y):
+        return ((x + 1) * u_slots + (j + 1)) * PITCH + (y + 1)
 
     def spread(i):
         part = [c_ref[pl.ds((i * coarse_k + k) * coarse_y, coarse_y), :] for k in range(coarse_k)]
@@ -545,113 +695,60 @@
             e_ref[pl.ds(base + 1, coarse_y, stride=2), :] = slots[k]
 
     loop(size_x // 2 + 2, spread)
-
-    low = lax.broadcasted_iota(jnp.int32, (8, LANES), 1) < PAIRS
-    z_first = jnp.where(low, flags[4], 1.0)
-    z_last = jnp.where(low, 1.0, flags[5])
-
-    def x_scale(x):
-        return jnp.where(x < 0, flags[0], jnp.where(x >= size_x, flags[1], 1.0))
-
-    def smooth(ref, row, x, j, y, centre):
-        around = centre[j - 1] + centre[j + 1]
-        around = around + ref[pl.ds(row(x, j, y - 1), 8), :] + ref[pl.ds(row(x, j, y + 1), 8), :]
-        around = around + ref[pl.ds(row(x - 1, j, y), 8), :] + ref[pl.ds(row(x + 1, j, y), 8), :]
-        return KEEP * centre[j] + SIDE * around
-
-    def column(ref, row, x, y, first, last):
-        return {j: ref[pl.ds(row(x, j, y), 8), :] for j in range(first, last)}
-
-    masks = [row_mask(-2 + 8 * i, 2, size_y, flags[2], flags[3]) for i in range(3)]
-
-    def correct(i):
-        x = i - 2
-        scale = x_scale(x)
-        for n in range(3):
-            y = -2 + 8 * n
-            centre = column(r_ref, r_row, x, y, -3, half + 3)
-            mask = masks[n] * scale
-            for j in range(-2, half + 2):
-                value = smooth(r_ref, r_row, x, j, y, centre) * mask
-                if j < 0:
-                    value = value * z_first
-                if j >= half:
-                    value = value * z_last
-                e_slot = (lax.div(i, 2) * e_slots + (j + 2) // 2) * PITCH + 8 * n
-                v_ref[pl.ds(v_row(x, j, y), 8), :] = SIDE * (centre[j] + value) + e_ref[pl.ds(e_slot, 8), :]
-
-    loop(size_x + 4, correct)
-
-    masks_1 = [row_mask(-1 + 8 * i, 1, size_y, flags[2], flags[3]) for i in range(3)]
-
-    def sweep(i):
-        x = i - 1
-        scale = x_scale(x)
+    z_first, z_last = edge_lanes(flags)
+    masks = [row_mask(-1 + 8 * i, 1, size_y, flags[2], flags[3]) for i in range(3)]
+
+    def first(i):
+        xc = i
         for n in range(3):
             y = -1 + 8 * n
-            centre = column(v_ref, v_row, x, y, -2, half + 2)
-            mask = masks_1[n] * scale
-            for j in range(-1, half + 1):
-                value = smooth(v_ref, v_row, x, j, y, centre) + SIDE * r_ref[pl.ds(r_row(x, j, y), 8), :]
-                value = value * mask
-                if j < 0:
-                    value = value * z_first
-                if j >= half:
-                    value = value * z_last
-                p_ref[pl.ds(p_row(x, j, y), 8), :] = value
-
-    loop(size_x + 2, sweep)
-
-    def last_sweep(x):
+            here = {d: {jc: e_ref[pl.ds(e_row(xc + d, jc, y), 8), :] for jc in range(-1, half // 2 + 1)} for d in (-1, 0)}
+            for d, x in ((-1, 2 * xc - 1), (0, 2 * xc)):
+                mask = masks[n] * plane_scale(flags, x, size_x)
+                base = {}
+                for jc in range(-1, half // 2 + 1):
+                    around = here[-1 - d][jc] + e_ref[pl.ds(e_row(xc + d, jc, y - 1), 8), :]
+                    around = around + e_ref[pl.ds(e_row(xc + d, jc, y + 1), 8), :]
+                    base[jc] = (KEEP + 2.0 * SIDE) * here[d][jc] + SIDE * around
+                for j in range(-1, half + 1):
+                    jc = j // 2
+                    other = jc + (1 if j % 2 else -1)
+                    value = base[jc] + SIDE * here[d][other]
+                    u_ref[pl.ds(u_row(x, j, y), 8), :] = inside(value, mask, j, half, z_first, z_last)
+
+    loop(size_x // 2 + 1, first)
+
+    def second(x):
         for n in range(size_y // 8):
             y = 8 * n
-            centre = column(p_ref, p_row, x, y, -1, half + 1)
+            centre = column(u_ref, u_row, x, y, -1, half + 1)
             slots = []
             for j in range(half):
-                slots.append(smooth(p_ref, p_row, x, j, y, centre) + SIDE * r_ref[pl.ds(r_row(x, j, y), 8), :])
+                psi = psi_ref[pl.ds((x * half + j) * size_y + y, 8), :]
+                slots.append(smoothed(u_ref, u_row, x, j, y, centre) + psi)
             for k, value in enumerate(unpack_slots(slots)):
                 out_ref[x, pl.ds(y, 8), pl.ds(LANES * k, LANES)] = value
 
-    loop(size_x, last_sweep)
-
-    both = jnp.zeros((LANES, LANES), jnp.float32)
-    for k in range(tiles):
-        lanes = pl.ds(LANES * k, LANES)
-        left = rho_ref[:, :, lanes].reshape(size_x * size_y, LANES)
-        right = out_ref[:, :, lanes].reshape(size_x * size_y, LANES)
-        both = both + lax.dot_general(
-            left, right, (((0,), (0,)), ((), ())),
-            precision=lax.Precision.HIGHEST, preferred_element_type=jnp.float32,
-        )
-    whole = both[:PAIRS] + swap(both[PAIRS:])
-    flat = half_select(whole[: PAIRS // 2], swap(whole[PAIRS // 2 :]))
-    for i in range(copies):
-        block_ref[i] = flat
-
-
-def finish(density, halos, received, copies):
-    size_x, size_y, merged = density.shape
+    loop(size_x, second)
+
+
+def correct(rows, psi, shape):
+    size_x, size_y, merged = shape
     half = merged // LANES
-    rows = received.shape[0]
     vmem = lambda n: pltpu.VMEM((n, LANES), jnp.float32)
     return pl.pallas_call(
-        functools.partial(finish_kernel, copies),
-        out_shape=(
-            jax.ShapeDtypeStruct(density.shape, jnp.float32),
-            jax.ShapeDtypeStruct((copies, PAIRS // 2, LANES), jnp.float32),
-        ),
-        in_specs=[pl.BlockSpec(memory_space=pltpu.VMEM)] * 8,
-        out_specs=(pl.BlockSpec(memory_space=pltpu.VMEM),) * 2,
+        correct_kernel,
+        out_shape=jax.ShapeDtypeStruct(shape, jnp.float32),
+        in_specs=[pl.BlockSpec(memory_space=pltpu.VMEM)] * 2,
+        out_specs=pl.BlockSpec(memory_space=pltpu.VMEM),
         scratch_shapes=[
-            vmem((size_x + 6) * (half + 6) * PITCH + 8),
-            vmem((size_x + 4) * (half + 4) * PITCH + 8),
+            vmem((size_x // 2 + 2) * (half // 2 + 2) * PITCH + 8),
             vmem((size_x + 2) * (half + 2) * PITCH + 8),
-            vmem((size_x // 2 + 2) * (half // 2 + 2) * PITCH + 8),
-            vmem(rows),
         ],
-        compiler_params=pltpu.CompilerParams(vmem_limit_bytes=56 << 20),
-        name="finish",
-    )(density, *halos, received)
+        compiler_params=pltpu.CompilerParams(vmem_limit_bytes=24 << 20),
+        cost_estimate=pl.CostEstimate(flops=20_000_000, bytes_accessed=2_000_000, transcendentals=0),
+        name="correct",
+    )(rows, psi)
 
 
 def total_kernel(scale, in_ref, out_ref):
@@ -700,24 +797,27 @@
     count = devices[0] * devices[1] * devices[2]
     block = (size_x // 2, size_y // 2, merged // PAIRS // 2)
 
-    xlo, xhi = shifted(density[:3], density[-3:], "gx")
-    messages = share(density)
-
-    def wide_x(part):
-        return jnp.concatenate([part(xlo), part(density), part(xhi)], axis=0)
-
-    ylo, yhi = shifted(wide_x(lambda a: a[:, :3]), wide_x(lambda a: a[:, -3:]), "gy")
-
-    def wide_xy(part):
-        return jnp.concatenate([part(ylo), wide_x(part), part(yhi)], axis=1)
+    deep = 4 * PAIRS
+    near = 2 * PAIRS
+    zlo, zhi = shifted(density[..., :deep], density[..., -deep:], "gz")
+    messages, shares = share(density)
+
+    def wide_z(part):
+        return jnp.concatenate([part(zlo[..., -near:]), part(density), part(zhi[..., :near])], axis=2)
+
+    ylo, yhi = shifted(wide_z(lambda a: a[:, :3]), wide_z(lambda a: a[:, -3:]), "gy")
+
+    def wide_yz(part):
+        return jnp.concatenate([part(ylo[:, -2:]), wide_z(part), part(yhi[:, :2])], axis=1)
 
     received = exchanged(messages)
-    deep = 4 * PAIRS
-    zlo, zhi = shifted(wide_xy(lambda a: a[..., :deep]), wide_xy(lambda a: a[..., -deep:]), "gz")
+    xlo, xhi = shifted(wide_yz(lambda a: a[:3]), wide_yz(lambda a: a[-3:]), "gx")
     answers = solve(received, devices, block, LEVELS - 1)
     correction = exchanged(answers)
-    potential, parts = finish(density, (xlo, xhi, ylo, yhi, zlo, zhi), correction, count)
+    psi, both = local_part(density, (zlo, zhi, ylo, yhi, xlo, xhi))
+    rows, parts = gram(correction, shares, both, count)
     parts = lax.all_to_all(parts, AXES, 0, 0, tiled=True)
+    potential = correct(rows, psi, density.shape)
     cells = size_x * size_y * (merged // PAIRS) * count
     return potential, total(parts, 4.0 / cells)
 

time: 94.1 us -> 80.6 us (0.86)
  blocking collectives: 20.8 us -> 0 us
  starting transfers between devices: 21 us -> 28.1 us
  waiting for transfers between devices: 23.9 us -> 18.3 us
  local copies, waits for them, and re-layouts: 3.03 us -> 6.07 us
  Pallas kernels: 22.6 us -> 24.7 us
    all_to_all x1 -> x0, blocking collectives: 20.8 us -> none  [fast_local(): parts = lax.all_to_all(parts, AXES, 0, 0, tiled=True)]
    ppermute x4, waiting for transfers between devices: 23.8 us -> 6.83 us  [shifted(): return (lax.ppermute(last, axis, up), lax.ppermute(first, axis, down))]
    all_to_all x0 -> x1, waiting for transfers between devices: none -> 11.5 us  [fast_local(): parts = lax.all_to_all(parts, AXES, 0, 0, tiled=True)]
    all_to_all x0 -> x1, starting transfers between devices: none -> 5.83 us  [fast_local(): parts = lax.all_to_all(parts, AXES, 0, 0, tiled=True)]
    pallas_call x2 -> x4, Pallas kernels: 17.7 us -> 19.7 us  [the longest x1 9.47 us: local_part(): pl.pallas_call(local_kernel, out_shape=(jax.ShapeDtypeStruct((size_x * ha...]
    slice x4 -> x6, local copies, waits for them, and re-layouts: 0.14 us -> 2 us  [the longest x1 1.15 us: fast_local(): zlo, zhi = shifted(density[..., :deep], density[..., -deep:], 'gz')]
    unnamed x18, local copies, waits for them, and re-layouts: 2.75 us -> 3.94 us
    all_to_all x2, starting transfers between devices: 8.39 us -> 9.5 us  [exchanged(): lax.all_to_all(shaped, axes, 0, 0, tiled=True).reshape(messages.shape)]
  transfers between devices with their start and end apart: 7 -> 8, of which waited for: 3 -> 3; matrix products, arithmetic and copies ran while one was open for 1% -> 4% of each run, Pallas kernels for 9% -> 27%
where the time goes in v2:
time: 80.6 us; the launch traced here: 80.1 us
  starting transfers between devices  28.1 us (35%)
  Pallas kernels  24.7 us (31%)
  waiting for transfers between devices  18.3 us (23%)
  local copies, waits for them, and re-layouts  6.07 us (8%)
  other arithmetic  2.05 us (3%)
  between operations  0.85 us (1%)
    ppermute x4, starting transfers between devices, shifted(): return (lax.ppermute(last, axis, up), lax.ppermute(first, axis, down))  11.5 us
    all_to_all x1, waiting for transfers between devices, fast_local(): parts = lax.all_to_all(parts, AXES, 0, 0, tiled=True)  11.5 us
    all_to_all x2, starting transfers between devices, exchanged(): lax.all_to_all(shaped, axes, 0, 0, tiled=True).reshape(messages.shape)  9.5 us
    pallas_call x1, Pallas kernels, local_part(): pl.pallas_call(local_kernel, out_shape=(jax.ShapeDtypeStruct((size_x * ha...  9.47 us
    ppermute x4, waiting for transfers between devices, shifted(): return (lax.ppermute(last, axis, up), lax.ppermute(first, axis, down))  6.83 us
    all_to_all x1, starting transfers between devices, fast_local(): parts = lax.all_to_all(parts, AXES, 0, 0, tiled=True)  5.83 us
    pallas_call x1, Pallas kernels, share(): pl.pallas_call(share_kernel, out_shape=(jax.ShapeDtypeStruct((rows, LANES...  5 us
    unnamed x18, local copies, waits for them, and re-layouts  3.94 us
  transfers between devices with their start and end apart: 8, of which 3 were waited for; matrix products, arithmetic and copies ran while one was open for 4% of the time, Pallas kernels for 27%

profile of v2, /device:TPU:1, one launch (start us, length us, event | category | flops | bytes accessed | tf_op | source)
XLA Modules:
  0.0 80.1 jit_solution(15076105262263043835)
XLA Ops:
  0.6 1.2 %fusion.2 = (f32[16,16,256]{2,1,0:T(8,128)S(1)}, f32[16,16,256]{2,1,0:T(8,128)S(1)}) fusion(f32[16,16,1024]{2,1,0:T(8,128)} %rho_ref.3), kind=kLoop, calls=%fused_computation.7 | loop fusion | bytes 1048576 | tf_op jit(solution)/shard_map/slice | solution.py:802
  1.8 1.3 %collective-permute-start.1 = (f32[16,16,256]{2,1,0:T(8,128)S(1)}, f32[16,16,256]{2,1,0:T(8,128)S(1)}, u32[]{:S(2)}, u32[]{:S(2)}) collective-permute-start(f32[16,16,256]{2,1,0:T(8,128)S(1)} %get-tuple-element.18), channel_id=1, source_target_pairs={{1,0},{2,1},{3,2},{5,4},{6,5},{7,6},{9,8},{10,9},{11,10},{13,12},{... | collective-permute-start | bytes 786440 | tf_op jit(solution)/shard_map/ppermute | solution.py:782
  3.1 4.7 %collective-permute-start = (f32[16,16,256]{2,1,0:T(8,128)S(1)}, f32[16,16,256]{2,1,0:T(8,128)S(1)}, u32[]{:S(2)}, u32[]{:S(2)}) collective-permute-start(f32[16,16,256]{2,1,0:T(8,128)S(1)} %get-tuple-element.19), channel_id=1, source_target_pairs={{0,1},{1,2},{2,3},{4,5},{5,6},{6,7},{8,9},{9,10},{10,11},{12,13},{... | collective-permute-start | bytes 786440 | tf_op jit(solution)/shard_map/ppermute | solution.py:782
  7.8 5.0 %share.1 = (f32[512,128]{1,0:T(8,128)}, f32[512,128]{1,0:T(8,128)S(1)}) custom-call(f32[16,16,1024]{2,1,0:T(8,128)S(1)} %copy-done), custom_call_target="tpu_custom_call" | custom-call | flops 20000000 | bytes 2000000 | tf_op jit(solution)/shard_map/share/pallas_call | solution.py:217
  13.5 6.0 %all-to-all-start = ((f32[32,16,128]{2,1,0:T(8,128)}), f32[32,16,128]{2,1,0:T(8,128)S(1)}, u32[]{:S(2)}, u32[]{:S(2)}) async-start(f32[32,16,128]{2,1,0:T(8,128)} %bitcast), calls=%async_computation | async-start | bytes 524288 | tf_op jit(solution)/shard_map/all_to_all | solution.py:791
  19.6 0.8 fusion
  20.5 3.5 %collective-permute-start.2 = (f32[16,3,1280]{2,1,0:T(4,128)S(1)}, f32[16,3,1280]{2,1,0:T(4,128)S(1)}, u32[]{:S(2)}, u32[]{:S(2)}) collective-permute-start(f32[16,3,1280]{2,1,0:T(4,128)S(1)} %pad_maximum_fusion), channel_id=1, source_target_pairs={{0,4},{4,8},{8,12},{1,5},{5,9},{9,13},{2,6},{6,10},{10,14},{3,7},{... | collective-permute-start | bytes 737288 | tf_op jit(solution)/shard_map/ppermute | solution.py:782
  24.1 2.1 %collective-permute-start.3 = (f32[16,3,1280]{2,1,0:T(4,128)S(1)}, f32[16,3,1280]{2,1,0:T(4,128)S(1)}, u32[]{:S(2)}, u32[]{:S(2)}) collective-permute-start(f32[16,3,1280]{2,1,0:T(4,128)S(1)} %pad_maximum_fusion.1), channel_id=1, source_target_pairs={{4,0},{8,4},{12,8},{5,1},{9,5},{13,9},{6,2},{10,6},{14,10},{7,3},{... | collective-permute-start | bytes 737288 | tf_op jit(solution)/shard_map/ppermute | solution.py:782
  26.2 2.7 %collective-permute-done.2.ylo_ref = f32[16,3,1280]{2,1,0:T(4,128)S(1)} collective-permute-done((f32[16,3,1280]{2,1,0:T(4,128)S(1)}, f32[16,3,1280]{2,1,0:T(4,128)S(1)}, u32[]{:S(2)}, u32[]{:S(2)}) %collective-permute-start.2) | collective-permute-done | bytes 245792 | tf_op jit(solution)/shard_map/ppermute | solution.py:782
  28.9 4.2 %collective-permute-done.3.yhi_ref = f32[16,3,1280]{2,1,0:T(4,128)S(1)} collective-permute-done((f32[16,3,1280]{2,1,0:T(4,128)S(1)}, f32[16,3,1280]{2,1,0:T(4,128)S(1)}, u32[]{:S(2)}, u32[]{:S(2)}) %collective-permute-start.3) | collective-permute-done | bytes 245792 | tf_op jit(solution)/shard_map/ppermute | solution.py:782
  33.1 0.9 %maximum_select_fusion = f32[3,20,1280]{2,1,0:T(8,128)} fusion(f32[3,2,1280]{2,1,0:T(2,128)S(1)} %get-tuple-element.25, f32[3,16,128]{2,1,0:T(8,128)S(1)} %get-tuple-element.29, f32[3,16,1024]{2,1,0:T(8,128)S(1)} %copy-done.8, f32[3,16,128]{2,1,0:T(8,128)S(1)} %get-tuple-element.27, f32[3,2,1280]{2,1,0:T(2,128)S(1)} %get-tuple-element.23, ...), kind=kLoop, calls=%fused_computation | loop fusion | flops 691200 | bytes 921601 | tf_op jit(solution)/shard_map/jit(_where)/select_n | solution.py:778
  34.0 1.2 %collective-permute-start.4 = (f32[3,20,1280]{2,1,0:T(8,128)}, f32[3,20,1280]{2,1,0:T(8,128)}, u32[]{:S(2)}, u32[]{:S(2)}) collective-permute-start(f32[3,20,1280]{2,1,0:T(8,128)} %maximum_select_fusion), channel_id=1, source_target_pairs={{0,16},{16,0},{1,17},{17,1},{2,18},{18,2},{3,19},{19,3},{4,20},{20... | collective-permute-start | bytes 921608 | tf_op jit(solution)/shard_map/ppermute | solution.py:778
  35.2 3.2 %solve.1 = f32[512,128]{1,0:T(8,128)} custom-call(f32[512,128]{1,0:T(8,128)S(1)} %bitcast.5, f32[512,512]{1,0:T(8,128)S(1)} %copy-done.1), custom_call_target="tpu_custom_call" | custom-call | flops 20000000 | bytes 2000000 | tf_op jit(solution)/shard_map/solve/pallas_call | solution.py:465
  38.4 3.5 %all-to-all-start.1 = ((f32[32,16,128]{2,1,0:T(8,128)}), f32[32,16,128]{2,1,0:T(8,128)S(1)}, u32[]{:S(2)}, u32[]{:S(2)}) async-start(f32[32,16,128]{2,1,0:T(8,128)} %bitcast.2), calls=%async_computation.1 | async-start | bytes 524288 | tf_op jit(solution)/shard_map/all_to_all | solution.py:791
  42.0 1.0 %broadcast_select_fusion = (f32[3,20,1280]{2,1,0:T(8,128)S(1)}, f32[3,20,1280]{2,1,0:T(8,128)S(1)}) fusion(f32[3,20,1280]{2,1,0:T(8,128)} %collective-permute-done.4, pred[]{:T(512)S(6)} %eq.2), kind=kLoop, calls=%fused_computation.3 | loop fusion | flops 153600 | bytes 921601 | tf_op jit(solution)/shard_map/jit(_where)/select_n | solution.py:779
  43.0 9.5 %local_part.1 = (f32[2048,128]{1,0:T(8,128)S(1)}, f32[128,128]{1,0:T(8,128)S(1)}) custom-call(f32[16,16,1024]{2,1,0:T(8,128)S(1)} %copy-done, f32[16,16,256]{2,1,0:T(8,128)S(1)} %collective-permute-done.zlo_ref, f32[16,16,256]{2,1,0:T(8,128)S(1)} %collective-permute-done.1.zhi_ref, f32[16,3,1280]{2,1,0:T(4,128)S(1)} %collective-permute-done.2.ylo_ref, ...), custom_call_target="tpu_custom_call" | custom-call | flops 30000000 | bytes 4000000 | tf_op jit(solution)/shard_map/local_part/pallas_call | solution.py:626
  53.1 0.9 %copy-done.3 = f32[512,128]{1,0:T(8,128)S(1)} copy-done((f32[512,128]{1,0:T(8,128)S(1)}, f32[512,128]{1,0:T(8,128)}, u32[]{:S(2)}) %copy-start.3) | copy-done | bytes 262168
  54.1 0.8 %copy-done.5 = f32[128,128]{1,0:T(8,128)S(1)} copy-done((f32[128,128]{1,0:T(8,128)S(1)}, f32[128,128]{1,0:T(8,128)}, u32[]{:S(2)}) %copy-start.5) | copy-done | bytes 65560
  54.9 1.5 %gram.1 = (f32[512,128]{1,0:T(8,128)S(1)}, f32[32,32,128]{2,1,0:T(8,128)}) custom-call(f32[512,128]{1,0:T(8,128)S(1)} %bitcast.4, f32[512,128]{1,0:T(8,128)S(1)} %copy-done.3, f32[128,128]{1,0:T(8,128)S(1)} %copy-done.5), custom_call_target="tpu_custom_call" | custom-call | tf_op jit(solution)/shard_map/gram/pallas_call | solution.py:658
  56.4 5.8 %all-to-all-start.2 = ((f32[32,32,128]{2,1,0:T(8,128)}), f32[32,32,128]{2,1,0:T(8,128)S(1)}, u32[]{:S(2)}, u32[]{:S(2)}) async-start(f32[32,32,128]{2,1,0:T(8,128)} %get-tuple-element.13), calls=%async_computation.2 | async-start | bytes 1048576 | tf_op jit(solution)/shard_map/all_to_all | solution.py:819
  62.2 3.8 %correct.1 = f32[16,16,1024]{2,1,0:T(8,128)} custom-call(f32[512,128]{1,0:T(8,128)S(1)} %get-tuple-element.11.c_ref, f32[2048,128]{1,0:T(8,128)S(1)} %get-tuple-element.12.psi_ref), custom_call_target="tpu_custom_call" | custom-call | flops 20000000 | bytes 2000000 | tf_op jit(solution)/shard_map/correct/pallas_call | solution.py:739
  66.0 11.5 %all-to-all-done.2.in_ref = f32[32,32,128]{2,1,0:T(8,128)S(1)} async-done(((f32[32,32,128]{2,1,0:T(8,128)}), f32[32,32,128]{2,1,0:T(8,128)S(1)}, u32[]{:S(2)}, u32[]{:S(2)}) %all-to-all-start.2) | async-done | bytes 524320 | tf_op jit(solution)/shard_map/all_to_all | solution.py:819
  77.5 0.8 %copy-done.6 = f32[32,32,128]{2,1,0:T(8,128)} copy-done((f32[32,32,128]{2,1,0:T(8,128)}, f32[32,32,128]{2,1,0:T(8,128)S(1)}, u32[]{:S(2)}) %copy-start.6) | copy-done | bytes 524312
  78.3 1.8 %total.1 = f32[64,64]{1,0:T(8,128)} custom-call(f32[32,32,128]{2,1,0:T(8,128)} %copy-done.6), custom_call_target="tpu_custom_call" | custom-call | tf_op jit(solution)/shard_map/total/pallas_call | solution.py:765
  (29 shorter events, 1.7 us)
Async XLA Ops:
  0.6 7.1 %copy-start = (f32[16,16,1024]{2,1,0:T(8,128)S(1)}, f32[16,16,1024]{2,1,0:T(8,128)}, u32[]{:S(2)}) copy-start(f32[16,16,1024]{2,1,0:T(8,128)} %rho_ref.3) | copy-start | bytes 3145732
  1.8 18.5 %collective-permute-start.1 = (f32[16,16,256]{2,1,0:T(8,128)S(1)}, f32[16,16,256]{2,1,0:T(8,128)S(1)}, u32[]{:S(2)}, u32[]{:S(2)}) collective-permute-start(f32[16,16,256]{2,1,0:T(8,128)S(1)} %get-tuple-element.18), channel_id=1, source_target_pairs={{1,0},{2,1},{3,2},{5,4},{6,5},{7,6},{9,8},{10,9},{11,10},{13,12},{... | collective-permute-start | bytes 786440 | tf_op jit(solution)/shard_map/ppermute | solution.py:782
  3.1 17.3 %collective-permute-start = (f32[16,16,256]{2,1,0:T(8,128)S(1)}, f32[16,16,256]{2,1,0:T(8,128)S(1)}, u32[]{:S(2)}, u32[]{:S(2)}) collective-permute-start(f32[16,16,256]{2,1,0:T(8,128)S(1)} %get-tuple-element.19), channel_id=1, source_target_pairs={{0,1},{1,2},{2,3},{4,5},{5,6},{6,7},{8,9},{9,10},{10,11},{12,13},{... | collective-permute-start | bytes 786440 | tf_op jit(solution)/shard_map/ppermute | solution.py:782
  12.8 0.7 copy-start.2
  13.5 21.7 %all-to-all-start = ((f32[32,16,128]{2,1,0:T(8,128)}), f32[32,16,128]{2,1,0:T(8,128)S(1)}, u32[]{:S(2)}, u32[]{:S(2)}) async-start(f32[32,16,128]{2,1,0:T(8,128)} %bitcast), calls=%async_computation | async-start | bytes 524288 | tf_op jit(solution)/shard_map/all_to_all | solution.py:791
  20.5 8.4 %collective-permute-start.2 = (f32[16,3,1280]{2,1,0:T(4,128)S(1)}, f32[16,3,1280]{2,1,0:T(4,128)S(1)}, u32[]{:S(2)}, u32[]{:S(2)}) collective-permute-start(f32[16,3,1280]{2,1,0:T(4,128)S(1)} %pad_maximum_fusion), channel_id=1, source_target_pairs={{0,4},{4,8},{8,12},{1,5},{5,9},{9,13},{2,6},{6,10},{10,14},{3,7},{... | collective-permute-start | bytes 737288 | tf_op jit(solution)/shard_map/ppermute | solution.py:782
  24.0 9.1 %copy-start.7 = (f32[3,16,1024]{2,1,0:T(8,128)S(1)}, f32[3,16,1024]{2,1,0:T(8,128)}, u32[]{:S(2)}) copy-start(f32[3,16,1024]{2,1,0:T(8,128)} %get-tuple-element.14) | copy-start | bytes 589828
  24.0 9.1 %copy-start.8 = (f32[3,16,1024]{2,1,0:T(8,128)S(1)}, f32[3,16,1024]{2,1,0:T(8,128)}, u32[]{:S(2)}) copy-start(f32[3,16,1024]{2,1,0:T(8,128)} %get-tuple-element.15) | copy-start | bytes 589828
  24.0 11.2 %copy-start.1 = (f32[512,512]{1,0:T(8,128)S(1)}, f32[512,512]{1,0:T(8,128)}, u32[]{:S(2)}) copy-start(f32[512,512]{1,0:T(8,128)} %constant.12.clone.dense_ref) | copy-start | bytes 3145732
  24.1 9.0 %collective-permute-start.3 = (f32[16,3,1280]{2,1,0:T(4,128)S(1)}, f32[16,3,1280]{2,1,0:T(4,128)S(1)}, u32[]{:S(2)}, u32[]{:S(2)}) collective-permute-start(f32[16,3,1280]{2,1,0:T(4,128)S(1)} %pad_maximum_fusion.1), channel_id=1, source_target_pairs={{4,0},{8,4},{12,8},{5,1},{9,5},{13,9},{6,2},{10,6},{14,10},{7,3},{... | collective-permute-start | bytes 737288 | tf_op jit(solution)/shard_map/ppermute | solution.py:782
  34.0 8.0 %collective-permute-start.4 = (f32[3,20,1280]{2,1,0:T(8,128)}, f32[3,20,1280]{2,1,0:T(8,128)}, u32[]{:S(2)}, u32[]{:S(2)}) collective-permute-start(f32[3,20,1280]{2,1,0:T(8,128)} %maximum_select_fusion), channel_id=1, source_target_pairs={{0,16},{16,0},{1,17},{17,1},{2,18},{18,2},{3,19},{19,3},{4,20},{20... | collective-permute-start | bytes 921608 | tf_op jit(solution)/shard_map/ppermute | solution.py:778
  38.4 14.7 %all-to-all-start.1 = ((f32[32,16,128]{2,1,0:T(8,128)}), f32[32,16,128]{2,1,0:T(8,128)S(1)}, u32[]{:S(2)}, u32[]{:S(2)}) async-start(f32[32,16,128]{2,1,0:T(8,128)} %bitcast.2), calls=%async_computation.1 | async-start | bytes 524288 | tf_op jit(solution)/shard_map/all_to_all | solution.py:791
  52.5 0.6 copy-start.4
  53.1 1.0 %copy-start.3 = (f32[512,128]{1,0:T(8,128)S(1)}, f32[512,128]{1,0:T(8,128)}, u32[]{:S(2)}) copy-start(f32[512,128]{1,0:T(8,128)} %copy-done.2) | copy-start | bytes 786436
  54.1 0.8 %copy-start.5 = (f32[128,128]{1,0:T(8,128)S(1)}, f32[128,128]{1,0:T(8,128)}, u32[]{:S(2)}) copy-start(f32[128,128]{1,0:T(8,128)} %copy-done.4) | copy-start | bytes 196612
  56.4 21.1 %all-to-all-start.2 = ((f32[32,32,128]{2,1,0:T(8,128)}), f32[32,32,128]{2,1,0:T(8,128)S(1)}, u32[]{:S(2)}, u32[]{:S(2)}) async-start(f32[32,32,128]{2,1,0:T(8,128)} %get-tuple-element.13), calls=%async_computation.2 | async-start | bytes 1048576 | tf_op jit(solution)/shard_map/all_to_all | solution.py:819
  77.5 0.8 %copy-start.6 = (f32[32,32,128]{2,1,0:T(8,128)}, f32[32,32,128]{2,1,0:T(8,128)S(1)}, u32[]{:S(2)}) copy-start(f32[32,32,128]{2,1,0:T(8,128)S(1)} %all-to-all-done.2.in_ref) | copy-start | bytes 1572868

commit v3 on v2

--- a/solution.py
+++ b/solution.py
@@ -18,6 +18,7 @@
 LANES = 128
 KEEP = 1.0 - OMEGA
 SIDE = OMEGA / 6.0
+RATIO = KEEP / SIDE
 PITCH = 24
 
 
@@ -69,7 +70,43 @@
     return jnp.where((cell < -reach) | (cell >= length + reach), 0.0, both)
 
 
-def share_kernel(rho_ref, out_ref, c_ref, r_ref, t_ref, q_ref, a_ref):
+def loop(count, body, unroll=1, start=0):
+    def step(i, carry):
+        body(i)
+        return carry
+
+    lax.fori_loop(start, start + count, step, 0, unroll=unroll)
+
+
+def weighted(ref, row, x, j, y, centre):
+    around = (centre[j - 1] + centre[j + 1]) + RATIO * centre[j]
+    beside = ref[pl.ds(row(x, j, y - 1), 8), :] + ref[pl.ds(row(x, j, y + 1), 8), :]
+    behind = ref[pl.ds(row(x - 1, j, y), 8), :] + ref[pl.ds(row(x + 1, j, y), 8), :]
+    return around + (beside + behind)
+
+
+def column(ref, row, x, y, first, last):
+    return {j: ref[pl.ds(row(x, j, y), 8), :] for j in range(first, last)}
+
+
+def edge_lanes(flags):
+    low = lax.broadcasted_iota(jnp.int32, (8, LANES), 1) < PAIRS
+    return jnp.where(low, flags[4], 1.0), jnp.where(low, 1.0, flags[5])
+
+
+def inside(value, mask, j, half, z_first, z_last):
+    if j < 0:
+        mask = mask * z_first
+    if j >= half:
+        mask = mask * z_last
+    return value * mask
+
+
+def plane_scale(flags, x, size_x):
+    return jnp.where(x < 0, flags[0], jnp.where(x >= size_x, flags[1], 1.0)) * SIDE
+
+
+def share_kernel(rho_ref, out_ref, share_ref, c_ref, r_ref, t_ref, q_ref, a_ref, sem):
     size_x, size_y, merged = rho_ref.shape
     tiles = merged // LANES
     half = tiles
@@ -79,32 +116,19 @@
     zeros = jnp.zeros((8, LANES), jnp.float32)
 
     def r_row(x, j, y):
-        return ((x + 2) * slots + (j + 2)) * PITCH + (y + 2)
+        return ((x + 1) * slots + (j + 2)) * PITCH + (y + 2)
 
     def t_row(x, j, y):
-        return ((x + 3) * inner + (j + 1)) * PITCH + (y + 3)
-
-    for first, count in ((0, 2), (size_x + 2, 2)):
-        base = first * slots * PITCH
-
-        def clear(i, carry, base=base):
-            r_ref[pl.ds(base + i * PITCH, PITCH), :] = jnp.zeros((PITCH, LANES), jnp.float32)
-            return carry
-
-        lax.fori_loop(0, count * slots, clear, 0)
-    r_ref[pl.ds((size_x + 4) * slots * PITCH, 8), :] = zeros
-    for x in (-3, size_x + 1):
-        base = (x + 3) * inner * PITCH
-
-        def clear_t(i, carry, base=base):
-            t_ref[pl.ds(base + i * PITCH, PITCH), :] = jnp.zeros((PITCH, LANES), jnp.float32)
-            return carry
-
-        lax.fori_loop(0, 2 * inner, clear_t, 0)
-    t_ref[pl.ds(t_row(-1, -1, -3), 8), :] = zeros
-    t_ref[pl.ds((size_x + 6) * inner * PITCH, 8), :] = zeros
-
-    def pack(x, carry):
+        return ((x + 1) * inner + (j + 1)) * PITCH + (y + 3)
+
+    for x in (-1, size_x):
+        for i in range(slots * PITCH // 8):
+            r_ref[pl.ds((x + 1) * slots * PITCH + 8 * i, 8), :] = zeros
+    r_ref[pl.ds((size_x + 2) * slots * PITCH, 8), :] = zeros
+    t_ref[pl.ds(0, 8), :] = zeros
+    t_ref[pl.ds((size_x + 2) * inner * PITCH, 8), :] = zeros
+
+    def pack(x):
         for i in range(size_y // 8):
             natural = [rho_ref[x, pl.ds(8 * i, 8), pl.ds(LANES * k, LANES)] for k in range(tiles)]
             packed = pack_tiles(natural)
@@ -117,75 +141,85 @@
         r_ref[pl.ds(r_row(x, -2, -2), 2), :] = zeros[:2]
         for j in range(-2, half + 2):
             r_ref[pl.ds(r_row(x, j, size_y), 8), :] = zeros
-        return carry
-
-    lax.fori_loop(0, size_x, pack, 0)
+
+    loop(size_x, pack, 4)
 
     masks = [row_mask(-1 + 8 * i, 1, size_y, flags[2], flags[3]) for i in range(3)]
-    low = lax.broadcasted_iota(jnp.int32, (8, LANES), 1) < PAIRS
-    z_first = jnp.where(low, flags[4], 1.0)
-    z_last = jnp.where(low, 1.0, flags[5])
-
-    def smooth(step, carry):
-        x = step - 1
-        scale = jnp.where(x < 0, flags[0], jnp.where(x >= size_x, flags[1], 1.0))
+    z_first, z_last = edge_lanes(flags)
+
+    def smooth(x):
         for i in range(3):
             y = -1 + 8 * i
-            centre = [r_ref[pl.ds(r_row(x, j, y), 8), :] for j in range(-2, half + 2)]
+            centre = column(r_ref, r_row, x, y, -2, half + 2)
+            mask = masks[i] * SIDE
             for j in range(-1, half + 1):
-                around = centre[j + 1] + centre[j + 3]
-                around = around + r_ref[pl.ds(r_row(x, j, y - 1), 8), :] + r_ref[pl.ds(r_row(x, j, y + 1), 8), :]
-                around = around + r_ref[pl.ds(r_row(x - 1, j, y), 8), :] + r_ref[pl.ds(r_row(x + 1, j, y), 8), :]
-                value = (KEEP * centre[j + 2] + SIDE * around) * (masks[i] * scale)
-                if j == -1:
-                    value = value * z_first
-                if j == half:
-                    value = value * z_last
+                value = inside(weighted(r_ref, r_row, x, j, y, centre), mask, j, half, z_first, z_last)
                 t_ref[pl.ds(t_row(x, j, y), 8), :] = value
-        return carry
-
-    lax.fori_loop(0, size_x + 2, smooth, 0)
-
+
+    loop(size_x, smooth)
+    for x, near in ((-1, 0), (size_x, size_x - 1)):
+        scale = plane_scale(flags, x, size_x)
+        for i in range(3):
+            y = -1 + 8 * i
+            mask = masks[i] * scale
+            for j in range(-1, half + 1):
+                value = inside(r_ref[pl.ds(r_row(near, j, y), 8), :], mask, j, half, z_first, z_last)
+                t_ref[pl.ds(t_row(x, j, y), 8), :] = value
+
+    coarse_x = size_x // 2 + 2
     coarse_y = size_y // 2 + 2
     coarse_k = half // 2 + 1
 
-    def coarsen(step, carry):
-        x = 2 * (step - 1)
+    def coarsen(step, own, other):
         for i in range(3):
             y = -3 + 8 * i
-            inside, outside = {}, {}
-            for j in range(-1, half + 1):
-                line = [t_ref[pl.ds(t_row(x + d, j, y), 8), :] for d in (-1, 0, 1, 2)]
-                inside[j] = line[1] + line[2]
-                outside[j] = line[0] + line[3]
-
-            def get(table, j):
-                return table.get(j, zeros)
+
+            def planes(at, j):
+                line = [t_ref[pl.ds(t_row(x, j, y), 8), :] for x in at]
+                return line[0] + line[1] if len(line) == 2 else line[0]
+
+            within = {j: planes(own, j) for j in range(-1, half + 1)}
+            beside = {j: planes(other, j) for j in range(-1, half + 1)}
+
+            def added(*terms):
+                known = [table[j] for table, j in terms if j in table]
+                total = known[0]
+                for term in known[1:]:
+                    total = total + term
+                return total
 
             whole, faces = [], []
             for jc in range(-1, half // 2 + 1):
                 j = 2 * jc
-                whole.append(get(inside, j) + get(inside, j + 1))
-                faces.append(
-                    get(inside, j - 1) + get(inside, j + 2) + get(outside, j) + get(outside, j + 1)
-                )
+                whole.append(added((within, j), (within, j + 1)))
+                faces.append(added((within, j - 1), (within, j + 2), (beside, j), (beside, j + 1)))
             for k in range(coarse_k):
                 w = half_select(whole[k], whole[k + 1])
                 f = half_select(faces[k], faces[k + 1])
-                a_ref[pl.ds(k * PITCH + 8 * i, 8), :] = w * (SIDE / 8.0)
-                q_ref[pl.ds(k * PITCH + 8 * i, 8), :] = w * ((KEEP + 3.0 * SIDE) / 8.0) + f * (SIDE / 8.0)
+                at = (step * coarse_k + k) * PITCH + 8 * i
+                a_ref[pl.ds(at, 8), :] = w
+                q_ref[pl.ds(at, 8), :] = w * (RATIO + 3.0) + f
+
+    coarsen(0, (-1,), (0,))
+    loop(size_x // 2, lambda i: coarsen(i + 1, (2 * i, 2 * i + 1), (2 * i - 1, 2 * i + 2)))
+    coarsen(coarse_x - 1, (size_x,), (size_x - 1,))
+
+    def along_y(step):
         for k in range(coarse_k):
+            at = (step * coarse_k + k) * PITCH
             for start, count in ((0, 8), (8, coarse_y - 8)):
-                base = k * PITCH + 2 * start
+                base = at + 2 * start
                 value = q_ref[pl.ds(base + 1, count, stride=2), :] + q_ref[pl.ds(base + 2, count, stride=2), :]
-                value = value + a_ref[pl.ds(base, count, stride=2), :] + a_ref[pl.ds(base + 3, count, stride=2), :]
-                c_ref[pl.ds((step * coarse_k + k) * coarse_y + start, count), :] = value
-        return carry
-
-    lax.fori_loop(0, size_x // 2 + 2, coarsen, 0)
-    used = (size_x // 2 + 2) * coarse_k * coarse_y
+                value = value + (a_ref[pl.ds(base, count, stride=2), :] + a_ref[pl.ds(base + 3, count, stride=2), :])
+                c_ref[pl.ds((step * coarse_k + k) * coarse_y + start, count), :] = value * (SIDE / 8.0)
+
+    loop(coarse_x, along_y, 2)
+    used = coarse_x * coarse_k * coarse_y
     c_ref[pl.ds(used, c_ref.shape[0] - used), :] = jnp.zeros((c_ref.shape[0] - used, LANES), jnp.float32)
+    keep = pltpu.make_async_copy(c_ref, share_ref, sem)
+    keep.start()
     to_messages(c_ref, out_ref)
+    keep.wait()
 
 
 def to_messages(c_ref, out_ref):
@@ -218,14 +252,16 @@
         share_kernel,
         out_shape=(jax.ShapeDtypeStruct((rows, LANES), jnp.float32),) * 2,
         in_specs=[pl.BlockSpec(memory_space=pltpu.VMEM)],
-        out_specs=(pl.BlockSpec(memory_space=pltpu.VMEM),) * 2,
+        out_specs=(pl.BlockSpec(memory_space=pltpu.VMEM), pl.BlockSpec(memory_space=pltpu.HBM)),
         scratch_shapes=[
-            vmem((size_x + 4) * (half + 4) * PITCH + 8),
-            vmem((size_x + 6) * (half + 2) * PITCH + 8),
-            vmem((half // 2 + 1) * PITCH + 8),
-            vmem((half // 2 + 1) * PITCH + 8),
+            vmem(rows),
+            vmem((size_x + 2) * (half + 4) * PITCH + 8),
+            vmem((size_x + 2) * (half + 2) * PITCH + 8),
+            vmem((size_x // 2 + 2) * (half // 2 + 1) * PITCH + 8),
+            vmem((size_x // 2 + 2) * (half // 2 + 1) * PITCH + 8),
+            pltpu.SemaphoreType.DMA,
         ],
-        compiler_params=pltpu.CompilerParams(vmem_limit_bytes=40 << 20),
+        compiler_params=pltpu.CompilerParams(vmem_limit_bytes=16 << 20),
         cost_estimate=pl.CostEstimate(flops=20_000_000, bytes_accessed=2_000_000, transcendentals=0),
         name="share",
     )(density)
@@ -468,71 +504,24 @@
         in_specs=[pl.BlockSpec(memory_space=pltpu.VMEM)] * 2,
         out_specs=pl.BlockSpec(memory_space=pltpu.VMEM),
         scratch_shapes=[vmem(rows)] + fields + [vmem(512), vmem(256)],
-        compiler_params=pltpu.CompilerParams(vmem_limit_bytes=40 << 20),
+        compiler_params=pltpu.CompilerParams(vmem_limit_bytes=16 << 20),
         cost_estimate=pl.CostEstimate(flops=20_000_000, bytes_accessed=2_000_000, transcendentals=0),
         name="solve",
     )(received, dense)
 
 
-def loop(count, body):
-    def step(i, carry):
-        body(i)
-        return carry
-
-    lax.fori_loop(0, count, step, 0)
-
-
-def smoothed(ref, row, x, j, y, centre):
-    around = centre[j - 1] + centre[j + 1]
-    around = around + ref[pl.ds(row(x, j, y - 1), 8), :] + ref[pl.ds(row(x, j, y + 1), 8), :]
-    around = around + ref[pl.ds(row(x - 1, j, y), 8), :] + ref[pl.ds(row(x + 1, j, y), 8), :]
-    return KEEP * centre[j] + SIDE * around
-
-
-def column(ref, row, x, y, first, last):
-    return {j: ref[pl.ds(row(x, j, y), 8), :] for j in range(first, last)}
-
-
-def edge_lanes(flags):
-    low = lax.broadcasted_iota(jnp.int32, (8, LANES), 1) < PAIRS
-    return jnp.where(low, flags[4], 1.0), jnp.where(low, 1.0, flags[5])
-
-
-def inside(value, mask, j, half, z_first, z_last):
-    value = value * mask
-    if j < 0:
-        value = value * z_first
-    if j >= half:
-        value = value * z_last
-    return value
-
-
-def plane_scale(flags, x, size_x):
-    return jnp.where(x < 0, flags[0], jnp.where(x >= size_x, flags[1], 1.0))
-
-
-def local_kernel(
-    rho_ref, zlo_ref, zhi_ref, ylo_ref, yhi_ref, xlo_ref, xhi_ref, psi_ref, both_ref, r_ref, v_ref, p_ref
-):
+def faces_kernel(rho_ref, zlo_ref, zhi_ref, own_ref, first_ref, last_ref, x_ref):
     size_x, size_y, merged = rho_ref.shape
-    tiles = merged // LANES
-    half = tiles
-    r_slots, v_slots, p_slots = half + 6, half + 4, half + 2
-    flags = device_flags()
-
-    def r_row(x, j, y):
-        return ((x + 3) * r_slots + (j + 3)) * PITCH + (y + 3)
-
-    def v_row(x, j, y):
-        return ((x + 2) * v_slots + (j + 2)) * PITCH + (y + 2)
-
-    def p_row(x, j, y):
-        return ((x + 1) * p_slots + (j + 1)) * PITCH + (y + 1)
+    half = merged // LANES
+    slots_in_all = half + 6
+
+    def own_row(x, j, y):
+        return (x * slots_in_all + (j + 3)) * size_y + y
 
     def lanes(ref, at, rows):
         return [ref[at, rows, pl.ds(LANES * k, LANES)] for k in range(ref.shape[2] // LANES)]
 
-    def pack_own(x):
+    def pack(x):
         for i in range(size_y // 8):
             rows = pl.ds(8 * i, 8)
             packed = pack_tiles(lanes(rho_ref, x, rows))
@@ -545,29 +534,87 @@
             for j in range(3):
                 slots[half + j] = half_select(swap(packed[j]), outer[j])
             for j, value in slots.items():
-                r_ref[pl.ds(r_row(x, j, 8 * i), 8), :] = value
-
-    def pack_wide(tile, x, y, count):
+                own_ref[pl.ds(own_row(x, j, 8 * i), 8), :] = value
+            for j in range(-2, half + 2):
+                if i == 0:
+                    first_ref[x, pl.ds((j + 2) * 3, 3), :] = slots[j][:3]
+                if i == size_y // 8 - 1:
+                    last_ref[x, pl.ds((j + 2) * 3, 3), :] = slots[j][5:]
+
+    loop(size_x, pack, 2)
+    start = jnp.where(lax.axis_index("gx") == 0, size_x - 3, 0)
+    for i in range(3):
         for j in range(-2, half + 2):
-            first, second = tile[(j + 2) // 2], tile[(j + 2) // 2 + half // 2]
-            if j % 2 == 0:
-                value = half_select(first, swap(second))
-            else:
-                value = half_select(swap(first), second)
-            r_ref[pl.ds(r_row(x, j, y), count), :] = value
-
-    def pack_plane(x):
-        pack_own(x)
-        pack_wide(lanes(ylo_ref, x, pl.ds(0, 3)), x, -3, 3)
-        pack_wide(lanes(yhi_ref, x, pl.ds(0, 3)), x, size_y, 3)
-
-    def pack_outer(i):
-        for ref, x in ((xlo_ref, i - 3), (xhi_ref, i + size_x)):
-            for start, count in ((0, 8), (8, 8), (16, 4)):
-                pack_wide(lanes(ref, i, pl.ds(start, count)), x, start - 2, count)
-
-    loop(size_x, pack_plane)
-    loop(3, pack_outer)
+            for y in range(0, size_y, 8):
+                x_ref[pl.ds((i * (half + 4) + (j + 2)) * size_y + y, 8), :] = own_ref[pl.ds(own_row(start + i, j, y), 8), :]
+
+
+def faces(density, zlo, zhi):
+    size_x, size_y, merged = density.shape
+    half = merged // LANES
+    rows = -(-3 * (half + 4) // 8) * 8
+    shape = lambda *dims: jax.ShapeDtypeStruct(dims + (LANES,), jnp.float32)
+    return pl.pallas_call(
+        faces_kernel,
+        out_shape=(
+            shape(size_x * (half + 6) * size_y),
+            shape(size_x, rows),
+            shape(size_x, rows),
+            shape(3 * (half + 4) * size_y),
+        ),
+        in_specs=[pl.BlockSpec(memory_space=pltpu.VMEM)] * 3,
+        out_specs=(pl.BlockSpec(memory_space=pltpu.VMEM),) * 4,
+        compiler_params=pltpu.CompilerParams(vmem_limit_bytes=12 << 20),
+        cost_estimate=pl.CostEstimate(flops=8_000_000, bytes_accessed=2_000_000, transcendentals=0),
+        name="faces",
+    )(density, zlo, zhi)
+
+
+def local_kernel(
+    shape, own_ref, ylo_ref, yhi_ref, x_ref, edge_ref, psi_ref, both_any, r_ref, v_ref, p_ref, both_ref, sem
+):
+    size_x, size_y, merged = shape
+    half = merged // LANES
+    r_slots, v_slots, p_slots = half + 6, half + 4, half + 2
+    flags = device_flags()
+
+    def own_row(x, j, y):
+        return (x * r_slots + (j + 3)) * size_y + y
+
+    def r_row(x, j, y):
+        return ((x + 3) * r_slots + (j + 3)) * PITCH + (y + 3)
+
+    def v_row(x, j, y):
+        return ((x + 2) * v_slots + (j + 2)) * PITCH + (y + 2)
+
+    def p_row(x, j, y):
+        return ((x + 1) * p_slots + (j + 1)) * PITCH + (y + 1)
+
+    def place(x):
+        for j in range(-3, half + 3):
+            for y in range(0, size_y, 8):
+                r_ref[pl.ds(r_row(x, j, y), 8), :] = own_ref[pl.ds(own_row(x, j, y), 8), :]
+        for j in range(-2, half + 2):
+            r_ref[pl.ds(r_row(x, j, -3), 3), :] = ylo_ref[x, pl.ds((j + 2) * 3, 3), :]
+            r_ref[pl.ds(r_row(x, j, size_y), 3), :] = yhi_ref[x, pl.ds((j + 2) * 3, 3), :]
+
+    loop(size_x, place, 2)
+
+    def place_outer(i):
+        for j in range(-2, half + 2):
+            for y in range(0, size_y, 8):
+                value = x_ref[pl.ds((i * (half + 4) + (j + 2)) * size_y + y, 8), :]
+                r_ref[pl.ds(r_row(i - 3, j, y), 8), :] = value * flags[0]
+                r_ref[pl.ds(r_row(i + size_x, j, y), 8), :] = value * flags[1]
+
+    loop(3, place_outer)
+    for i in range(2):
+        for j in range(-2, half + 2):
+            low = edge_ref[i, pl.ds((j + 2) * 3 + 1, 2), :]
+            high = edge_ref[i + 2, pl.ds((j + 2) * 3, 2), :]
+            for x, scale in ((i - 2, flags[0]), (i + size_x, flags[1])):
+                r_ref[pl.ds(r_row(x, j, -2), 2), :] = low * scale
+                r_ref[pl.ds(r_row(x, j, size_y), 2), :] = high * scale
 
     z_first, z_last = edge_lanes(flags)
     masks = [row_mask(-2 + 8 * i, 2, size_y, flags[2], flags[3]) for i in range(3)]
@@ -580,8 +627,8 @@
             centre = column(r_ref, r_row, x, y, -3, half + 3)
             mask = masks[n] * scale
             for j in range(-2, half + 2):
-                value = inside(smoothed(r_ref, r_row, x, j, y, centre), mask, j, half, z_first, z_last)
-                v_ref[pl.ds(v_row(x, j, y), 8), :] = SIDE * (centre[j] + value)
+                value = inside(weighted(r_ref, r_row, x, j, y, centre), mask, j, half, z_first, z_last)
+                v_ref[pl.ds(v_row(x, j, y), 8), :] = centre[j] + value
 
     loop(size_x + 4, first_sweep)
     masks_1 = [row_mask(-1 + 8 * i, 1, size_y, flags[2], flags[3]) for i in range(3)]
@@ -594,76 +641,102 @@
             centre = column(v_ref, v_row, x, y, -2, half + 2)
             mask = masks_1[n] * scale
             for j in range(-1, half + 1):
-                value = smoothed(v_ref, v_row, x, j, y, centre) + SIDE * r_ref[pl.ds(r_row(x, j, y), 8), :]
-                p_ref[pl.ds(p_row(x, j, y), 8), :] = inside(value, mask, j, half, z_first, z_last)
+                value = inside(weighted(v_ref, v_row, x, j, y, centre), mask, j, half, z_first, z_last)
+                p_ref[pl.ds(p_row(x, j, y), 8), :] = r_ref[pl.ds(r_row(x, j, y), 8), :] + value
 
     loop(size_x + 2, second_sweep)
-    both_ref[...] = jnp.zeros_like(both_ref)
 
     def third_sweep(x):
-        left, right = [], []
         for n in range(size_y // 8):
             y = 8 * n
             centre = column(p_ref, p_row, x, y, -1, half + 1)
             for j in range(half):
                 rho = r_ref[pl.ds(r_row(x, j, y), 8), :]
-                value = smoothed(p_ref, p_row, x, j, y, centre) + SIDE * rho
+                value = SIDE * rho + (SIDE * SIDE) * weighted(p_ref, p_row, x, j, y, centre)
                 psi_ref[pl.ds((x * half + j) * size_y + y, 8), :] = value
-                left.append(rho)
-                right.append(value)
-        both_ref[...] += lax.dot_general(
-            jnp.concatenate(left, axis=0), jnp.concatenate(right, axis=0), (((0,), (0,)), ((), ())),
-            precision=lax.Precision.HIGHEST, preferred_element_type=jnp.float32,
-        )
 
     loop(size_x, third_sweep)
-
-
-def local_part(density, halos):
-    size_x, size_y, merged = density.shape
+    left = jnp.concatenate([own_ref[pl.ds(own_row(x, 0, 0), half * size_y), :] for x in range(size_x)], axis=0)
+    both_ref[...] = lax.dot_general(
+        left, psi_ref[...], (((0,), (0,)), ((), ())),
+        precision=lax.Precision.HIGHEST, preferred_element_type=jnp.float32,
+    )
+    keep = pltpu.make_async_copy(both_ref, both_any, sem)
+    keep.start()
+    keep.wait()
+
+
+def local_part(shape, own, halos):
+    size_x, size_y, merged = shape
     half = merged // LANES
     vmem = lambda n: pltpu.VMEM((n, LANES), jnp.float32)
     return pl.pallas_call(
-        local_kernel,
+        functools.partial(local_kernel, shape),
         out_shape=(
             jax.ShapeDtypeStruct((size_x * half * size_y, LANES), jnp.float32),
             jax.ShapeDtypeStruct((LANES, LANES), jnp.float32),
         ),
-        in_specs=[pl.BlockSpec(memory_space=pltpu.VMEM)] * 7,
-        out_specs=(pl.BlockSpec(memory_space=pltpu.VMEM),) * 2,
+        in_specs=[pl.BlockSpec(memory_space=pltpu.VMEM)] * 5,
+        out_specs=(pl.BlockSpec(memory_space=pltpu.VMEM), pl.BlockSpec(memory_space=pltpu.HBM)),
         scratch_shapes=[
             vmem((size_x + 6) * (half + 6) * PITCH + 8),
             vmem((size_x + 4) * (half + 4) * PITCH + 8),
             vmem((size_x + 2) * (half + 2) * PITCH + 8),
+            vmem(LANES),
+            pltpu.SemaphoreType.DMA,
         ],
-        compiler_params=pltpu.CompilerParams(vmem_limit_bytes=40 << 20),
+        compiler_params=pltpu.CompilerParams(vmem_limit_bytes=20 << 20),
         cost_estimate=pl.CostEstimate(flops=30_000_000, bytes_accessed=4_000_000, transcendentals=0),
         name="local_part",
-    )(density, *halos)
-
-
-def gram_kernel(copies, in_ref, share_ref, both_ref, c_ref, block_ref):
+    )(own, *halos)
+
+
+def gram_kernel(copies, in_ref, share_any, both_any, c_ref, block_ref, share_ref, both_ref, sems):
+    moves = [
+        pltpu.make_async_copy(share_any, share_ref, sems.at[0]),
+        pltpu.make_async_copy(both_any, both_ref, sems.at[1]),
+    ]
+    for move in moves:
+        move.start()
     from_messages(in_ref, c_ref)
+    for move in moves:
+        move.wait()
     both = both_ref[...] + 8.0 * lax.dot_general(
         share_ref[...], c_ref[...], (((0,), (0,)), ((), ())),
         precision=lax.Precision.HIGHEST, preferred_element_type=jnp.float32,
     )
     whole = both[:PAIRS] + swap(both[PAIRS:])
-    flat = half_select(whole[: PAIRS // 2], swap(whole[PAIRS // 2 :]))
+    quarter = PAIRS // 2
+    corner = pltpu.roll(whole[quarter:], LANES - quarter, 1)
+    row = lax.broadcasted_iota(jnp.int32, (quarter, LANES), 0)
+    lane = lax.broadcasted_iota(jnp.int32, (quarter, LANES), 1)
+    packed = jnp.where(row > lane, corner, whole[:quarter])
+    diagonal = jnp.sum(jnp.where(row == lane, corner, 0.0), axis=0, keepdims=True)
+    flat = half_select(packed[: quarter // 2], swap(packed[quarter // 2 :]))
+    last = jnp.concatenate([diagonal, jnp.zeros((3, LANES), jnp.float32)], axis=0)
+    groups = block_ref.shape[0] // copies
     for i in range(copies):
-        block_ref[i] = flat
+        for g in range(groups - 1):
+            block_ref[i * groups + g] = flat[4 * g : 4 * g + 4]
+        block_ref[i * groups + groups - 1] = last
 
 
 def gram(received, shares, both, copies):
+    groups = PAIRS // 16 + 1
     return pl.pallas_call(
         functools.partial(gram_kernel, copies),
         out_shape=(
             jax.ShapeDtypeStruct(received.shape, jnp.float32),
-            jax.ShapeDtypeStruct((copies, PAIRS // 2, LANES), jnp.float32),
+            jax.ShapeDtypeStruct((copies * groups, 4, LANES), jnp.float32),
         ),
-        in_specs=[pl.BlockSpec(memory_space=pltpu.VMEM)] * 3,
+        in_specs=[pl.BlockSpec(memory_space=pltpu.VMEM)] + [pl.BlockSpec(memory_space=pltpu.HBM)] * 2,
         out_specs=(pl.BlockSpec(memory_space=pltpu.VMEM),) * 2,
-        compiler_params=pltpu.CompilerParams(vmem_limit_bytes=16 << 20),
+        scratch_shapes=[
+            pltpu.VMEM(shares.shape, jnp.float32),
+            pltpu.VMEM(both.shape, jnp.float32),
+            pltpu.SemaphoreType.DMA((2,)),
+        ],
+        compiler_params=pltpu.CompilerParams(vmem_limit_bytes=8 << 20),
         name="gram",
     )(received, shares, both)
 
@@ -694,7 +767,7 @@
             e_ref[pl.ds(base, coarse_y, stride=2), :] = slots[k]
             e_ref[pl.ds(base + 1, coarse_y, stride=2), :] = slots[k]
 
-    loop(size_x // 2 + 2, spread)
+    loop(size_x // 2 + 2, spread, 5)
     z_first, z_last = edge_lanes(flags)
     masks = [row_mask(-1 + 8 * i, 1, size_y, flags[2], flags[3]) for i in range(3)]
 
@@ -709,11 +782,11 @@
                 for jc in range(-1, half // 2 + 1):
                     around = here[-1 - d][jc] + e_ref[pl.ds(e_row(xc + d, jc, y - 1), 8), :]
                     around = around + e_ref[pl.ds(e_row(xc + d, jc, y + 1), 8), :]
-                    base[jc] = (KEEP + 2.0 * SIDE) * here[d][jc] + SIDE * around
+                    base[jc] = (RATIO + 2.0) * here[d][jc] + around
                 for j in range(-1, half + 1):
                     jc = j // 2
                     other = jc + (1 if j % 2 else -1)
-                    value = base[jc] + SIDE * here[d][other]
+                    value = base[jc] + here[d][other]
                     u_ref[pl.ds(u_row(x, j, y), 8), :] = inside(value, mask, j, half, z_first, z_last)
 
     loop(size_x // 2 + 1, first)
@@ -725,11 +798,11 @@
             slots = []
             for j in range(half):
                 psi = psi_ref[pl.ds((x * half + j) * size_y + y, 8), :]
-                slots.append(smoothed(u_ref, u_row, x, j, y, centre) + psi)
+                slots.append(SIDE * weighted(u_ref, u_row, x, j, y, centre) + psi)
             for k, value in enumerate(unpack_slots(slots)):
                 out_ref[x, pl.ds(y, 8), pl.ds(LANES * k, LANES)] = value
 
-    loop(size_x, second)
+    loop(size_x, second, 2)
 
 
 def correct(rows, psi, shape):
@@ -745,40 +818,55 @@
             vmem((size_x // 2 + 2) * (half // 2 + 2) * PITCH + 8),
             vmem((size_x + 2) * (half + 2) * PITCH + 8),
         ],
-        compiler_params=pltpu.CompilerParams(vmem_limit_bytes=24 << 20),
+        compiler_params=pltpu.CompilerParams(vmem_limit_bytes=12 << 20),
         cost_estimate=pl.CostEstimate(flops=20_000_000, bytes_accessed=2_000_000, transcendentals=0),
         name="correct",
     )(rows, psi)
 
 
-def total_kernel(scale, in_ref, out_ref):
-    total = in_ref[0]
-    for i in range(1, in_ref.shape[0]):
-        total = total + in_ref[i]
-    total = total * scale
-    half = PAIRS // 2
-    out_ref[pl.ds(0, half), :] = total[:, :PAIRS]
-    out_ref[pl.ds(half, half), :] = swap(total)[:, :PAIRS]
+def total_kernel(scale, groups, in_ref, out_ref):
+    copies = in_ref.shape[0] // groups
+    sums = []
+    for g in range(groups):
+        terms = [in_ref[i * groups + g] for i in range(copies)]
+        while len(terms) > 1:
+            terms = [terms[i] + terms[i + 1] for i in range(0, len(terms) - 1, 2)] + terms[len(terms) & ~1 :]
+        sums.append(terms[0] * scale)
+    flat = jnp.concatenate(sums[:-1], axis=0)
+    diagonal = sums[-1][:1]
+    quarter = PAIRS // 2
+    packed = jnp.concatenate([flat, swap(flat)], axis=0)
+    tall = jnp.concatenate([packed, jnp.zeros((LANES - quarter, LANES), jnp.float32)], axis=0)
+    turned = tall.T
+    row = lax.broadcasted_iota(jnp.int32, (quarter, LANES), 0)
+    lane = lax.broadcasted_iota(jnp.int32, (quarter, LANES), 1)
+    mirror = turned[:quarter]
+    top = jnp.where(lane >= row, packed, mirror)
+    corner = jnp.where(row > lane, packed, jnp.where(row == lane, jnp.broadcast_to(diagonal, row.shape), mirror))
+    bottom = jnp.where(lane < quarter, turned[quarter:PAIRS], pltpu.roll(corner, quarter, 1))
+    out_ref[pl.ds(0, quarter), :] = top[:, :PAIRS]
+    out_ref[pl.ds(quarter, quarter), :] = bottom[:, :PAIRS]
 
 
 def total(parts, scale):
+    groups = PAIRS // 16 + 1
     return pl.pallas_call(
-        functools.partial(total_kernel, scale),
+        functools.partial(total_kernel, scale, groups),
         out_shape=jax.ShapeDtypeStruct((PAIRS, PAIRS), jnp.float32),
         in_specs=[pl.BlockSpec(memory_space=pltpu.VMEM)],
         out_specs=pl.BlockSpec(memory_space=pltpu.VMEM),
+        compiler_params=pltpu.CompilerParams(vmem_limit_bytes=4 << 20),
         name="total",
     )(parts)
 
 
+def along(size):
+    up = [(i, i + 1) for i in range(size - 1)]
+    return up, [(j, i) for i, j in up]
+
+
 def shifted(first, last, axis):
-    size = lax.axis_size(axis)
-    where = lax.axis_index(axis)
-    if size == 2:
-        got = lax.ppermute(jnp.where(where == 0, last, first), axis, [(0, 1), (1, 0)])
-        return jnp.where(where == 0, 0.0, got), jnp.where(where == 0, got, 0.0)
-    up = [(i, i + 1) for i in range(size - 1)]
-    down = [(j, i) for i, j in up]
+    up, down = along(lax.axis_size(axis))
     return lax.ppermute(last, axis, up), lax.ppermute(first, axis, down)
 
 
@@ -798,23 +886,19 @@
     block = (size_x // 2, size_y // 2, merged // PAIRS // 2)
 
     deep = 4 * PAIRS
-    near = 2 * PAIRS
+    swapped = [(0, 1), (1, 0)]
     zlo, zhi = shifted(density[..., :deep], density[..., -deep:], "gz")
     messages, shares = share(density)
-
-    def wide_z(part):
-        return jnp.concatenate([part(zlo[..., -near:]), part(density), part(zhi[..., :near])], axis=2)
-
-    ylo, yhi = shifted(wide_z(lambda a: a[:, :3]), wide_z(lambda a: a[:, -3:]), "gy")
-
-    def wide_yz(part):
-        return jnp.concatenate([part(ylo[:, -2:]), wide_z(part), part(yhi[:, :2])], axis=1)
-
     received = exchanged(messages)
-    xlo, xhi = shifted(wide_yz(lambda a: a[:3]), wide_yz(lambda a: a[-3:]), "gx")
+    own, first, last, plane = faces(density, zlo, zhi)
+    ylo, yhi = shifted(first, last, "gy")
+    beside = lax.ppermute(plane, "gx", swapped)
     answers = solve(received, devices, block, LEVELS - 1)
     correction = exchanged(answers)
-    psi, both = local_part(density, (zlo, zhi, ylo, yhi, xlo, xhi))
+    low = lax.axis_index("gx") == 0
+    edge = jnp.concatenate([jnp.where(low, a[-2:], a[:2]) for a in (ylo, yhi)], axis=0)
+    edge = lax.ppermute(edge, "gx", swapped)
+    psi, both = local_part(density.shape, own, (ylo, yhi, beside, edge))
     rows, parts = gram(correction, shares, both, count)
     parts = lax.all_to_all(parts, AXES, 0, 0, tiled=True)
     potential = correct(rows, psi, density.shape)
@@ -960,12 +1044,13 @@
     return (solved.reshape(cells_x, cells_y, merged), coulomb)
 
 
-def suits(shape, count):
+def suits(shape, count, devices_x):
     size_x, size_y, merged = shape
     size_z = merged // PAIRS
     equal = size_x == size_y == size_z
     return (
         2 * PAIRS == LANES
+        and devices_x == 2
         and PAIRS % count == 0
         and equal
         and size_x % 8 == 0
@@ -979,7 +1064,7 @@
     count = 1
     for axis in AXES:
         count *= lax.axis_size(axis)
-    if suits(density.shape, count):
+    if suits(density.shape, count, lax.axis_size("gx")):
         return fast_local(density)
     return general_local(density)
 

time: 80.6 us -> 69.9 us (0.87)
  Pallas kernels: 24.7 us -> 17.1 us
  waiting for transfers between devices: 18.3 us -> 12.9 us
  starting transfers between devices: 28.1 us -> 31.5 us
  other arithmetic: 2.05 us -> 0.02 us
  local copies, waits for them, and re-layouts: 6.07 us -> 6.93 us
    ppermute x4, waiting for transfers between devices: 6.83 us -> 0.01 us  [shifted(): return (lax.ppermute(last, axis, up), lax.ppermute(first, axis, down))]
    pallas_call x2 -> x3, Pallas kernels: 11.2 us -> 7.01 us  [the longest x1 3.98 us: local_part(): pl.pallas_call(functools.partial(local_kernel, shape), out_shape=(jax.Sha...]
    ppermute x1 -> x2, waiting for transfers between devices: 0.01 us -> 3.79 us  [the longest x1 3.79 us: fast_local(): edge = lax.ppermute(edge, 'gx', swapped)]
    all_to_all x1, waiting for transfers between devices: 11.5 us -> 9.06 us  [fast_local(): parts = lax.all_to_all(parts, AXES, 0, 0, tiled=True)]
    pallas_call x1, Pallas kernels: 5 us -> 2.75 us  [share(): pl.pallas_call(share_kernel, out_shape=(jax.ShapeDtypeStruct((rows, LANES...]
    all_to_all x2, starting transfers between devices: 9.5 us -> 11.4 us  [exchanged(): lax.all_to_all(shaped, axes, 0, 0, tiled=True).reshape(messages.shape)]
    select_n x2, other arithmetic: 1.89 us -> 0.01 us  [fast_local(): jnp.where(low, a[-2:], a[:2])]
    unnamed x18 -> x20, local copies, waits for them, and re-layouts: 3.94 us -> 5.77 us
  transfers between devices with their start and end apart: 8 -> 9, of which waited for: 3 -> 3; matrix products, arithmetic and copies ran while one was open for 4% -> 0% of each run, Pallas kernels for 27% -> 21%
where the time goes in v3:
time: 69.9 us; the launch traced here: 69.4 us
  starting transfers between devices  31.5 us (45%)
  Pallas kernels  17.1 us (24%)
  waiting for transfers between devices  12.9 us (18%)
  local copies, waits for them, and re-layouts  6.93 us (10%)
  between operations  0.84 us (1%)
    all_to_all x2, starting transfers between devices, exchanged(): lax.all_to_all(shaped, axes, 0, 0, tiled=True).reshape(messages.shape)  11.4 us
    ppermute x4, starting transfers between devices, shifted(): return (lax.ppermute(last, axis, up), lax.ppermute(first, axis, down))  10.9 us
    all_to_all x1, waiting for transfers between devices, fast_local(): parts = lax.all_to_all(parts, AXES, 0, 0, tiled=True)  9.06 us
    all_to_all x1, starting transfers between devices, fast_local(): parts = lax.all_to_all(parts, AXES, 0, 0, tiled=True)  6.36 us
    unnamed x20, local copies, waits for them, and re-layouts  5.77 us
    pallas_call x1, Pallas kernels, local_part(): pl.pallas_call(functools.partial(local_kernel, shape), out_shape=(jax.Sha...  3.98 us
    ppermute x1, waiting for transfers between devices, fast_local(): edge = lax.ppermute(edge, 'gx', swapped)  3.79 us
    pallas_call x1, Pallas kernels, solve(): pl.pallas_call(functools.partial(solve_kernel, devices, own, block, level...  3.23 us
  transfers between devices with their start and end apart: 9, of which 3 were waited for; matrix products, arithmetic and copies ran while one was open for 0% of the time, Pallas kernels for 21%

profile of v3, /device:TPU:1, one launch (start us, length us, event | category | flops | bytes accessed | tf_op | source)
XLA Modules:
  0.0 69.4 jit_solution(6441256628296993241)
XLA Ops:
  0.6 1.2 %fusion = (f32[16,16,256]{2,1,0:T(8,128)S(1)}, f32[16,16,256]{2,1,0:T(8,128)S(1)}) fusion(f32[16,16,1024]{2,1,0:T(8,128)} %rho_ref.3), kind=kLoop, calls=%fused_computation.3 | loop fusion | bytes 1048576 | tf_op jit(solution)/shard_map/slice | solution.py:890
  1.8 4.0 %collective-permute-start = (f32[16,16,256]{2,1,0:T(8,128)S(1)}, f32[16,16,256]{2,1,0:T(8,128)S(1)}, u32[]{:S(2)}, u32[]{:S(2)}) collective-permute-start(f32[16,16,256]{2,1,0:T(8,128)S(1)} %get-tuple-element.23), channel_id=1, source_target_pairs={{0,1},{1,2},{2,3},{4,5},{5,6},{6,7},{8,9},{9,10},{10,11},{12,13},{... | collective-permute-start | bytes 786440 | tf_op jit(solution)/shard_map/ppermute | solution.py:870
  5.8 1.3 %collective-permute-start.1 = (f32[16,16,256]{2,1,0:T(8,128)S(1)}, f32[16,16,256]{2,1,0:T(8,128)S(1)}, u32[]{:S(2)}, u32[]{:S(2)}) collective-permute-start(f32[16,16,256]{2,1,0:T(8,128)S(1)} %get-tuple-element.22), channel_id=1, source_target_pairs={{1,0},{2,1},{3,2},{5,4},{6,5},{7,6},{9,8},{10,9},{11,10},{13,12},{... | collective-permute-start | bytes 786440 | tf_op jit(solution)/shard_map/ppermute | solution.py:870
  7.2 1.2 %copy-done = f32[16,16,1024]{2,1,0:T(8,128)S(1)} copy-done((f32[16,16,1024]{2,1,0:T(8,128)S(1)}, f32[16,16,1024]{2,1,0:T(8,128)}, u32[]{:S(2)}) %copy-start) | copy-done | bytes 1048600
  8.4 2.8 %share.1 = (f32[512,128]{1,0:T(8,128)}, f32[512,128]{1,0:T(8,128)S(1)}) custom-call(f32[16,16,1024]{2,1,0:T(8,128)S(1)} %copy-done), custom_call_target="tpu_custom_call" | custom-call | flops 20000000 | bytes 2000000 | tf_op jit(solution)/shard_map/share/pallas_call | solution.py:251
  11.1 0.7 %copy-done.5 = f32[512,128]{1,0:T(8,128)} copy-done((f32[512,128]{1,0:T(8,128)}, f32[512,128]{1,0:T(8,128)S(1)}, u32[]{:S(2)}) %copy-start.5) | copy-done | bytes 262168
  11.8 7.6 %all-to-all-start = ((f32[32,16,128]{2,1,0:T(8,128)}), f32[32,16,128]{2,1,0:T(8,128)S(1)}, u32[]{:S(2)}, u32[]{:S(2)}) async-start(f32[32,16,128]{2,1,0:T(8,128)} %bitcast), calls=%async_computation | async-start | bytes 524288 | tf_op jit(solution)/shard_map/all_to_all | solution.py:879
  20.2 0.9 %copy-done.8 = f32[16,16,256]{2,1,0:T(8,128)S(1)} copy-done((f32[16,16,256]{2,1,0:T(8,128)S(1)}, f32[16,16,256]{2,1,0:T(8,128)}, u32[]{:S(2)}) %copy-start.8) | copy-done | bytes 262168
  21.1 2.2 %faces.1 = (f32[3584,128]{1,0:T(8,128)S(1)}, f32[16,40,128]{2,1,0:T(8,128)}, f32[16,40,128]{2,1,0:T(8,128)}, f32[576,128]{1,0:T(8,128)S(1)}) custom-call(f32[16,16,1024]{2,1,0:T(8,128)S(1)} %copy-done.1, f32[16,16,256]{2,1,0:T(8,128)S(1)} %collective-permute-done.zlo_ref, f32[16,16,256]{2,1,0:T(8,128)S(1)} %copy-done.8), custom_call_target="tpu_custom_call" | custom-call | flops 8000000 | bytes 2000000 | tf_op jit(solution)/shard_map/faces/pallas_call | solution.py:557
  23.3 2.2 %collective-permute-start.3 = (f32[16,40,128]{2,1,0:T(8,128)}, f32[16,40,128]{2,1,0:T(8,128)S(1)}, u32[]{:S(2)}, u32[]{:S(2)}) collective-permute-start(f32[16,40,128]{2,1,0:T(8,128)} %get-tuple-element.16), channel_id=1, source_target_pairs={{4,0},{8,4},{12,8},{5,1},{9,5},{13,9},{6,2},{10,6},{14,10},{7,3},{... | collective-permute-start | bytes 983048 | tf_op jit(solution)/shard_map/ppermute | solution.py:870
  25.5 3.4 %collective-permute-start.2 = (f32[16,40,128]{2,1,0:T(8,128)}, f32[16,40,128]{2,1,0:T(8,128)S(1)}, u32[]{:S(2)}, u32[]{:S(2)}) collective-permute-start(f32[16,40,128]{2,1,0:T(8,128)} %get-tuple-element.15), channel_id=1, source_target_pairs={{0,4},{4,8},{8,12},{1,5},{5,9},{9,13},{2,6},{6,10},{10,14},{3,7},{... | collective-permute-start | bytes 983048 | tf_op jit(solution)/shard_map/ppermute | solution.py:870
  28.9 1.4 %collective-permute-start.4 = (f32[576,128]{1,0:T(8,128)}, f32[576,128]{1,0:T(8,128)S(1)}, u32[]{:S(2)}, u32[]{:S(2)}) collective-permute-start(f32[576,128]{1,0:T(8,128)} %copy-done.9), channel_id=1, source_target_pairs={{0,16},{16,0},{1,17},{17,1},{2,18},{18,2},{3,19},{19,3},{4,20},{20... | collective-permute-start | bytes 884744 | tf_op jit(solution)/shard_map/ppermute | solution.py:895
  30.3 1.2 %copy-done.2 = f32[512,512]{1,0:T(8,128)S(1)} copy-done((f32[512,512]{1,0:T(8,128)S(1)}, f32[512,512]{1,0:T(8,128)}, u32[]{:S(2)}) %copy-start.2) | copy-done | bytes 1048600
  31.5 3.2 %solve.1 = f32[512,128]{1,0:T(8,128)} custom-call(f32[512,128]{1,0:T(8,128)S(1)} %bitcast.5, f32[512,512]{1,0:T(8,128)S(1)} %copy-done.2), custom_call_target="tpu_custom_call" | custom-call | flops 20000000 | bytes 2000000 | tf_op jit(solution)/shard_map/solve/pallas_call | solution.py:501
  34.8 3.8 %all-to-all-start.1 = ((f32[32,16,128]{2,1,0:T(8,128)}), f32[32,16,128]{2,1,0:T(8,128)S(1)}, u32[]{:S(2)}, u32[]{:S(2)}) async-start(f32[32,16,128]{2,1,0:T(8,128)} %bitcast.2), calls=%async_computation.1 | async-start | bytes 524288 | tf_op jit(solution)/shard_map/all_to_all | solution.py:879
  38.7 1.4 %collective-permute-start.5 = (f32[4,40,128]{2,1,0:T(8,128)S(1)}, f32[4,40,128]{2,1,0:T(8,128)S(1)}, u32[]{:S(2)}, u32[]{:S(2)}) collective-permute-start(f32[4,40,128]{2,1,0:T(8,128)S(1)} %pad_maximum_fusion), channel_id=1, source_target_pairs={{0,16},{16,0},{1,17},{17,1},{2,18},{18,2},{3,19},{19,3},{4,20},{20... | collective-permute-start | bytes 245768 | tf_op jit(solution)/shard_map/ppermute | solution.py:900
  40.1 3.8 %collective-permute-done.5.edge_ref = f32[4,40,128]{2,1,0:T(8,128)S(1)} collective-permute-done((f32[4,40,128]{2,1,0:T(8,128)S(1)}, f32[4,40,128]{2,1,0:T(8,128)S(1)}, u32[]{:S(2)}, u32[]{:S(2)}) %collective-permute-start.5) | collective-permute-done | bytes 81952 | tf_op jit(solution)/shard_map/ppermute | solution.py:900
  43.9 4.0 %local_part.1 = (f32[2048,128]{1,0:T(8,128)S(1)}, f32[128,128]{1,0:T(8,128)S(1)}) custom-call(f32[3584,128]{1,0:T(8,128)S(1)} %get-tuple-element.14.own_ref, f32[16,40,128]{2,1,0:T(8,128)S(1)} %collective-permute-done.2.ylo_ref, f32[16,40,128]{2,1,0:T(8,128)S(1)} %collective-permute-done.3.yhi_ref, f32[576,128]{1,0:T(8,128)S(1)} %collective-permute-done.4.x_ref, ...), custom_call_target="tpu_custom_call" | custom-call | flops 30000000 | bytes 4000000 | tf_op jit(solution)/shard_map/local_part/pallas_call | solution.py:673
  47.9 1.0 %copy-done.3 = f32[2048,128]{1,0:T(8,128)} copy-done((f32[2048,128]{1,0:T(8,128)}, f32[2048,128]{1,0:T(8,128)S(1)}, u32[]{:S(2)}) %copy-start.3) | copy-done | bytes 1048600
  48.9 1.6 %gram.1 = (f32[512,128]{1,0:T(8,128)S(1)}, f32[160,4,128]{2,1,0:T(4,128)}) custom-call(f32[512,128]{1,0:T(8,128)S(1)} %bitcast.4, f32[512,128]{1,0:T(8,128)S(1)} %copy-done.6, f32[128,128]{1,0:T(8,128)S(1)} %get-tuple-element.18.both_any), custom_call_target="tpu_custom_call" | custom-call | tf_op jit(solution)/shard_map/gram/pallas_call | solution.py:726
  50.6 6.4 %all-to-all-start.2 = ((f32[160,4,128]{2,1,0:T(4,128)}), f32[160,4,128]{2,1,0:T(4,128)S(1)}, u32[]{:S(2)}, u32[]{:S(2)}) async-start(f32[160,4,128]{2,1,0:T(4,128)} %get-tuple-element.21), calls=%async_computation.2 | async-start | bytes 655360 | tf_op jit(solution)/shard_map/all_to_all | solution.py:903
  56.9 2.5 %correct.1 = f32[16,16,1024]{2,1,0:T(8,128)} custom-call(f32[512,128]{1,0:T(8,128)S(1)} %get-tuple-element.19.c_ref, f32[2048,128]{1,0:T(8,128)S(1)} %copy-done.4), custom_call_target="tpu_custom_call" | custom-call | flops 20000000 | bytes 2000000 | tf_op jit(solution)/shard_map/correct/pallas_call | solution.py:812
  59.5 9.1 %all-to-all-done.2.in_ref = f32[160,4,128]{2,1,0:T(4,128)S(1)} async-done(((f32[160,4,128]{2,1,0:T(4,128)}), f32[160,4,128]{2,1,0:T(4,128)S(1)}, u32[]{:S(2)}, u32[]{:S(2)}) %all-to-all-start.2) | async-done | bytes 327712 | tf_op jit(solution)/shard_map/all_to_all | solution.py:903
  68.5 0.8 %total.1 = f32[64,64]{1,0:T(8,128)} custom-call(f32[160,4,128]{2,1,0:T(4,128)S(1)} %all-to-all-done.2.in_ref), custom_call_target="tpu_custom_call" | custom-call | tf_op jit(solution)/shard_map/total/pallas_call | solution.py:853
  (25 shorter events, 0.8 us)
Async XLA Ops:
  0.6 19.6 %copy-start.1 = (f32[16,16,1024]{2,1,0:T(8,128)S(1)}, f32[16,16,1024]{2,1,0:T(8,128)}, u32[]{:S(2)}) copy-start(f32[16,16,1024]{2,1,0:T(8,128)} %rho_ref.3) | copy-start | bytes 3145732
  1.8 17.7 %collective-permute-start = (f32[16,16,256]{2,1,0:T(8,128)S(1)}, f32[16,16,256]{2,1,0:T(8,128)S(1)}, u32[]{:S(2)}, u32[]{:S(2)}) collective-permute-start(f32[16,16,256]{2,1,0:T(8,128)S(1)} %get-tuple-element.23), channel_id=1, source_target_pairs={{0,1},{1,2},{2,3},{4,5},{5,6},{6,7},{8,9},{9,10},{10,11},{12,13},{... | collective-permute-start | bytes 786440 | tf_op jit(solution)/shard_map/ppermute | solution.py:870
  5.8 13.6 %collective-permute-start.1 = (f32[16,16,256]{2,1,0:T(8,128)S(1)}, f32[16,16,256]{2,1,0:T(8,128)S(1)}, u32[]{:S(2)}, u32[]{:S(2)}) collective-permute-start(f32[16,16,256]{2,1,0:T(8,128)S(1)} %get-tuple-element.22), channel_id=1, source_target_pairs={{1,0},{2,1},{3,2},{5,4},{6,5},{7,6},{9,8},{10,9},{11,10},{13,12},{... | collective-permute-start | bytes 786440 | tf_op jit(solution)/shard_map/ppermute | solution.py:870
  7.1 1.2 %copy-start = (f32[16,16,1024]{2,1,0:T(8,128)S(1)}, f32[16,16,1024]{2,1,0:T(8,128)}, u32[]{:S(2)}) copy-start(f32[16,16,1024]{2,1,0:T(8,128)} %rho_ref.3) | copy-start | bytes 3145732
  11.1 0.7 %copy-start.5 = (f32[512,128]{1,0:T(8,128)}, f32[512,128]{1,0:T(8,128)S(1)}, u32[]{:S(2)}) copy-start(f32[512,128]{1,0:T(8,128)S(1)} %get-tuple-element.13.share_any) | copy-start | bytes 786436
  11.8 18.5 %all-to-all-start = ((f32[32,16,128]{2,1,0:T(8,128)}), f32[32,16,128]{2,1,0:T(8,128)S(1)}, u32[]{:S(2)}, u32[]{:S(2)}) async-start(f32[32,16,128]{2,1,0:T(8,128)} %bitcast), calls=%async_computation | async-start | bytes 524288 | tf_op jit(solution)/shard_map/all_to_all | solution.py:879
  19.5 0.7 %copy-start.7 = (f32[16,16,256]{2,1,0:T(8,128)}, f32[16,16,256]{2,1,0:T(8,128)S(1)}, u32[]{:S(2)}) copy-start(f32[16,16,256]{2,1,0:T(8,128)S(1)} %collective-permute-done.1.zhi_ref) | copy-start | bytes 786436
  20.2 1.0 %copy-start.8 = (f32[16,16,256]{2,1,0:T(8,128)S(1)}, f32[16,16,256]{2,1,0:T(8,128)}, u32[]{:S(2)}) copy-start(f32[16,16,256]{2,1,0:T(8,128)} %copy-done.7) | copy-start | bytes 786436
  23.3 2.2 %copy-start.9 = (f32[576,128]{1,0:T(8,128)}, f32[576,128]{1,0:T(8,128)S(1)}, u32[]{:S(2)}) copy-start(f32[576,128]{1,0:T(8,128)S(1)} %get-tuple-element.17) | copy-start | bytes 884740
  23.3 15.3 %collective-permute-start.3 = (f32[16,40,128]{2,1,0:T(8,128)}, f32[16,40,128]{2,1,0:T(8,128)S(1)}, u32[]{:S(2)}, u32[]{:S(2)}) collective-permute-start(f32[16,40,128]{2,1,0:T(8,128)} %get-tuple-element.16), channel_id=1, source_target_pairs={{4,0},{8,4},{12,8},{5,1},{9,5},{13,9},{6,2},{10,6},{14,10},{7,3},{... | collective-permute-start | bytes 983048 | tf_op jit(solution)/shard_map/ppermute | solution.py:870
  25.5 13.1 %collective-permute-start.2 = (f32[16,40,128]{2,1,0:T(8,128)}, f32[16,40,128]{2,1,0:T(8,128)S(1)}, u32[]{:S(2)}, u32[]{:S(2)}) collective-permute-start(f32[16,40,128]{2,1,0:T(8,128)} %get-tuple-element.15), channel_id=1, source_target_pairs={{0,4},{4,8},{8,12},{1,5},{5,9},{9,13},{2,6},{6,10},{10,14},{3,7},{... | collective-permute-start | bytes 983048 | tf_op jit(solution)/shard_map/ppermute | solution.py:870
  28.9 11.2 %collective-permute-start.4 = (f32[576,128]{1,0:T(8,128)}, f32[576,128]{1,0:T(8,128)S(1)}, u32[]{:S(2)}, u32[]{:S(2)}) collective-permute-start(f32[576,128]{1,0:T(8,128)} %copy-done.9), channel_id=1, source_target_pairs={{0,16},{16,0},{1,17},{17,1},{2,18},{18,2},{3,19},{19,3},{4,20},{20... | collective-permute-start | bytes 884744 | tf_op jit(solution)/shard_map/ppermute | solution.py:895
  30.3 1.2 %copy-start.2 = (f32[512,512]{1,0:T(8,128)S(1)}, f32[512,512]{1,0:T(8,128)}, u32[]{:S(2)}) copy-start(f32[512,512]{1,0:T(8,128)} %constant.10.clone.dense_ref) | copy-start | bytes 3145732
  34.8 14.2 %copy-start.6 = (f32[512,128]{1,0:T(8,128)S(1)}, f32[512,128]{1,0:T(8,128)}, u32[]{:S(2)}) copy-start(f32[512,128]{1,0:T(8,128)} %copy-done.5) | copy-start | bytes 786436
  34.8 14.1 %all-to-all-start.1 = ((f32[32,16,128]{2,1,0:T(8,128)}), f32[32,16,128]{2,1,0:T(8,128)S(1)}, u32[]{:S(2)}, u32[]{:S(2)}) async-start(f32[32,16,128]{2,1,0:T(8,128)} %bitcast.2), calls=%async_computation.1 | async-start | bytes 524288 | tf_op jit(solution)/shard_map/all_to_all | solution.py:879
  38.7 5.2 %collective-permute-start.5 = (f32[4,40,128]{2,1,0:T(8,128)S(1)}, f32[4,40,128]{2,1,0:T(8,128)S(1)}, u32[]{:S(2)}, u32[]{:S(2)}) collective-permute-start(f32[4,40,128]{2,1,0:T(8,128)S(1)} %pad_maximum_fusion), channel_id=1, source_target_pairs={{0,16},{16,0},{1,17},{17,1},{2,18},{18,2},{3,19},{19,3},{4,20},{20... | collective-permute-start | bytes 245768 | tf_op jit(solution)/shard_map/ppermute | solution.py:900
  47.9 1.0 %copy-start.3 = (f32[2048,128]{1,0:T(8,128)}, f32[2048,128]{1,0:T(8,128)S(1)}, u32[]{:S(2)}) copy-start(f32[2048,128]{1,0:T(8,128)S(1)} %get-tuple-element.20.psi_ref) | copy-start | bytes 3145732
  48.9 8.0 %copy-start.4 = (f32[2048,128]{1,0:T(8,128)S(1)}, f32[2048,128]{1,0:T(8,128)}, u32[]{:S(2)}) copy-start(f32[2048,128]{1,0:T(8,128)} %copy-done.3) | copy-start | bytes 3145732
  50.6 18.0 %all-to-all-start.2 = ((f32[160,4,128]{2,1,0:T(4,128)}), f32[160,4,128]{2,1,0:T(4,128)S(1)}, u32[]{:S(2)}, u32[]{:S(2)}) async-start(f32[160,4,128]{2,1,0:T(4,128)} %get-tuple-element.21), calls=%async_computation.2 | async-start | bytes 655360 | tf_op jit(solution)/shard_map/all_to_all | solution.py:903

commit v4 on v3

--- a/solution.py
+++ b/solution.py
@@ -19,6 +19,7 @@
 KEEP = 1.0 - OMEGA
 SIDE = OMEGA / 6.0
 RATIO = KEEP / SIDE
+FETCHES = 4
 PITCH = 24
 
 
@@ -106,8 +107,19 @@
     return jnp.where(x < 0, flags[0], jnp.where(x >= size_x, flags[1], 1.0)) * SIDE
 
 
-def share_kernel(rho_ref, out_ref, share_ref, c_ref, r_ref, t_ref, q_ref, a_ref, sem):
+def fetch_planes(source_any, target_ref, sems):
+    planes = target_ref.shape[0] // FETCHES
+    moves = []
+    for part in range(FETCHES):
+        at = pl.ds(part * planes, planes)
+        moves.append(pltpu.make_async_copy(source_any.at[at], target_ref.at[at], sems.at[part]))
+        moves[-1].start()
+    return lambda part: moves[part].wait()
+
+
+def share_kernel(rho_any, out_ref, rho_ref, c_ref, r_ref, t_ref, q_ref, a_ref, sems):
     size_x, size_y, merged = rho_ref.shape
+    arrive = fetch_planes(rho_any, rho_ref, sems)
     tiles = merged // LANES
     half = tiles
     slots = half + 4
@@ -142,7 +154,9 @@
         for j in range(-2, half + 2):
             r_ref[pl.ds(r_row(x, j, size_y), 8), :] = zeros
 
-    loop(size_x, pack, 4)
+    for part in range(FETCHES):
+        arrive(part)
+        loop(size_x // FETCHES, pack, 4, part * (size_x // FETCHES))
 
     masks = [row_mask(-1 + 8 * i, 1, size_y, flags[2], flags[3]) for i in range(3)]
     z_first, z_last = edge_lanes(flags)
@@ -216,10 +230,7 @@
     loop(coarse_x, along_y, 2)
     used = coarse_x * coarse_k * coarse_y
     c_ref[pl.ds(used, c_ref.shape[0] - used), :] = jnp.zeros((c_ref.shape[0] - used, LANES), jnp.float32)
-    keep = pltpu.make_async_copy(c_ref, share_ref, sem)
-    keep.start()
     to_messages(c_ref, out_ref)
-    keep.wait()
 
 
 def to_messages(c_ref, out_ref):
@@ -236,6 +247,10 @@
         low = in_ref[pl.ds(c, PAIRS, stride=2 * chunks), :]
         high = in_ref[pl.ds(chunks + c, PAIRS, stride=2 * chunks), :]
         c_ref[pl.ds(c * LANES, LANES), :] = jnp.concatenate([low, high], axis=0).T
+
+
+def in_hbm(value):
+    return pltpu.with_memory_space_constraint(value, pltpu.HBM)
 
 
 def message_rows(block):
@@ -250,16 +265,17 @@
     vmem = lambda n: pltpu.VMEM((n, LANES), jnp.float32)
     return pl.pallas_call(
         share_kernel,
-        out_shape=(jax.ShapeDtypeStruct((rows, LANES), jnp.float32),) * 2,
-        in_specs=[pl.BlockSpec(memory_space=pltpu.VMEM)],
-        out_specs=(pl.BlockSpec(memory_space=pltpu.VMEM), pl.BlockSpec(memory_space=pltpu.HBM)),
+        out_shape=jax.ShapeDtypeStruct((rows, LANES), jnp.float32),
+        in_specs=[pl.BlockSpec(memory_space=pltpu.HBM)],
+        out_specs=pl.BlockSpec(memory_space=pltpu.VMEM),
         scratch_shapes=[
+            pltpu.VMEM(density.shape, jnp.float32),
             vmem(rows),
             vmem((size_x + 2) * (half + 4) * PITCH + 8),
             vmem((size_x + 2) * (half + 2) * PITCH + 8),
             vmem((size_x // 2 + 2) * (half // 2 + 1) * PITCH + 8),
             vmem((size_x // 2 + 2) * (half // 2 + 1) * PITCH + 8),
-            pltpu.SemaphoreType.DMA,
+            pltpu.SemaphoreType.DMA((FETCHES,)),
         ],
         compiler_params=pltpu.CompilerParams(vmem_limit_bytes=16 << 20),
         cost_estimate=pl.CostEstimate(flops=20_000_000, bytes_accessed=2_000_000, transcendentals=0),
@@ -311,7 +327,7 @@
     return lambda value: pltpu.roll(value, shift % LANES, 1)
 
 
-def solve_kernel(devices, own, block, levels_below, in_ref, dense_ref, out_ref, c_ref, *scratch):
+def solve_kernel(devices, own, block, in_ref, dense_any, out_ref, dense_ref, sem, c_ref, *scratch):
     devs_x, devs_y, devs_z = devices
     step_z = own
     step_y = step_z * devs_z
@@ -394,6 +410,9 @@
     onces = [Field(ref, s) for ref, s in zip(t_refs, sizes)]
     values = [Field(ref, s) for ref, s in zip(v_refs, sizes)]
     others = [Field(ref, s) for ref, s in zip(u_refs, sizes)]
+
+    fetch = pltpu.make_async_copy(dense_any, dense_ref, sem)
+    fetch.start()
 
     size = sizes[0]
     slots, wide = size // 2 + 1, size + 2
@@ -444,6 +463,7 @@
 
     row = jnp.concatenate([small_ref[pl.ds(i, 1), :] for i in range(4)], axis=1)
     row = jnp.broadcast_to(row, (8, 4 * LANES))
+    fetch.wait()
     solved = jnp.dot(row, dense_ref[...], precision=lax.Precision.HIGHEST, preferred_element_type=jnp.float32)
     for i in range(4):
         small_ref[pl.ds(i, 1), :] = solved[0:1, i * LANES : (i + 1) * LANES]
@@ -499,54 +519,60 @@
         for size in sizes:
             fields.append(vmem((size + 2) * (size // 2 + 2) * (16 if size > 6 else 8) + 8))
     return pl.pallas_call(
-        functools.partial(solve_kernel, devices, own, block, levels_below),
+        functools.partial(solve_kernel, devices, own, block),
         out_shape=jax.ShapeDtypeStruct((rows, LANES), jnp.float32),
-        in_specs=[pl.BlockSpec(memory_space=pltpu.VMEM)] * 2,
+        in_specs=[pl.BlockSpec(memory_space=pltpu.VMEM), pl.BlockSpec(memory_space=pltpu.HBM)],
         out_specs=pl.BlockSpec(memory_space=pltpu.VMEM),
-        scratch_shapes=[vmem(rows)] + fields + [vmem(512), vmem(256)],
+        scratch_shapes=[pltpu.VMEM(dense.shape, jnp.float32), pltpu.SemaphoreType.DMA, vmem(rows)]
+        + fields
+        + [vmem(512), vmem(256)],
         compiler_params=pltpu.CompilerParams(vmem_limit_bytes=16 << 20),
         cost_estimate=pl.CostEstimate(flops=20_000_000, bytes_accessed=2_000_000, transcendentals=0),
         name="solve",
-    )(received, dense)
-
-
-def faces_kernel(rho_ref, zlo_ref, zhi_ref, own_ref, first_ref, last_ref, x_ref):
+    )(received, in_hbm(jnp.asarray(dense)))
+
+
+def lane_tiles(ref, at, rows):
+    return [ref[at, rows, pl.ds(LANES * k, LANES)] for k in range(ref.shape[2] // LANES)]
+
+
+def slots_with_halo(natural, before, after, reach):
+    packed = pack_tiles(natural)
+    half = len(packed)
+    slots = {j: packed[j] for j in range(half)}
+    for j in range(-reach, 0):
+        outer = before[(j + 4) // 2] if j % 2 == 0 else swap(before[(j + 4) // 2])
+        slots[j] = half_select(outer, swap(packed[half + j]))
+    for j in range(reach):
+        outer = after[j // 2] if j % 2 else swap(after[j // 2])
+        slots[half + j] = half_select(swap(packed[j]), outer)
+    return slots
+
+
+def faces_kernel(rho_ref, zlo_ref, zhi_ref, first_ref, last_ref, x_ref):
     size_x, size_y, merged = rho_ref.shape
     half = merged // LANES
-    slots_in_all = half + 6
-
-    def own_row(x, j, y):
-        return (x * slots_in_all + (j + 3)) * size_y + y
-
-    def lanes(ref, at, rows):
-        return [ref[at, rows, pl.ds(LANES * k, LANES)] for k in range(ref.shape[2] // LANES)]
 
     def pack(x):
-        for i in range(size_y // 8):
-            rows = pl.ds(8 * i, 8)
-            packed = pack_tiles(lanes(rho_ref, x, rows))
-            slots = {j: packed[j] for j in range(half)}
-            before, after = lanes(zlo_ref, x, rows), lanes(zhi_ref, x, rows)
-            outer = {-1: swap(before[1]), -2: before[1], -3: swap(before[0])}
-            for j in (-3, -2, -1):
-                slots[j] = half_select(outer[j], swap(packed[half + j]))
-            outer = {0: swap(after[0]), 1: after[0], 2: swap(after[1])}
-            for j in range(3):
-                slots[half + j] = half_select(swap(packed[j]), outer[j])
-            for j, value in slots.items():
-                own_ref[pl.ds(own_row(x, j, 8 * i), 8), :] = value
-            for j in range(-2, half + 2):
-                if i == 0:
-                    first_ref[x, pl.ds((j + 2) * 3, 3), :] = slots[j][:3]
-                if i == size_y // 8 - 1:
-                    last_ref[x, pl.ds((j + 2) * 3, 3), :] = slots[j][5:]
-
-    loop(size_x, pack, 2)
+        def rows(ref):
+            first, last = lane_tiles(ref, x, pl.ds(0, 8)), lane_tiles(ref, x, pl.ds(size_y - 8, 8))
+            upper = lax.broadcasted_iota(jnp.int32, (8, LANES), 0) < 4
+            return [jnp.where(upper, f, l) for f, l in zip(first, last)]
+
+        slots = slots_with_halo(rows(rho_ref), rows(zlo_ref), rows(zhi_ref), 2)
+        for j in range(-2, half + 2):
+            first_ref[x, pl.ds((j + 2) * 3, 3), :] = slots[j][:3]
+            last_ref[x, pl.ds((j + 2) * 3, 3), :] = slots[j][5:]
+
+    loop(size_x, pack, 4)
     start = jnp.where(lax.axis_index("gx") == 0, size_x - 3, 0)
     for i in range(3):
-        for j in range(-2, half + 2):
-            for y in range(0, size_y, 8):
-                x_ref[pl.ds((i * (half + 4) + (j + 2)) * size_y + y, 8), :] = own_ref[pl.ds(own_row(start + i, j, y), 8), :]
+        for y in range(0, size_y, 8):
+            rows = pl.ds(y, 8)
+            natural, before, after = (lane_tiles(ref, start + i, rows) for ref in (rho_ref, zlo_ref, zhi_ref))
+            slots = slots_with_halo(natural, before, after, 2)
+            for j in range(-2, half + 2):
+                x_ref[pl.ds((i * (half + 4) + (j + 2)) * size_y + y, 8), :] = slots[j]
 
 
 def faces(density, zlo, zhi):
@@ -556,31 +582,28 @@
     shape = lambda *dims: jax.ShapeDtypeStruct(dims + (LANES,), jnp.float32)
     return pl.pallas_call(
         faces_kernel,
-        out_shape=(
-            shape(size_x * (half + 6) * size_y),
-            shape(size_x, rows),
-            shape(size_x, rows),
-            shape(3 * (half + 4) * size_y),
-        ),
+        out_shape=(shape(size_x, rows), shape(size_x, rows), shape(3 * (half + 4) * size_y)),
         in_specs=[pl.BlockSpec(memory_space=pltpu.VMEM)] * 3,
-        out_specs=(pl.BlockSpec(memory_space=pltpu.VMEM),) * 4,
-        compiler_params=pltpu.CompilerParams(vmem_limit_bytes=12 << 20),
+        out_specs=(pl.BlockSpec(memory_space=pltpu.VMEM),) * 3,
+        compiler_params=pltpu.CompilerParams(vmem_limit_bytes=8 << 20),
         cost_estimate=pl.CostEstimate(flops=8_000_000, bytes_accessed=2_000_000, transcendentals=0),
         name="faces",
     )(density, zlo, zhi)
 
 
 def local_kernel(
-    shape, own_ref, ylo_ref, yhi_ref, x_ref, edge_ref, psi_ref, both_any, r_ref, v_ref, p_ref, both_ref, sem
+    rho_any, sent_any, zlo_ref, zhi_ref, ylo_ref, yhi_ref, x_ref, edge_ref, psi_ref,
+    rho_ref, r_ref, v_ref, p_ref, sems, sem
 ):
-    size_x, size_y, merged = shape
+    arrive = fetch_planes(rho_any, rho_ref, sems)
+    size_x, size_y, merged = rho_ref.shape
     half = merged // LANES
+    cells = size_x * half * size_y
+    forward = pltpu.make_async_copy(sent_any, psi_ref.at[pl.ds(cells + LANES, sent_any.shape[0])], sem)
+    forward.start()
     r_slots, v_slots, p_slots = half + 6, half + 4, half + 2
     flags = device_flags()
 
-    def own_row(x, j, y):
-        return (x * r_slots + (j + 3)) * size_y + y
-
     def r_row(x, j, y):
         return ((x + 3) * r_slots + (j + 3)) * PITCH + (y + 3)
 
@@ -591,14 +614,17 @@
         return ((x + 1) * p_slots + (j + 1)) * PITCH + (y + 1)
 
     def place(x):
-        for j in range(-3, half + 3):
-            for y in range(0, size_y, 8):
-                r_ref[pl.ds(r_row(x, j, y), 8), :] = own_ref[pl.ds(own_row(x, j, y), 8), :]
+        for y in range(0, size_y, 8):
+            natural, before, after = (lane_tiles(ref, x, pl.ds(y, 8)) for ref in (rho_ref, zlo_ref, zhi_ref))
+            for j, value in slots_with_halo(natural, before, after, 3).items():
+                r_ref[pl.ds(r_row(x, j, y), 8), :] = value
+
+    def place_y(x):
         for j in range(-2, half + 2):
             r_ref[pl.ds(r_row(x, j, -3), 3), :] = ylo_ref[x, pl.ds((j + 2) * 3, 3), :]
             r_ref[pl.ds(r_row(x, j, size_y), 3), :] = yhi_ref[x, pl.ds((j + 2) * 3, 3), :]
 
-    loop(size_x, place, 2)
+    loop(size_x, place_y, 2)
 
     def place_outer(i):
         for j in range(-2, half + 2):
@@ -615,6 +641,10 @@
             for x, scale in ((i - 2, flags[0]), (i + size_x, flags[1])):
                 r_ref[pl.ds(r_row(x, j, -2), 2), :] = low * scale
                 r_ref[pl.ds(r_row(x, j, size_y), 2), :] = high * scale
+
+    for part in range(FETCHES):
+        arrive(part)
+        loop(size_x // FETCHES, place, 2, part * (size_x // FETCHES))
 
     z_first, z_last = edge_lanes(flags)
     masks = [row_mask(-2 + 8 * i, 2, size_y, flags[2], flags[3]) for i in range(3)]
@@ -653,59 +683,56 @@
             for j in range(half):
                 rho = r_ref[pl.ds(r_row(x, j, y), 8), :]
                 value = SIDE * rho + (SIDE * SIDE) * weighted(p_ref, p_row, x, j, y, centre)
-                psi_ref[pl.ds((x * half + j) * size_y + y, 8), :] = value
+                at = pl.ds((x * half + j) * size_y + y, 8)
+                psi_ref[at, :] = value
+                v_ref[at, :] = rho
 
     loop(size_x, third_sweep)
-    left = jnp.concatenate([own_ref[pl.ds(own_row(x, 0, 0), half * size_y), :] for x in range(size_x)], axis=0)
-    both_ref[...] = lax.dot_general(
-        left, psi_ref[...], (((0,), (0,)), ((), ())),
+    psi_ref[pl.ds(cells, LANES), :] = lax.dot_general(
+        v_ref[pl.ds(0, cells), :], psi_ref[pl.ds(0, cells), :], (((0,), (0,)), ((), ())),
         precision=lax.Precision.HIGHEST, preferred_element_type=jnp.float32,
     )
-    keep = pltpu.make_async_copy(both_ref, both_any, sem)
-    keep.start()
-    keep.wait()
-
-
-def local_part(shape, own, halos):
-    size_x, size_y, merged = shape
+    forward.wait()
+
+
+def local_part(density, sent, halos):
+    size_x, size_y, merged = density.shape
     half = merged // LANES
     vmem = lambda n: pltpu.VMEM((n, LANES), jnp.float32)
     return pl.pallas_call(
-        functools.partial(local_kernel, shape),
-        out_shape=(
-            jax.ShapeDtypeStruct((size_x * half * size_y, LANES), jnp.float32),
-            jax.ShapeDtypeStruct((LANES, LANES), jnp.float32),
-        ),
-        in_specs=[pl.BlockSpec(memory_space=pltpu.VMEM)] * 5,
-        out_specs=(pl.BlockSpec(memory_space=pltpu.VMEM), pl.BlockSpec(memory_space=pltpu.HBM)),
+        local_kernel,
+        out_shape=jax.ShapeDtypeStruct((size_x * half * size_y + LANES + sent.shape[0], LANES), jnp.float32),
+        in_specs=[pl.BlockSpec(memory_space=pltpu.HBM)] * 2 + [pl.BlockSpec(memory_space=pltpu.VMEM)] * 6,
+        out_specs=pl.BlockSpec(memory_space=pltpu.VMEM),
         scratch_shapes=[
+            pltpu.VMEM(density.shape, jnp.float32),
             vmem((size_x + 6) * (half + 6) * PITCH + 8),
             vmem((size_x + 4) * (half + 4) * PITCH + 8),
             vmem((size_x + 2) * (half + 2) * PITCH + 8),
-            vmem(LANES),
+            pltpu.SemaphoreType.DMA((FETCHES,)),
             pltpu.SemaphoreType.DMA,
         ],
         compiler_params=pltpu.CompilerParams(vmem_limit_bytes=20 << 20),
         cost_estimate=pl.CostEstimate(flops=30_000_000, bytes_accessed=4_000_000, transcendentals=0),
         name="local_part",
-    )(own, *halos)
-
-
-def gram_kernel(copies, in_ref, share_any, both_any, c_ref, block_ref, share_ref, both_ref, sems):
-    moves = [
-        pltpu.make_async_copy(share_any, share_ref, sems.at[0]),
-        pltpu.make_async_copy(both_any, both_ref, sems.at[1]),
-    ]
-    for move in moves:
-        move.start()
-    from_messages(in_ref, c_ref)
-    for move in moves:
-        move.wait()
-    both = both_ref[...] + 8.0 * lax.dot_general(
-        share_ref[...], c_ref[...], (((0,), (0,)), ((), ())),
+    )(in_hbm(density), sent, *halos)
+
+
+def gram_kernel(copies, in_ref, local_ref, block_ref):
+    rows = in_ref.shape[0]
+    count = rows // PAIRS
+    cells = local_ref.shape[0] - rows - LANES
+
+    def by_pair(ref, first):
+        return jnp.concatenate([ref[pl.ds(first + c, PAIRS, stride=count), :] for c in range(count)], axis=1)
+
+    coarse = lax.dot_general(
+        by_pair(local_ref, cells + LANES), by_pair(in_ref, 0), (((1,), (1,)), ((), ())),
         precision=lax.Precision.HIGHEST, preferred_element_type=jnp.float32,
     )
+    both = local_ref[pl.ds(cells, LANES), :]
     whole = both[:PAIRS] + swap(both[PAIRS:])
+    whole = whole + 8.0 * jnp.concatenate([coarse, jnp.zeros_like(coarse)], axis=1)
     quarter = PAIRS // 2
     corner = pltpu.roll(whole[quarter:], LANES - quarter, 1)
     row = lax.broadcasted_iota(jnp.int32, (quarter, LANES), 0)
@@ -721,27 +748,20 @@
         block_ref[i * groups + groups - 1] = last
 
 
-def gram(received, shares, both, copies):
+def gram(received, local, copies):
     groups = PAIRS // 16 + 1
     return pl.pallas_call(
         functools.partial(gram_kernel, copies),
-        out_shape=(
-            jax.ShapeDtypeStruct(received.shape, jnp.float32),
-            jax.ShapeDtypeStruct((copies * groups, 4, LANES), jnp.float32),
-        ),
-        in_specs=[pl.BlockSpec(memory_space=pltpu.VMEM)] + [pl.BlockSpec(memory_space=pltpu.HBM)] * 2,
-        out_specs=(pl.BlockSpec(memory_space=pltpu.VMEM),) * 2,
-        scratch_shapes=[
-            pltpu.VMEM(shares.shape, jnp.float32),
-            pltpu.VMEM(both.shape, jnp.float32),
-            pltpu.SemaphoreType.DMA((2,)),
-        ],
+        out_shape=jax.ShapeDtypeStruct((copies * groups, 4, LANES), jnp.float32),
+        in_specs=[pl.BlockSpec(memory_space=pltpu.VMEM)] * 2,
+        out_specs=pl.BlockSpec(memory_space=pltpu.VMEM),
         compiler_params=pltpu.CompilerParams(vmem_limit_bytes=8 << 20),
         name="gram",
-    )(received, shares, both)
-
-
-def correct_kernel(c_ref, psi_ref, out_ref, e_ref, u_ref):
+    )(received, local)
+
+
+def correct_kernel(in_ref, psi_ref, out_ref, c_ref, e_ref, u_ref):
+    from_messages(in_ref, c_ref)
     size_x, size_y, merged = out_ref.shape
     half = merged // LANES
     flags = device_flags()
@@ -805,8 +825,8 @@
     loop(size_x, second, 2)
 
 
-def correct(rows, psi, shape):
-    size_x, size_y, merged = shape
+def correct(received, psi, shape):
+    size_x, _, merged = shape
     half = merged // LANES
     vmem = lambda n: pltpu.VMEM((n, LANES), jnp.float32)
     return pl.pallas_call(
@@ -815,13 +835,14 @@
         in_specs=[pl.BlockSpec(memory_space=pltpu.VMEM)] * 2,
         out_specs=pl.BlockSpec(memory_space=pltpu.VMEM),
         scratch_shapes=[
+            vmem(received.shape[0]),
             vmem((size_x // 2 + 2) * (half // 2 + 2) * PITCH + 8),
             vmem((size_x + 2) * (half + 2) * PITCH + 8),
         ],
         compiler_params=pltpu.CompilerParams(vmem_limit_bytes=12 << 20),
         cost_estimate=pl.CostEstimate(flops=20_000_000, bytes_accessed=2_000_000, transcendentals=0),
         name="correct",
-    )(rows, psi)
+    )(received, psi)
 
 
 def total_kernel(scale, groups, in_ref, out_ref):
@@ -888,9 +909,9 @@
     deep = 4 * PAIRS
     swapped = [(0, 1), (1, 0)]
     zlo, zhi = shifted(density[..., :deep], density[..., -deep:], "gz")
-    messages, shares = share(density)
+    messages = share(in_hbm(density))
     received = exchanged(messages)
-    own, first, last, plane = faces(density, zlo, zhi)
+    first, last, plane = faces(density, zlo, zhi)
     ylo, yhi = shifted(first, last, "gy")
     beside = lax.ppermute(plane, "gx", swapped)
     answers = solve(received, devices, block, LEVELS - 1)
@@ -898,10 +919,10 @@
     low = lax.axis_index("gx") == 0
     edge = jnp.concatenate([jnp.where(low, a[-2:], a[:2]) for a in (ylo, yhi)], axis=0)
     edge = lax.ppermute(edge, "gx", swapped)
-    psi, both = local_part(density.shape, own, (ylo, yhi, beside, edge))
-    rows, parts = gram(correction, shares, both, count)
+    psi = local_part(density, messages, (zlo, zhi, ylo, yhi, beside, edge))
+    parts = gram(correction, psi, count)
     parts = lax.all_to_all(parts, AXES, 0, 0, tiled=True)
-    potential = correct(rows, psi, density.shape)
+    potential = correct(correction, psi, density.shape)
     cells = size_x * size_y * (merged // PAIRS) * count
     return potential, total(parts, 4.0 / cells)
 
@@ -953,13 +974,13 @@
     factor = 0.25 ** (grid_level - 1)
     current = OMEGA * source / (6.0 * factor)
     if grid_level == LEVELS:
-        for repeat_no in range(COARSE_SWEEPS - 1):
+        for _ in range(COARSE_SWEEPS - 1):
             current = sweep_inner(zero_rim(current), source, factor)
         return current
     current = sweep_inner(zero_rim(current), source, factor)
     residual = source - apply_inner(zero_rim(current), factor)
     current = current + prolong(global_cycle(restrict(residual), grid_level + 1))
-    for repeat_no in range(2):
+    for _ in range(2):
         current = sweep_inner(zero_rim(current), source, factor)
     return current
 
@@ -973,7 +994,7 @@
 
 
 def own_block(gathered, block_shape):
-    size_x, size_y, size_z, count = block_shape
+    size_x, size_y, size_z, _ = block_shape
     starts = (
         lax.axis_index("gx") * size_x,
         lax.axis_index("gy") * size_y,

time: 69.9 us -> 66.8 us (0.956)
  local copies, waits for them, and re-layouts: 6.93 us -> 1.16 us
  Pallas kernels: 17.1 us -> 19.4 us
  waiting for transfers between devices: 12.9 us -> 14.5 us
  starting transfers between devices: 31.5 us -> 30.4 us
    unnamed x20 -> x2, local copies, waits for them, and re-layouts: 5.77 us -> 0.01 us
    pallas_call x5, Pallas kernels: 13.8 us -> 15.9 us  [the longest x1 5.9 us: local_part(): pl.pallas_call(local_kernel, out_shape=jax.ShapeDtypeStruct((size_x * hal...]
    all_to_all x2, waiting for transfers between devices: 0.08 us -> 1.77 us  [exchanged(): lax.all_to_all(shaped, axes, 0, 0, tiled=True).reshape(messages.shape)]
    all_to_all x2, starting transfers between devices: 11.4 us -> 10.3 us  [exchanged(): lax.all_to_all(shaped, axes, 0, 0, tiled=True).reshape(messages.shape)]
  transfers between devices with their start and end apart: 9 -> 9, of which waited for: 3 -> 3; matrix products, arithmetic and copies ran while one was open for 0% -> 0% of each run, Pallas kernels for 21% -> 26%
where the time goes in v4:
time: 66.8 us; the launch traced here: 66.4 us
  starting transfers between devices  30.4 us (46%)
  Pallas kernels  19.4 us (29%)
  waiting for transfers between devices  14.5 us (22%)
  local copies, waits for them, and re-layouts  1.16 us (2%)
  between operations  0.8 us (1%)
    ppermute x4, starting transfers between devices, shifted(): return (lax.ppermute(last, axis, up), lax.ppermute(first, axis, down))  10.9 us
    all_to_all x2, starting transfers between devices, exchanged(): lax.all_to_all(shaped, axes, 0, 0, tiled=True).reshape(messages.shape)  10.3 us
    all_to_all x1, waiting for transfers between devices, fast_local(): parts = lax.all_to_all(parts, AXES, 0, 0, tiled=True)  8.95 us
    all_to_all x1, starting transfers between devices, fast_local(): parts = lax.all_to_all(parts, AXES, 0, 0, tiled=True)  6.44 us
    pallas_call x1, Pallas kernels, local_part(): pl.pallas_call(local_kernel, out_shape=jax.ShapeDtypeStruct((size_x * hal...  5.9 us
    ppermute x1, waiting for transfers between devices, fast_local(): edge = lax.ppermute(edge, 'gx', swapped)  3.79 us
    pallas_call x1, Pallas kernels, share(): pl.pallas_call(share_kernel, out_shape=jax.ShapeDtypeStruct((rows, LANES)...  3.66 us
    pallas_call x1, Pallas kernels, solve(): pl.pallas_call(functools.partial(solve_kernel, devices, own, block), out_...  3.54 us
  transfers between devices with their start and end apart: 9, of which 3 were waited for; matrix products, arithmetic and copies ran while one was open for 0% of the time, Pallas kernels for 26%

profile of v4, /device:TPU:1, one launch (start us, length us, event | category | flops | bytes accessed | tf_op | source)
XLA Modules:
  0.0 66.4 jit_solution(3676735552905083072)
XLA Ops:
  0.6 0.0 copy-start
  0.6 1.2 %fusion = (f32[16,16,256]{2,1,0:T(8,128)S(1)}, f32[16,16,256]{2,1,0:T(8,128)S(1)}) fusion(f32[16,16,1024]{2,1,0:T(8,128)} %rho_any.3), kind=kLoop, calls=%fused_computation.3 | loop fusion | bytes 1048576 | tf_op jit(solution)/shard_map/slice | solution.py:911
  1.8 4.0 %collective-permute-start = (f32[16,16,256]{2,1,0:T(8,128)S(1)}, f32[16,16,256]{2,1,0:T(8,128)S(1)}, u32[]{:S(2)}, u32[]{:S(2)}) collective-permute-start(f32[16,16,256]{2,1,0:T(8,128)S(1)} %get-tuple-element.9), channel_id=1, source_target_pairs={{0,1},{1,2},{2,3},{4,5},{5,6},{6,7},{8,9},{9,10},{10,11},{12,13},{... | collective-permute-start | bytes 786440 | tf_op jit(solution)/shard_map/ppermute | solution.py:891
  5.8 1.3 %collective-permute-start.1 = (f32[16,16,256]{2,1,0:T(8,128)S(1)}, f32[16,16,256]{2,1,0:T(8,128)S(1)}, u32[]{:S(2)}, u32[]{:S(2)}) collective-permute-start(f32[16,16,256]{2,1,0:T(8,128)S(1)} %get-tuple-element.8), channel_id=1, source_target_pairs={{1,0},{2,1},{3,2},{5,4},{6,5},{7,6},{9,8},{10,9},{11,10},{13,12},{... | collective-permute-start | bytes 786440 | tf_op jit(solution)/shard_map/ppermute | solution.py:891
  7.1 3.7 %share.1.sent_any = f32[512,128]{1,0:T(8,128)} custom-call(f32[16,16,1024]{2,1,0:T(8,128)} %rho_any.3), custom_call_target="tpu_custom_call" | custom-call | flops 20000000 | bytes 2000000 | tf_op jit(solution)/shard_map/share/pallas_call | solution.py:266
  10.8 7.6 %all-to-all-start = ((f32[32,16,128]{2,1,0:T(8,128)}), f32[32,16,128]{2,1,0:T(8,128)S(1)}, u32[]{:S(2)}, u32[]{:S(2)}) async-start(f32[32,16,128]{2,1,0:T(8,128)} %bitcast), calls=%async_computation | async-start | bytes 524288 | tf_op jit(solution)/shard_map/all_to_all | solution.py:900
  18.4 0.0 collective-permute-done.zlo_ref
  18.5 1.5 %faces.1 = (f32[16,40,128]{2,1,0:T(8,128)}, f32[16,40,128]{2,1,0:T(8,128)S(1)}, f32[576,128]{1,0:T(8,128)}) custom-call(f32[16,16,1024]{2,1,0:T(8,128)S(1)} %copy-done, f32[16,16,256]{2,1,0:T(8,128)S(1)} %collective-permute-done.zlo_ref, f32[16,16,256]{2,1,0:T(8,128)S(1)} %collective-permute-done.1.zhi_ref), custom_call_target="tpu_custom_call" | custom-call | flops 8000000 | bytes 2000000 | tf_op jit(solution)/shard_map/faces/pallas_call | solution.py:583
  20.0 2.2 %collective-permute-start.3 = (f32[16,40,128]{2,1,0:T(8,128)}, f32[16,40,128]{2,1,0:T(8,128)S(1)}, u32[]{:S(2)}, u32[]{:S(2)}) collective-permute-start(f32[16,40,128]{2,1,0:T(8,128)} %get-tuple-element.6), channel_id=1, source_target_pairs={{4,0},{8,4},{12,8},{5,1},{9,5},{13,9},{6,2},{10,6},{14,10},{7,3},{... | collective-permute-start | bytes 983048 | tf_op jit(solution)/shard_map/ppermute | solution.py:891
  22.2 3.4 %collective-permute-start.2 = (f32[16,40,128]{2,1,0:T(8,128)S(1)}, f32[16,40,128]{2,1,0:T(8,128)S(1)}, u32[]{:S(2)}, u32[]{:S(2)}) collective-permute-start(f32[16,40,128]{2,1,0:T(8,128)S(1)} %get-tuple-element.5), channel_id=1, source_target_pairs={{0,4},{4,8},{8,12},{1,5},{5,9},{9,13},{2,6},{6,10},{10,14},{3,7},{... | collective-permute-start | bytes 983048 | tf_op jit(solution)/shard_map/ppermute | solution.py:891
  25.6 1.4 %collective-permute-start.4 = (f32[576,128]{1,0:T(8,128)}, f32[576,128]{1,0:T(8,128)S(1)}, u32[]{:S(2)}, u32[]{:S(2)}) collective-permute-start(f32[576,128]{1,0:T(8,128)} %get-tuple-element.7), channel_id=1, source_target_pairs={{0,16},{16,0},{1,17},{17,1},{2,18},{18,2},{3,19},{19,3},{4,20},{20... | collective-permute-start | bytes 884744 | tf_op jit(solution)/shard_map/ppermute | solution.py:916
  27.0 1.8 %all-to-all-done = f32[32,16,128]{2,1,0:T(8,128)S(1)} async-done(((f32[32,16,128]{2,1,0:T(8,128)}), f32[32,16,128]{2,1,0:T(8,128)S(1)}, u32[]{:S(2)}, u32[]{:S(2)}) %all-to-all-start) | async-done | bytes 262176 | tf_op jit(solution)/shard_map/all_to_all | solution.py:900
  28.8 3.5 %solve.1 = f32[512,128]{1,0:T(8,128)} custom-call(f32[512,128]{1,0:T(8,128)S(1)} %bitcast.6, f32[512,512]{1,0:T(8,128)} %constant.10.clone.dense_any), custom_call_target="tpu_custom_call" | custom-call | flops 20000000 | bytes 2000000 | tf_op jit(solution)/shard_map/solve/pallas_call | solution.py:521
  32.3 2.7 %all-to-all-start.1 = ((f32[32,16,128]{2,1,0:T(8,128)}), f32[32,16,128]{2,1,0:T(8,128)S(1)}, u32[]{:S(2)}, u32[]{:S(2)}) async-start(f32[32,16,128]{2,1,0:T(8,128)} %bitcast.2), calls=%async_computation.1 | async-start | bytes 524288 | tf_op jit(solution)/shard_map/all_to_all | solution.py:900
  35.0 0.0 collective-permute-done.2.ylo_ref
  35.1 1.4 %collective-permute-start.5 = (f32[4,40,128]{2,1,0:T(8,128)S(1)}, f32[4,40,128]{2,1,0:T(8,128)S(1)}, u32[]{:S(2)}, u32[]{:S(2)}) collective-permute-start(f32[4,40,128]{2,1,0:T(8,128)S(1)} %pad_maximum_fusion), channel_id=1, source_target_pairs={{0,16},{16,0},{1,17},{17,1},{2,18},{18,2},{3,19},{19,3},{4,20},{20... | collective-permute-start | bytes 245768 | tf_op jit(solution)/shard_map/ppermute | solution.py:921
  36.5 3.8 %collective-permute-done.5.edge_ref = f32[4,40,128]{2,1,0:T(8,128)S(1)} collective-permute-done((f32[4,40,128]{2,1,0:T(8,128)S(1)}, f32[4,40,128]{2,1,0:T(8,128)S(1)}, u32[]{:S(2)}, u32[]{:S(2)}) %collective-permute-start.5) | collective-permute-done | bytes 81952 | tf_op jit(solution)/shard_map/ppermute | solution.py:921
  40.3 5.9 %local_part.1.psi_ref.local_ref = f32[2688,128]{1,0:T(8,128)S(1)} custom-call(f32[16,16,1024]{2,1,0:T(8,128)} %rho_any.3, f32[512,128]{1,0:T(8,128)} %share.1.sent_any, f32[16,16,256]{2,1,0:T(8,128)S(1)} %collective-permute-done.zlo_ref, f32[16,16,256]{2,1,0:T(8,128)S(1)} %collective-permute-done.1.zhi_ref, ...), custom_call_target="tpu_custom_call" | custom-call | flops 30000000 | bytes 4000000 | tf_op jit(solution)/shard_map/local_part/pallas_call | solution.py:702
  46.2 0.0 all-to-all-done.1
  46.2 1.3 %gram.1 = f32[160,4,128]{2,1,0:T(4,128)} custom-call(f32[512,128]{1,0:T(8,128)S(1)} %bitcast.4, f32[2688,128]{1,0:T(8,128)S(1)} %local_part.1.psi_ref.local_ref), custom_call_target="tpu_custom_call" | custom-call | tf_op jit(solution)/shard_map/gram/pallas_call | solution.py:753
  47.5 6.4 %all-to-all-start.2 = ((f32[160,4,128]{2,1,0:T(4,128)}), f32[160,4,128]{2,1,0:T(4,128)S(1)}, u32[]{:S(2)}, u32[]{:S(2)}) async-start(f32[160,4,128]{2,1,0:T(4,128)} %gram.1), calls=%async_computation.2 | async-start | bytes 655360 | tf_op jit(solution)/shard_map/all_to_all | solution.py:924
  53.9 2.7 %correct.1 = f32[16,16,1024]{2,1,0:T(8,128)} custom-call(f32[512,128]{1,0:T(8,128)S(1)} %bitcast.5, f32[2688,128]{1,0:T(8,128)S(1)} %local_part.1.psi_ref.local_ref), custom_call_target="tpu_custom_call" | custom-call | flops 20000000 | bytes 2000000 | tf_op jit(solution)/shard_map/correct/pallas_call | solution.py:832
  56.6 9.0 %all-to-all-done.2.in_ref = f32[160,4,128]{2,1,0:T(4,128)S(1)} async-done(((f32[160,4,128]{2,1,0:T(4,128)}), f32[160,4,128]{2,1,0:T(4,128)S(1)}, u32[]{:S(2)}, u32[]{:S(2)}) %all-to-all-start.2) | async-done | bytes 327712 | tf_op jit(solution)/shard_map/all_to_all | solution.py:924
  65.5 0.8 %total.1 = f32[64,64]{1,0:T(8,128)} custom-call(f32[160,4,128]{2,1,0:T(4,128)S(1)} %all-to-all-done.2.in_ref), custom_call_target="tpu_custom_call" | custom-call | tf_op jit(solution)/shard_map/total/pallas_call | solution.py:874
  (7 shorter events, 0.0 us)
Async XLA Ops:
  0.6 17.8 %copy-start = (f32[16,16,1024]{2,1,0:T(8,128)S(1)}, f32[16,16,1024]{2,1,0:T(8,128)}, u32[]{:S(2)}) copy-start(f32[16,16,1024]{2,1,0:T(8,128)} %rho_any.3) | copy-start | bytes 3145732
  1.8 16.6 %collective-permute-start = (f32[16,16,256]{2,1,0:T(8,128)S(1)}, f32[16,16,256]{2,1,0:T(8,128)S(1)}, u32[]{:S(2)}, u32[]{:S(2)}) collective-permute-start(f32[16,16,256]{2,1,0:T(8,128)S(1)} %get-tuple-element.9), channel_id=1, source_target_pairs={{0,1},{1,2},{2,3},{4,5},{5,6},{6,7},{8,9},{9,10},{10,11},{12,13},{... | collective-permute-start | bytes 786440 | tf_op jit(solution)/shard_map/ppermute | solution.py:891
  5.8 12.6 %collective-permute-start.1 = (f32[16,16,256]{2,1,0:T(8,128)S(1)}, f32[16,16,256]{2,1,0:T(8,128)S(1)}, u32[]{:S(2)}, u32[]{:S(2)}) collective-permute-start(f32[16,16,256]{2,1,0:T(8,128)S(1)} %get-tuple-element.8), channel_id=1, source_target_pairs={{1,0},{2,1},{3,2},{5,4},{6,5},{7,6},{9,8},{10,9},{11,10},{13,12},{... | collective-permute-start | bytes 786440 | tf_op jit(solution)/shard_map/ppermute | solution.py:891
  10.8 17.9 %all-to-all-start = ((f32[32,16,128]{2,1,0:T(8,128)}), f32[32,16,128]{2,1,0:T(8,128)S(1)}, u32[]{:S(2)}, u32[]{:S(2)}) async-start(f32[32,16,128]{2,1,0:T(8,128)} %bitcast), calls=%async_computation | async-start | bytes 524288 | tf_op jit(solution)/shard_map/all_to_all | solution.py:900
  20.0 15.0 %collective-permute-start.3 = (f32[16,40,128]{2,1,0:T(8,128)}, f32[16,40,128]{2,1,0:T(8,128)S(1)}, u32[]{:S(2)}, u32[]{:S(2)}) collective-permute-start(f32[16,40,128]{2,1,0:T(8,128)} %get-tuple-element.6), channel_id=1, source_target_pairs={{4,0},{8,4},{12,8},{5,1},{9,5},{13,9},{6,2},{10,6},{14,10},{7,3},{... | collective-permute-start | bytes 983048 | tf_op jit(solution)/shard_map/ppermute | solution.py:891
  22.2 12.8 %collective-permute-start.2 = (f32[16,40,128]{2,1,0:T(8,128)S(1)}, f32[16,40,128]{2,1,0:T(8,128)S(1)}, u32[]{:S(2)}, u32[]{:S(2)}) collective-permute-start(f32[16,40,128]{2,1,0:T(8,128)S(1)} %get-tuple-element.5), channel_id=1, source_target_pairs={{0,4},{4,8},{8,12},{1,5},{5,9},{9,13},{2,6},{6,10},{10,14},{3,7},{... | collective-permute-start | bytes 983048 | tf_op jit(solution)/shard_map/ppermute | solution.py:891
  25.6 10.9 %collective-permute-start.4 = (f32[576,128]{1,0:T(8,128)}, f32[576,128]{1,0:T(8,128)S(1)}, u32[]{:S(2)}, u32[]{:S(2)}) collective-permute-start(f32[576,128]{1,0:T(8,128)} %get-tuple-element.7), channel_id=1, source_target_pairs={{0,16},{16,0},{1,17},{17,1},{2,18},{18,2},{3,19},{19,3},{4,20},{20... | collective-permute-start | bytes 884744 | tf_op jit(solution)/shard_map/ppermute | solution.py:916
  32.3 13.9 %all-to-all-start.1 = ((f32[32,16,128]{2,1,0:T(8,128)}), f32[32,16,128]{2,1,0:T(8,128)S(1)}, u32[]{:S(2)}, u32[]{:S(2)}) async-start(f32[32,16,128]{2,1,0:T(8,128)} %bitcast.2), calls=%async_computation.1 | async-start | bytes 524288 | tf_op jit(solution)/shard_map/all_to_all | solution.py:900
  35.1 5.2 %collective-permute-start.5 = (f32[4,40,128]{2,1,0:T(8,128)S(1)}, f32[4,40,128]{2,1,0:T(8,128)S(1)}, u32[]{:S(2)}, u32[]{:S(2)}) collective-permute-start(f32[4,40,128]{2,1,0:T(8,128)S(1)} %pad_maximum_fusion), channel_id=1, source_target_pairs={{0,16},{16,0},{1,17},{17,1},{2,18},{18,2},{3,19},{19,3},{4,20},{20... | collective-permute-start | bytes 245768 | tf_op jit(solution)/shard_map/ppermute | solution.py:921
  47.5 18.1 %all-to-all-start.2 = ((f32[160,4,128]{2,1,0:T(4,128)}), f32[160,4,128]{2,1,0:T(4,128)S(1)}, u32[]{:S(2)}, u32[]{:S(2)}) async-start(f32[160,4,128]{2,1,0:T(4,128)} %gram.1), calls=%async_computation.2 | async-start | bytes 655360 | tf_op jit(solution)/shard_map/all_to_all | solution.py:924

commit v5 on v4

--- a/solution.py
+++ b/solution.py
@@ -117,9 +117,8 @@
     return lambda part: moves[part].wait()
 
 
-def share_kernel(rho_any, out_ref, rho_ref, c_ref, r_ref, t_ref, q_ref, a_ref, sems):
+def share_kernel(rho_ref, out_ref, c_ref, r_ref, t_ref, q_ref, a_ref):
     size_x, size_y, merged = rho_ref.shape
-    arrive = fetch_planes(rho_any, rho_ref, sems)
     tiles = merged // LANES
     half = tiles
     slots = half + 4
@@ -154,9 +153,7 @@
         for j in range(-2, half + 2):
             r_ref[pl.ds(r_row(x, j, size_y), 8), :] = zeros
 
-    for part in range(FETCHES):
-        arrive(part)
-        loop(size_x // FETCHES, pack, 4, part * (size_x // FETCHES))
+    loop(size_x, pack, 4)
 
     masks = [row_mask(-1 + 8 * i, 1, size_y, flags[2], flags[3]) for i in range(3)]
     z_first, z_last = edge_lanes(flags)
@@ -266,16 +263,14 @@
     return pl.pallas_call(
         share_kernel,
         out_shape=jax.ShapeDtypeStruct((rows, LANES), jnp.float32),
-        in_specs=[pl.BlockSpec(memory_space=pltpu.HBM)],
+        in_specs=[pl.BlockSpec(memory_space=pltpu.VMEM)],
         out_specs=pl.BlockSpec(memory_space=pltpu.VMEM),
         scratch_shapes=[
-            pltpu.VMEM(density.shape, jnp.float32),
             vmem(rows),
             vmem((size_x + 2) * (half + 4) * PITCH + 8),
             vmem((size_x + 2) * (half + 2) * PITCH + 8),
             vmem((size_x // 2 + 2) * (half // 2 + 1) * PITCH + 8),
             vmem((size_x // 2 + 2) * (half // 2 + 1) * PITCH + 8),
-            pltpu.SemaphoreType.DMA((FETCHES,)),
         ],
         compiler_params=pltpu.CompilerParams(vmem_limit_bytes=16 << 20),
         cost_estimate=pl.CostEstimate(flops=20_000_000, bytes_accessed=2_000_000, transcendentals=0),
@@ -909,7 +904,7 @@
     deep = 4 * PAIRS
     swapped = [(0, 1), (1, 0)]
     zlo, zhi = shifted(density[..., :deep], density[..., -deep:], "gz")
-    messages = share(in_hbm(density))
+    messages = share(density)
     received = exchanged(messages)
     first, last, plane = faces(density, zlo, zhi)
     ylo, yhi = shifted(first, last, "gy")

time: 66.8 us -> 65.9 us (0.987)
  Pallas kernels: 19.4 us -> 18.5 us
    pallas_call x1, Pallas kernels: 3.66 us -> 2.69 us  [share(): pl.pallas_call(share_kernel, out_shape=jax.ShapeDtypeStruct((rows, LANES)...]
  transfers between devices with their start and end apart: 9 -> 9, of which waited for: 3 -> 3; matrix products, arithmetic and copies ran while one was open for 0% -> 0% of each run, Pallas kernels for 26% -> 25%
where the time goes in v5:
time: 65.9 us; the launch traced here: 65.4 us
  starting transfers between devices  30.4 us (46%)
  Pallas kernels  18.5 us (28%)
  waiting for transfers between devices  14.5 us (22%)
  local copies, waits for them, and re-layouts  1.16 us (2%)
  between operations  0.79 us (1%)
    ppermute x4, starting transfers between devices, shifted(): return (lax.ppermute(last, axis, up), lax.ppermute(first, axis, down))  10.9 us
    all_to_all x2, starting transfers between devices, exchanged(): lax.all_to_all(shaped, axes, 0, 0, tiled=True).reshape(messages.shape)  10.3 us
    all_to_all x1, waiting for transfers between devices, fast_local(): parts = lax.all_to_all(parts, AXES, 0, 0, tiled=True)  8.95 us
    all_to_all x1, starting transfers between devices, fast_local(): parts = lax.all_to_all(parts, AXES, 0, 0, tiled=True)  6.43 us
    pallas_call x1, Pallas kernels, local_part(): pl.pallas_call(local_kernel, out_shape=jax.ShapeDtypeStruct((size_x * hal...  5.9 us
    ppermute x1, waiting for transfers between devices, fast_local(): edge = lax.ppermute(edge, 'gx', swapped)  3.79 us
    pallas_call x1, Pallas kernels, solve(): pl.pallas_call(functools.partial(solve_kernel, devices, own, block), out_...  3.54 us
    pallas_call x1, Pallas kernels, share(): pl.pallas_call(share_kernel, out_shape=jax.ShapeDtypeStruct((rows, LANES)...  2.69 us
  transfers between devices with their start and end apart: 9, of which 3 were waited for; matrix products, arithmetic and copies ran while one was open for 0% of the time, Pallas kernels for 25%

profile of v5, /device:TPU:1, one launch (start us, length us, event | category | flops | bytes accessed | tf_op | source)
XLA Modules:
  0.0 65.4 jit_solution(16948032777777140224)
XLA Ops:
  0.6 0.0 copy-start
  0.6 1.2 %fusion = (f32[16,16,256]{2,1,0:T(8,128)S(1)}, f32[16,16,256]{2,1,0:T(8,128)S(1)}) fusion(f32[16,16,1024]{2,1,0:T(8,128)} %rho_any.1), kind=kLoop, calls=%fused_computation.3 | loop fusion | bytes 1048576 | tf_op jit(solution)/shard_map/slice | solution.py:906
  1.8 4.0 %collective-permute-start = (f32[16,16,256]{2,1,0:T(8,128)S(1)}, f32[16,16,256]{2,1,0:T(8,128)S(1)}, u32[]{:S(2)}, u32[]{:S(2)}) collective-permute-start(f32[16,16,256]{2,1,0:T(8,128)S(1)} %get-tuple-element.9), channel_id=1, source_target_pairs={{0,1},{1,2},{2,3},{4,5},{5,6},{6,7},{8,9},{9,10},{10,11},{12,13},{... | collective-permute-start | bytes 786440 | tf_op jit(solution)/shard_map/ppermute | solution.py:886
  5.8 1.3 %collective-permute-start.1 = (f32[16,16,256]{2,1,0:T(8,128)S(1)}, f32[16,16,256]{2,1,0:T(8,128)S(1)}, u32[]{:S(2)}, u32[]{:S(2)}) collective-permute-start(f32[16,16,256]{2,1,0:T(8,128)S(1)} %get-tuple-element.8), channel_id=1, source_target_pairs={{1,0},{2,1},{3,2},{5,4},{6,5},{7,6},{9,8},{10,9},{11,10},{13,12},{... | collective-permute-start | bytes 786440 | tf_op jit(solution)/shard_map/ppermute | solution.py:886
  7.2 2.7 %share.1.sent_any = f32[512,128]{1,0:T(8,128)} custom-call(f32[16,16,1024]{2,1,0:T(8,128)S(1)} %copy-done), custom_call_target="tpu_custom_call" | custom-call | flops 20000000 | bytes 2000000 | tf_op jit(solution)/shard_map/share/pallas_call | solution.py:263
  9.8 7.6 %all-to-all-start = ((f32[32,16,128]{2,1,0:T(8,128)}), f32[32,16,128]{2,1,0:T(8,128)S(1)}, u32[]{:S(2)}, u32[]{:S(2)}) async-start(f32[32,16,128]{2,1,0:T(8,128)} %bitcast), calls=%async_computation | async-start | bytes 524288 | tf_op jit(solution)/shard_map/all_to_all | solution.py:895
  17.5 0.0 collective-permute-done.zlo_ref
  17.5 1.5 %faces.1 = (f32[16,40,128]{2,1,0:T(8,128)}, f32[16,40,128]{2,1,0:T(8,128)S(1)}, f32[576,128]{1,0:T(8,128)}) custom-call(f32[16,16,1024]{2,1,0:T(8,128)S(1)} %copy-done, f32[16,16,256]{2,1,0:T(8,128)S(1)} %collective-permute-done.zlo_ref, f32[16,16,256]{2,1,0:T(8,128)S(1)} %collective-permute-done.1.zhi_ref), custom_call_target="tpu_custom_call" | custom-call | flops 8000000 | bytes 2000000 | tf_op jit(solution)/shard_map/faces/pallas_call | solution.py:578
  19.0 2.2 %collective-permute-start.3 = (f32[16,40,128]{2,1,0:T(8,128)}, f32[16,40,128]{2,1,0:T(8,128)S(1)}, u32[]{:S(2)}, u32[]{:S(2)}) collective-permute-start(f32[16,40,128]{2,1,0:T(8,128)} %get-tuple-element.6), channel_id=1, source_target_pairs={{4,0},{8,4},{12,8},{5,1},{9,5},{13,9},{6,2},{10,6},{14,10},{7,3},{... | collective-permute-start | bytes 983048 | tf_op jit(solution)/shard_map/ppermute | solution.py:886
  21.2 3.4 %collective-permute-start.2 = (f32[16,40,128]{2,1,0:T(8,128)S(1)}, f32[16,40,128]{2,1,0:T(8,128)S(1)}, u32[]{:S(2)}, u32[]{:S(2)}) collective-permute-start(f32[16,40,128]{2,1,0:T(8,128)S(1)} %get-tuple-element.5), channel_id=1, source_target_pairs={{0,4},{4,8},{8,12},{1,5},{5,9},{9,13},{2,6},{6,10},{10,14},{3,7},{... | collective-permute-start | bytes 983048 | tf_op jit(solution)/shard_map/ppermute | solution.py:886
  24.6 1.4 %collective-permute-start.4 = (f32[576,128]{1,0:T(8,128)}, f32[576,128]{1,0:T(8,128)S(1)}, u32[]{:S(2)}, u32[]{:S(2)}) collective-permute-start(f32[576,128]{1,0:T(8,128)} %get-tuple-element.7), channel_id=1, source_target_pairs={{0,16},{16,0},{1,17},{17,1},{2,18},{18,2},{3,19},{19,3},{4,20},{20... | collective-permute-start | bytes 884744 | tf_op jit(solution)/shard_map/ppermute | solution.py:911
  26.0 1.8 %all-to-all-done = f32[32,16,128]{2,1,0:T(8,128)S(1)} async-done(((f32[32,16,128]{2,1,0:T(8,128)}), f32[32,16,128]{2,1,0:T(8,128)S(1)}, u32[]{:S(2)}, u32[]{:S(2)}) %all-to-all-start) | async-done | bytes 262176 | tf_op jit(solution)/shard_map/all_to_all | solution.py:895
  27.8 3.5 %solve.1 = f32[512,128]{1,0:T(8,128)} custom-call(f32[512,128]{1,0:T(8,128)S(1)} %bitcast.6, f32[512,512]{1,0:T(8,128)} %constant.10.clone.dense_any), custom_call_target="tpu_custom_call" | custom-call | flops 20000000 | bytes 2000000 | tf_op jit(solution)/shard_map/solve/pallas_call | solution.py:516
  31.3 2.7 %all-to-all-start.1 = ((f32[32,16,128]{2,1,0:T(8,128)}), f32[32,16,128]{2,1,0:T(8,128)S(1)}, u32[]{:S(2)}, u32[]{:S(2)}) async-start(f32[32,16,128]{2,1,0:T(8,128)} %bitcast.2), calls=%async_computation.1 | async-start | bytes 524288 | tf_op jit(solution)/shard_map/all_to_all | solution.py:895
  34.0 0.0 collective-permute-done.3.yhi_ref
  34.1 1.4 %collective-permute-start.5 = (f32[4,40,128]{2,1,0:T(8,128)S(1)}, f32[4,40,128]{2,1,0:T(8,128)S(1)}, u32[]{:S(2)}, u32[]{:S(2)}) collective-permute-start(f32[4,40,128]{2,1,0:T(8,128)S(1)} %pad_maximum_fusion), channel_id=1, source_target_pairs={{0,16},{16,0},{1,17},{17,1},{2,18},{18,2},{3,19},{19,3},{4,20},{20... | collective-permute-start | bytes 245768 | tf_op jit(solution)/shard_map/ppermute | solution.py:916
  35.5 3.8 %collective-permute-done.5.edge_ref = f32[4,40,128]{2,1,0:T(8,128)S(1)} collective-permute-done((f32[4,40,128]{2,1,0:T(8,128)S(1)}, f32[4,40,128]{2,1,0:T(8,128)S(1)}, u32[]{:S(2)}, u32[]{:S(2)}) %collective-permute-start.5) | collective-permute-done | bytes 81952 | tf_op jit(solution)/shard_map/ppermute | solution.py:916
  39.3 5.9 %local_part.1.psi_ref.local_ref = f32[2688,128]{1,0:T(8,128)S(1)} custom-call(f32[16,16,1024]{2,1,0:T(8,128)} %rho_any.1, f32[512,128]{1,0:T(8,128)} %share.1.sent_any, f32[16,16,256]{2,1,0:T(8,128)S(1)} %collective-permute-done.zlo_ref, f32[16,16,256]{2,1,0:T(8,128)S(1)} %collective-permute-done.1.zhi_ref, ...), custom_call_target="tpu_custom_call" | custom-call | flops 30000000 | bytes 4000000 | tf_op jit(solution)/shard_map/local_part/pallas_call | solution.py:697
  45.2 0.0 all-to-all-done.1
  45.2 1.3 %gram.1 = f32[160,4,128]{2,1,0:T(4,128)} custom-call(f32[512,128]{1,0:T(8,128)S(1)} %bitcast.4, f32[2688,128]{1,0:T(8,128)S(1)} %local_part.1.psi_ref.local_ref), custom_call_target="tpu_custom_call" | custom-call | tf_op jit(solution)/shard_map/gram/pallas_call | solution.py:748
  46.5 6.4 %all-to-all-start.2 = ((f32[160,4,128]{2,1,0:T(4,128)}), f32[160,4,128]{2,1,0:T(4,128)S(1)}, u32[]{:S(2)}, u32[]{:S(2)}) async-start(f32[160,4,128]{2,1,0:T(4,128)} %gram.1), calls=%async_computation.2 | async-start | bytes 655360 | tf_op jit(solution)/shard_map/all_to_all | solution.py:919
  52.9 2.7 %correct.1 = f32[16,16,1024]{2,1,0:T(8,128)} custom-call(f32[512,128]{1,0:T(8,128)S(1)} %bitcast.5, f32[2688,128]{1,0:T(8,128)S(1)} %local_part.1.psi_ref.local_ref), custom_call_target="tpu_custom_call" | custom-call | flops 20000000 | bytes 2000000 | tf_op jit(solution)/shard_map/correct/pallas_call | solution.py:827
  55.6 9.0 %all-to-all-done.2.in_ref = f32[160,4,128]{2,1,0:T(4,128)S(1)} async-done(((f32[160,4,128]{2,1,0:T(4,128)}), f32[160,4,128]{2,1,0:T(4,128)S(1)}, u32[]{:S(2)}, u32[]{:S(2)}) %all-to-all-start.2) | async-done | bytes 327712 | tf_op jit(solution)/shard_map/all_to_all | solution.py:919
  64.6 0.8 %total.1 = f32[64,64]{1,0:T(8,128)} custom-call(f32[160,4,128]{2,1,0:T(4,128)S(1)} %all-to-all-done.2.in_ref), custom_call_target="tpu_custom_call" | custom-call | tf_op jit(solution)/shard_map/total/pallas_call | solution.py:869
  (7 shorter events, 0.0 us)
Async XLA Ops:
  0.6 6.5 %copy-start = (f32[16,16,1024]{2,1,0:T(8,128)S(1)}, f32[16,16,1024]{2,1,0:T(8,128)}, u32[]{:S(2)}) copy-start(f32[16,16,1024]{2,1,0:T(8,128)} %rho_any.1) | copy-start | bytes 3145732
  1.8 15.7 %collective-permute-start = (f32[16,16,256]{2,1,0:T(8,128)S(1)}, f32[16,16,256]{2,1,0:T(8,128)S(1)}, u32[]{:S(2)}, u32[]{:S(2)}) collective-permute-start(f32[16,16,256]{2,1,0:T(8,128)S(1)} %get-tuple-element.9), channel_id=1, source_target_pairs={{0,1},{1,2},{2,3},{4,5},{5,6},{6,7},{8,9},{9,10},{10,11},{12,13},{... | collective-permute-start | bytes 786440 | tf_op jit(solution)/shard_map/ppermute | solution.py:886
  5.8 11.6 %collective-permute-start.1 = (f32[16,16,256]{2,1,0:T(8,128)S(1)}, f32[16,16,256]{2,1,0:T(8,128)S(1)}, u32[]{:S(2)}, u32[]{:S(2)}) collective-permute-start(f32[16,16,256]{2,1,0:T(8,128)S(1)} %get-tuple-element.8), channel_id=1, source_target_pairs={{1,0},{2,1},{3,2},{5,4},{6,5},{7,6},{9,8},{10,9},{11,10},{13,12},{... | collective-permute-start | bytes 786440 | tf_op jit(solution)/shard_map/ppermute | solution.py:886
  9.8 17.9 %all-to-all-start = ((f32[32,16,128]{2,1,0:T(8,128)}), f32[32,16,128]{2,1,0:T(8,128)S(1)}, u32[]{:S(2)}, u32[]{:S(2)}) async-start(f32[32,16,128]{2,1,0:T(8,128)} %bitcast), calls=%async_computation | async-start | bytes 524288 | tf_op jit(solution)/shard_map/all_to_all | solution.py:895
  19.0 15.0 %collective-permute-start.3 = (f32[16,40,128]{2,1,0:T(8,128)}, f32[16,40,128]{2,1,0:T(8,128)S(1)}, u32[]{:S(2)}, u32[]{:S(2)}) collective-permute-start(f32[16,40,128]{2,1,0:T(8,128)} %get-tuple-element.6), channel_id=1, source_target_pairs={{4,0},{8,4},{12,8},{5,1},{9,5},{13,9},{6,2},{10,6},{14,10},{7,3},{... | collective-permute-start | bytes 983048 | tf_op jit(solution)/shard_map/ppermute | solution.py:886
  21.2 12.9 %collective-permute-start.2 = (f32[16,40,128]{2,1,0:T(8,128)S(1)}, f32[16,40,128]{2,1,0:T(8,128)S(1)}, u32[]{:S(2)}, u32[]{:S(2)}) collective-permute-start(f32[16,40,128]{2,1,0:T(8,128)S(1)} %get-tuple-element.5), channel_id=1, source_target_pairs={{0,4},{4,8},{8,12},{1,5},{5,9},{9,13},{2,6},{6,10},{10,14},{3,7},{... | collective-permute-start | bytes 983048 | tf_op jit(solution)/shard_map/ppermute | solution.py:886
  24.6 10.9 %collective-permute-start.4 = (f32[576,128]{1,0:T(8,128)}, f32[576,128]{1,0:T(8,128)S(1)}, u32[]{:S(2)}, u32[]{:S(2)}) collective-permute-start(f32[576,128]{1,0:T(8,128)} %get-tuple-element.7), channel_id=1, source_target_pairs={{0,16},{16,0},{1,17},{17,1},{2,18},{18,2},{3,19},{19,3},{4,20},{20... | collective-permute-start | bytes 884744 | tf_op jit(solution)/shard_map/ppermute | solution.py:911
  31.3 13.9 %all-to-all-start.1 = ((f32[32,16,128]{2,1,0:T(8,128)}), f32[32,16,128]{2,1,0:T(8,128)S(1)}, u32[]{:S(2)}, u32[]{:S(2)}) async-start(f32[32,16,128]{2,1,0:T(8,128)} %bitcast.2), calls=%async_computation.1 | async-start | bytes 524288 | tf_op jit(solution)/shard_map/all_to_all | solution.py:895
  34.1 5.2 %collective-permute-start.5 = (f32[4,40,128]{2,1,0:T(8,128)S(1)}, f32[4,40,128]{2,1,0:T(8,128)S(1)}, u32[]{:S(2)}, u32[]{:S(2)}) collective-permute-start(f32[4,40,128]{2,1,0:T(8,128)S(1)} %pad_maximum_fusion), channel_id=1, source_target_pairs={{0,16},{16,0},{1,17},{17,1},{2,18},{18,2},{3,19},{19,3},{4,20},{20... | collective-permute-start | bytes 245768 | tf_op jit(solution)/shard_map/ppermute | solution.py:916
  46.5 18.1 %all-to-all-start.2 = ((f32[160,4,128]{2,1,0:T(4,128)}), f32[160,4,128]{2,1,0:T(4,128)S(1)}, u32[]{:S(2)}, u32[]{:S(2)}) async-start(f32[160,4,128]{2,1,0:T(4,128)} %gram.1), calls=%async_computation.2 | async-start | bytes 655360 | tf_op jit(solution)/shard_map/all_to_all | solution.py:919

commit v6 on v5

--- a/solution.py
+++ b/solution.py
@@ -230,20 +230,29 @@
     to_messages(c_ref, out_ref)
 
 
-def to_messages(c_ref, out_ref):
+def message_lines(chunk, chunks, group):
+    step = 2 * chunks
+    return [pl.ds(chunk + i * step, PAIRS // group, stride=group * step) for i in range(group)]
+
+
+def to_messages(c_ref, out_ref, group=1):
+    chunks = c_ref.shape[0] // LANES
+    size = PAIRS // group
+    for c in range(chunks):
+        turned = c_ref[pl.ds(c * LANES, LANES), :].T
+        for part in range(2):
+            for i, line in enumerate(message_lines(part * chunks + c, chunks, group)):
+                at = part * PAIRS + i * size
+                out_ref[line, :] = turned[at : at + size]
+
+
+def from_messages(in_ref, c_ref, group=1):
     chunks = c_ref.shape[0] // LANES
     for c in range(chunks):
-        turned = c_ref[pl.ds(c * LANES, LANES), :].T
-        out_ref[pl.ds(c, PAIRS, stride=2 * chunks), :] = turned[:PAIRS]
-        out_ref[pl.ds(chunks + c, PAIRS, stride=2 * chunks), :] = turned[PAIRS:]
-
-
-def from_messages(in_ref, c_ref):
-    chunks = c_ref.shape[0] // LANES
-    for c in range(chunks):
-        low = in_ref[pl.ds(c, PAIRS, stride=2 * chunks), :]
-        high = in_ref[pl.ds(chunks + c, PAIRS, stride=2 * chunks), :]
-        c_ref[pl.ds(c * LANES, LANES), :] = jnp.concatenate([low, high], axis=0).T
+        parts = []
+        for part in range(2):
+            parts += [in_ref[line, :] for line in message_lines(part * chunks + c, chunks, group)]
+        c_ref[pl.ds(c * LANES, LANES), :] = jnp.concatenate(parts, axis=0).T
 
 
 def in_hbm(value):
@@ -305,17 +314,15 @@
     return current
 
 
-def dense_operator(devices, own, levels):
+def dense_operator(devices, levels):
     devs_x, devs_y, devs_z = devices
     size = (2 * devs_x, 2 * devs_y, 2 * devs_z)
     cells = size[0] * size[1] * size[2]
     basis = np.eye(cells).reshape(size + (cells,))
     matrix = 4.0 * unit_cycle(basis, levels).reshape(cells, cells)
     grid = np.arange(cells).reshape(devs_x, 2, devs_y, 2, devs_z, 2)
-    order = grid.transpose(1, 3, 5, 0, 2, 4).reshape(-1)
-    matrix = matrix[order][:, order].T
-    wide = np.kron(matrix, np.eye(own))
-    return wide.astype(np.float32)
+    order = grid.transpose(1, 5, 3, 0, 2, 4).reshape(-1)
+    return matrix[order][:, order].T.astype(np.float32)
 
 
 def make_lane_roll(shift):
@@ -324,14 +331,16 @@
 
 def solve_kernel(devices, own, block, in_ref, dense_any, out_ref, dense_ref, sem, c_ref, *scratch):
     devs_x, devs_y, devs_z = devices
-    step_z = own
+    step_z = 1
     step_y = step_z * devs_z
     step_x = step_y * devs_y
+    everyone = step_x * devs_x
     lane = lax.broadcasted_iota(jnp.int32, (1, LANES), 1)
-    device = lane % PAIRS
-    at_z = (device // step_z) % devs_z
+    device = lane % everyone
+    at_z = device % devs_z
     at_y = (device // step_y) % devs_y
     at_x = device // step_x
+    first_pair = (lane // everyone) % own == 0
     low = lane < PAIRS
     as_f = lambda cond: jnp.where(cond, 1.0, 0.0)
     has_before_x, has_after_x = as_f(at_x > 0), as_f(at_x < devs_x - 1)
@@ -412,7 +421,7 @@
     size = sizes[0]
     slots, wide = size // 2 + 1, size + 2
     plane = slots * wide
-    from_messages(in_ref, c_ref)
+    from_messages(in_ref, c_ref, own)
     rows = lambda x: pl.ds((x + 1) * plane, plane)
     c_ref[rows(size - 1), :] += from_after_x(c_ref[rows(-1), :]) * has_after_x
     c_ref[rows(0), :] += from_before_x(c_ref[rows(size), :]) * has_before_x
@@ -456,12 +465,22 @@
         else:
             small_ref[pl.ds(0, count), :] = coarse
 
-    row = jnp.concatenate([small_ref[pl.ds(i, 1), :] for i in range(4)], axis=1)
-    row = jnp.broadcast_to(row, (8, 4 * LANES))
+    def pairs_apart(even, odd):
+        return (
+            jnp.where(first_pair, even, pltpu.roll(odd, everyone, 1)),
+            jnp.where(first_pair, pltpu.roll(even, LANES - everyone, 1), odd),
+        )
+
+    apart = [pairs_apart(small_ref[pl.ds(2 * i, 1), :], small_ref[pl.ds(2 * i + 1, 1), :]) for i in range(2)]
+    row = jnp.concatenate([jnp.concatenate([each[i] for each in apart], axis=1) for i in range(2)], axis=0)
+    row = jnp.concatenate([row] * 4, axis=0)
     fetch.wait()
     solved = jnp.dot(row, dense_ref[...], precision=lax.Precision.HIGHEST, preferred_element_type=jnp.float32)
-    for i in range(4):
-        small_ref[pl.ds(i, 1), :] = solved[0:1, i * LANES : (i + 1) * LANES]
+    for i in range(2):
+        group = solved[:, i * LANES : (i + 1) * LANES]
+        together = pairs_apart(group[0:1], group[1:2])
+        small_ref[pl.ds(2 * i, 1), :] = together[0]
+        small_ref[pl.ds(2 * i + 1, 1), :] = together[1]
     correction = small_ref[pl.ds(0, 4), :]
 
     for number in reversed(range(len(sizes))):
@@ -496,7 +515,7 @@
         part = [result.get(x, k, -1, wide) for k in range(-1, source.half + 1)]
         for k in range(slots):
             c_ref[pl.ds((x + 1) * plane + k * wide, wide), :] = choose(part[k], part[k + 1])
-    to_messages(c_ref, out_ref)
+    to_messages(c_ref, out_ref, own)
 
 
 def solve(received, devices, block, levels_below):
@@ -507,7 +526,7 @@
     while size > 2:
         sizes.append(size)
         size //= 2
-    dense = dense_operator(devices, own, levels_below - len(sizes))
+    dense = dense_operator(devices, levels_below - len(sizes))
     vmem = lambda n: pltpu.VMEM((n, LANES), jnp.float32)
     fields = []
     for _ in range(4):
@@ -735,19 +754,17 @@
     packed = jnp.where(row > lane, corner, whole[:quarter])
     diagonal = jnp.sum(jnp.where(row == lane, corner, 0.0), axis=0, keepdims=True)
     flat = half_select(packed[: quarter // 2], swap(packed[quarter // 2 :]))
-    last = jnp.concatenate([diagonal, jnp.zeros((3, LANES), jnp.float32)], axis=0)
-    groups = block_ref.shape[0] // copies
+    lines = [flat[r : r + 1] for r in range(quarter // 2)] + [diagonal]
     for i in range(copies):
-        for g in range(groups - 1):
-            block_ref[i * groups + g] = flat[4 * g : 4 * g + 4]
-        block_ref[i * groups + groups - 1] = last
+        for r, value in enumerate(lines):
+            block_ref[i, :, pl.ds(r * LANES, LANES)] = value
 
 
 def gram(received, local, copies):
-    groups = PAIRS // 16 + 1
+    rows = PAIRS // 4 + 1
     return pl.pallas_call(
         functools.partial(gram_kernel, copies),
-        out_shape=jax.ShapeDtypeStruct((copies * groups, 4, LANES), jnp.float32),
+        out_shape=jax.ShapeDtypeStruct((copies, 1, rows * LANES), jnp.float32),
         in_specs=[pl.BlockSpec(memory_space=pltpu.VMEM)] * 2,
         out_specs=pl.BlockSpec(memory_space=pltpu.VMEM),
         compiler_params=pltpu.CompilerParams(vmem_limit_bytes=8 << 20),
@@ -840,16 +857,15 @@
     )(received, psi)
 
 
-def total_kernel(scale, groups, in_ref, out_ref):
-    copies = in_ref.shape[0] // groups
-    sums = []
-    for g in range(groups):
-        terms = [in_ref[i * groups + g] for i in range(copies)]
-        while len(terms) > 1:
-            terms = [terms[i] + terms[i + 1] for i in range(0, len(terms) - 1, 2)] + terms[len(terms) & ~1 :]
-        sums.append(terms[0] * scale)
-    flat = jnp.concatenate(sums[:-1], axis=0)
-    diagonal = sums[-1][:1]
+def total_kernel(scale, in_ref, out_ref):
+    copies, _, width = in_ref.shape
+    terms = [in_ref[i] for i in range(copies)]
+    while len(terms) > 1:
+        terms = [terms[i] + terms[i + 1] for i in range(0, len(terms) - 1, 2)] + terms[len(terms) & ~1 :]
+    line = terms[0] * scale
+    lines = [line[:, r * LANES : (r + 1) * LANES] for r in range(width // LANES)]
+    flat = jnp.concatenate(lines[:-1], axis=0)
+    diagonal = lines[-1]
     quarter = PAIRS // 2
     packed = jnp.concatenate([flat, swap(flat)], axis=0)
     tall = jnp.concatenate([packed, jnp.zeros((LANES - quarter, LANES), jnp.float32)], axis=0)
@@ -865,9 +881,8 @@
 
 
 def total(parts, scale):
-    groups = PAIRS // 16 + 1
     return pl.pallas_call(
-        functools.partial(total_kernel, scale, groups),
+        functools.partial(total_kernel, scale),
         out_shape=jax.ShapeDtypeStruct((PAIRS, PAIRS), jnp.float32),
         in_specs=[pl.BlockSpec(memory_space=pltpu.VMEM)],
         out_specs=pl.BlockSpec(memory_space=pltpu.VMEM),
@@ -1067,7 +1082,7 @@
     return (
         2 * PAIRS == LANES
         and devices_x == 2
-        and PAIRS % count == 0
+        and PAIRS == 2 * count
         and equal
         and size_x % 8 == 0
         and size_x & (size_x - 1) == 0

time: 65.9 us -> 64.6 us (0.980)
  waiting for transfers between devices: 14.5 us -> 13.6 us
    all_to_all x1, waiting for transfers between devices: 8.95 us -> 7.98 us  [fast_local(): parts = lax.all_to_all(parts, AXES, 0, 0, tiled=True)]
where the time goes in v6:
time: 64.6 us; the launch traced here: 64.1 us
  starting transfers between devices  30.4 us (47%)
  Pallas kernels  18.1 us (28%)
  waiting for transfers between devices  13.6 us (21%)
  local copies, waits for them, and re-layouts  1.16 us (2%)
  between operations  0.79 us (1%)
    ppermute x4, starting transfers between devices, shifted(): return (lax.ppermute(last, axis, up), lax.ppermute(first, axis, down))  10.9 us
    all_to_all x2, starting transfers between devices, exchanged(): lax.all_to_all(shaped, axes, 0, 0, tiled=True).reshape(messages.shape)  10.3 us
    all_to_all x1, waiting for transfers between devices, fast_local(): parts = lax.all_to_all(parts, AXES, 0, 0, tiled=True)  7.98 us
    all_to_all x1, starting transfers between devices, fast_local(): parts = lax.all_to_all(parts, AXES, 0, 0, tiled=True)  6.42 us
    pallas_call x1, Pallas kernels, local_part(): pl.pallas_call(local_kernel, out_shape=jax.ShapeDtypeStruct((size_x * hal...  5.91 us
    ppermute x1, waiting for transfers between devices, fast_local(): edge = lax.ppermute(edge, 'gx', swapped)  3.79 us
    pallas_call x1, Pallas kernels, solve(): pl.pallas_call(functools.partial(solve_kernel, devices, own, block), out_...  3.1 us
    pallas_call x1, Pallas kernels, share(): pl.pallas_call(share_kernel, out_shape=jax.ShapeDtypeStruct((rows, LANES)...  2.69 us
  transfers between devices with their start and end apart: 9, of which 3 were waited for; matrix products, arithmetic and copies ran while one was open for 0% of the time, Pallas kernels for 25%

profile of v6, /device:TPU:1, one launch (start us, length us, event | category | flops | bytes accessed | tf_op | source)
XLA Modules:
  0.0 64.1 jit_solution(16840790504334008422)
XLA Ops:
  0.6 0.0 copy-start
  0.6 1.2 %fusion = (f32[16,16,256]{2,1,0:T(8,128)S(1)}, f32[16,16,256]{2,1,0:T(8,128)S(1)}) fusion(f32[16,16,1024]{2,1,0:T(8,128)} %rho_any.1), kind=kLoop, calls=%fused_computation.3 | loop fusion | bytes 1048576 | tf_op jit(solution)/shard_map/slice | solution.py:921
  1.8 4.0 %collective-permute-start = (f32[16,16,256]{2,1,0:T(8,128)S(1)}, f32[16,16,256]{2,1,0:T(8,128)S(1)}, u32[]{:S(2)}, u32[]{:S(2)}) collective-permute-start(f32[16,16,256]{2,1,0:T(8,128)S(1)} %get-tuple-element.9), channel_id=1, source_target_pairs={{0,1},{1,2},{2,3},{4,5},{5,6},{6,7},{8,9},{9,10},{10,11},{12,13},{... | collective-permute-start | bytes 786440 | tf_op jit(solution)/shard_map/ppermute | solution.py:901
  5.8 1.3 %collective-permute-start.1 = (f32[16,16,256]{2,1,0:T(8,128)S(1)}, f32[16,16,256]{2,1,0:T(8,128)S(1)}, u32[]{:S(2)}, u32[]{:S(2)}) collective-permute-start(f32[16,16,256]{2,1,0:T(8,128)S(1)} %get-tuple-element.8), channel_id=1, source_target_pairs={{1,0},{2,1},{3,2},{5,4},{6,5},{7,6},{9,8},{10,9},{11,10},{13,12},{... | collective-permute-start | bytes 786440 | tf_op jit(solution)/shard_map/ppermute | solution.py:901
  7.2 2.7 %share.1.sent_any = f32[512,128]{1,0:T(8,128)} custom-call(f32[16,16,1024]{2,1,0:T(8,128)S(1)} %copy-done), custom_call_target="tpu_custom_call" | custom-call | flops 20000000 | bytes 2000000 | tf_op jit(solution)/shard_map/share/pallas_call | solution.py:272
  9.8 7.6 %all-to-all-start = ((f32[32,16,128]{2,1,0:T(8,128)}), f32[32,16,128]{2,1,0:T(8,128)S(1)}, u32[]{:S(2)}, u32[]{:S(2)}) async-start(f32[32,16,128]{2,1,0:T(8,128)} %bitcast), calls=%async_computation | async-start | bytes 524288 | tf_op jit(solution)/shard_map/all_to_all | solution.py:910
  17.5 0.0 collective-permute-done.zlo_ref
  17.5 1.5 %faces.1 = (f32[16,40,128]{2,1,0:T(8,128)}, f32[16,40,128]{2,1,0:T(8,128)S(1)}, f32[576,128]{1,0:T(8,128)}) custom-call(f32[16,16,1024]{2,1,0:T(8,128)S(1)} %copy-done, f32[16,16,256]{2,1,0:T(8,128)S(1)} %collective-permute-done.zlo_ref, f32[16,16,256]{2,1,0:T(8,128)S(1)} %collective-permute-done.1.zhi_ref), custom_call_target="tpu_custom_call" | custom-call | flops 8000000 | bytes 2000000 | tf_op jit(solution)/shard_map/faces/pallas_call | solution.py:597
  19.0 2.2 %collective-permute-start.3 = (f32[16,40,128]{2,1,0:T(8,128)}, f32[16,40,128]{2,1,0:T(8,128)S(1)}, u32[]{:S(2)}, u32[]{:S(2)}) collective-permute-start(f32[16,40,128]{2,1,0:T(8,128)} %get-tuple-element.6), channel_id=1, source_target_pairs={{4,0},{8,4},{12,8},{5,1},{9,5},{13,9},{6,2},{10,6},{14,10},{7,3},{... | collective-permute-start | bytes 983048 | tf_op jit(solution)/shard_map/ppermute | solution.py:901
  21.2 3.4 %collective-permute-start.2 = (f32[16,40,128]{2,1,0:T(8,128)S(1)}, f32[16,40,128]{2,1,0:T(8,128)S(1)}, u32[]{:S(2)}, u32[]{:S(2)}) collective-permute-start(f32[16,40,128]{2,1,0:T(8,128)S(1)} %get-tuple-element.5), channel_id=1, source_target_pairs={{0,4},{4,8},{8,12},{1,5},{5,9},{9,13},{2,6},{6,10},{10,14},{3,7},{... | collective-permute-start | bytes 983048 | tf_op jit(solution)/shard_map/ppermute | solution.py:901
  24.6 1.4 %collective-permute-start.4 = (f32[576,128]{1,0:T(8,128)}, f32[576,128]{1,0:T(8,128)S(1)}, u32[]{:S(2)}, u32[]{:S(2)}) collective-permute-start(f32[576,128]{1,0:T(8,128)} %get-tuple-element.7), channel_id=1, source_target_pairs={{0,16},{16,0},{1,17},{17,1},{2,18},{18,2},{3,19},{19,3},{4,20},{20... | collective-permute-start | bytes 884744 | tf_op jit(solution)/shard_map/ppermute | solution.py:926
  26.0 1.8 %all-to-all-done = f32[32,16,128]{2,1,0:T(8,128)S(1)} async-done(((f32[32,16,128]{2,1,0:T(8,128)}), f32[32,16,128]{2,1,0:T(8,128)S(1)}, u32[]{:S(2)}, u32[]{:S(2)}) %all-to-all-start) | async-done | bytes 262176 | tf_op jit(solution)/shard_map/all_to_all | solution.py:910
  27.8 3.1 %solve.1 = f32[512,128]{1,0:T(8,128)} custom-call(f32[512,128]{1,0:T(8,128)S(1)} %bitcast.6, f32[256,256]{1,0:T(8,128)} %constant.10.clone.dense_any), custom_call_target="tpu_custom_call" | custom-call | flops 20000000 | bytes 2000000 | tf_op jit(solution)/shard_map/solve/pallas_call | solution.py:535
  30.9 2.7 %all-to-all-start.1 = ((f32[32,16,128]{2,1,0:T(8,128)}), f32[32,16,128]{2,1,0:T(8,128)S(1)}, u32[]{:S(2)}, u32[]{:S(2)}) async-start(f32[32,16,128]{2,1,0:T(8,128)} %bitcast.2), calls=%async_computation.1 | async-start | bytes 524288 | tf_op jit(solution)/shard_map/all_to_all | solution.py:910
  33.6 0.0 collective-permute-done.3.yhi_ref
  33.6 1.4 %collective-permute-start.5 = (f32[4,40,128]{2,1,0:T(8,128)S(1)}, f32[4,40,128]{2,1,0:T(8,128)S(1)}, u32[]{:S(2)}, u32[]{:S(2)}) collective-permute-start(f32[4,40,128]{2,1,0:T(8,128)S(1)} %pad_maximum_fusion), channel_id=1, source_target_pairs={{0,16},{16,0},{1,17},{17,1},{2,18},{18,2},{3,19},{19,3},{4,20},{20... | collective-permute-start | bytes 245768 | tf_op jit(solution)/shard_map/ppermute | solution.py:931
  35.1 0.0 collective-permute-done.4.x_ref
  35.1 3.8 %collective-permute-done.5.edge_ref = f32[4,40,128]{2,1,0:T(8,128)S(1)} collective-permute-done((f32[4,40,128]{2,1,0:T(8,128)S(1)}, f32[4,40,128]{2,1,0:T(8,128)S(1)}, u32[]{:S(2)}, u32[]{:S(2)}) %collective-permute-start.5) | collective-permute-done | bytes 81952 | tf_op jit(solution)/shard_map/ppermute | solution.py:931
  38.9 5.9 %local_part.1.psi_ref.local_ref = f32[2688,128]{1,0:T(8,128)S(1)} custom-call(f32[16,16,1024]{2,1,0:T(8,128)} %rho_any.1, f32[512,128]{1,0:T(8,128)} %share.1.sent_any, f32[16,16,256]{2,1,0:T(8,128)S(1)} %collective-permute-done.zlo_ref, f32[16,16,256]{2,1,0:T(8,128)S(1)} %collective-permute-done.1.zhi_ref, ...), custom_call_target="tpu_custom_call" | custom-call | flops 30000000 | bytes 4000000 | tf_op jit(solution)/shard_map/local_part/pallas_call | solution.py:716
  44.8 1.4 %gram.1 = f32[32,1,2176]{2,1,0:T(1,128)} custom-call(f32[512,128]{1,0:T(8,128)S(1)} %bitcast.4, f32[2688,128]{1,0:T(8,128)S(1)} %local_part.1.psi_ref.local_ref), custom_call_target="tpu_custom_call" | custom-call | tf_op jit(solution)/shard_map/gram/pallas_call | solution.py:765
  46.2 6.4 %all-to-all-start.2 = ((f32[32,1,2176]{2,1,0:T(1,128)}), f32[32,1,2176]{2,1,0:T(1,128)S(1)}, u32[]{:S(2)}, u32[]{:S(2)}) async-start(f32[32,1,2176]{2,1,0:T(1,128)} %gram.1), calls=%async_computation.2 | async-start | bytes 557056 | tf_op jit(solution)/shard_map/all_to_all | solution.py:934
  52.6 2.7 %correct.1 = f32[16,16,1024]{2,1,0:T(8,128)} custom-call(f32[512,128]{1,0:T(8,128)S(1)} %bitcast.5, f32[2688,128]{1,0:T(8,128)S(1)} %local_part.1.psi_ref.local_ref), custom_call_target="tpu_custom_call" | custom-call | flops 20000000 | bytes 2000000 | tf_op jit(solution)/shard_map/correct/pallas_call | solution.py:844
  55.2 8.0 %all-to-all-done.2.in_ref = f32[32,1,2176]{2,1,0:T(1,128)S(1)} async-done(((f32[32,1,2176]{2,1,0:T(1,128)}), f32[32,1,2176]{2,1,0:T(1,128)S(1)}, u32[]{:S(2)}, u32[]{:S(2)}) %all-to-all-start.2) | async-done | bytes 278560 | tf_op jit(solution)/shard_map/all_to_all | solution.py:934
  63.2 0.8 %total.1 = f32[64,64]{1,0:T(8,128)} custom-call(f32[32,1,2176]{2,1,0:T(1,128)S(1)} %all-to-all-done.2.in_ref), custom_call_target="tpu_custom_call" | custom-call | tf_op jit(solution)/shard_map/total/pallas_call | solution.py:884
  (7 shorter events, 0.0 us)
Async XLA Ops:
  0.6 6.5 %copy-start = (f32[16,16,1024]{2,1,0:T(8,128)S(1)}, f32[16,16,1024]{2,1,0:T(8,128)}, u32[]{:S(2)}) copy-start(f32[16,16,1024]{2,1,0:T(8,128)} %rho_any.1) | copy-start | bytes 3145732
  1.8 15.7 %collective-permute-start = (f32[16,16,256]{2,1,0:T(8,128)S(1)}, f32[16,16,256]{2,1,0:T(8,128)S(1)}, u32[]{:S(2)}, u32[]{:S(2)}) collective-permute-start(f32[16,16,256]{2,1,0:T(8,128)S(1)} %get-tuple-element.9), channel_id=1, source_target_pairs={{0,1},{1,2},{2,3},{4,5},{5,6},{6,7},{8,9},{9,10},{10,11},{12,13},{... | collective-permute-start | bytes 786440 | tf_op jit(solution)/shard_map/ppermute | solution.py:901
  5.8 11.6 %collective-permute-start.1 = (f32[16,16,256]{2,1,0:T(8,128)S(1)}, f32[16,16,256]{2,1,0:T(8,128)S(1)}, u32[]{:S(2)}, u32[]{:S(2)}) collective-permute-start(f32[16,16,256]{2,1,0:T(8,128)S(1)} %get-tuple-element.8), channel_id=1, source_target_pairs={{1,0},{2,1},{3,2},{5,4},{6,5},{7,6},{9,8},{10,9},{11,10},{13,12},{... | collective-permute-start | bytes 786440 | tf_op jit(solution)/shard_map/ppermute | solution.py:901
  9.8 17.9 %all-to-all-start = ((f32[32,16,128]{2,1,0:T(8,128)}), f32[32,16,128]{2,1,0:T(8,128)S(1)}, u32[]{:S(2)}, u32[]{:S(2)}) async-start(f32[32,16,128]{2,1,0:T(8,128)} %bitcast), calls=%async_computation | async-start | bytes 524288 | tf_op jit(solution)/shard_map/all_to_all | solution.py:910
  19.0 14.6 %collective-permute-start.3 = (f32[16,40,128]{2,1,0:T(8,128)}, f32[16,40,128]{2,1,0:T(8,128)S(1)}, u32[]{:S(2)}, u32[]{:S(2)}) collective-permute-start(f32[16,40,128]{2,1,0:T(8,128)} %get-tuple-element.6), channel_id=1, source_target_pairs={{4,0},{8,4},{12,8},{5,1},{9,5},{13,9},{6,2},{10,6},{14,10},{7,3},{... | collective-permute-start | bytes 983048 | tf_op jit(solution)/shard_map/ppermute | solution.py:901
  21.2 12.4 %collective-permute-start.2 = (f32[16,40,128]{2,1,0:T(8,128)S(1)}, f32[16,40,128]{2,1,0:T(8,128)S(1)}, u32[]{:S(2)}, u32[]{:S(2)}) collective-permute-start(f32[16,40,128]{2,1,0:T(8,128)S(1)} %get-tuple-element.5), channel_id=1, source_target_pairs={{0,4},{4,8},{8,12},{1,5},{5,9},{9,13},{2,6},{6,10},{10,14},{3,7},{... | collective-permute-start | bytes 983048 | tf_op jit(solution)/shard_map/ppermute | solution.py:901
  24.6 10.5 %collective-permute-start.4 = (f32[576,128]{1,0:T(8,128)}, f32[576,128]{1,0:T(8,128)S(1)}, u32[]{:S(2)}, u32[]{:S(2)}) collective-permute-start(f32[576,128]{1,0:T(8,128)} %get-tuple-element.7), channel_id=1, source_target_pairs={{0,16},{16,0},{1,17},{17,1},{2,18},{18,2},{3,19},{19,3},{4,20},{20... | collective-permute-start | bytes 884744 | tf_op jit(solution)/shard_map/ppermute | solution.py:926
  30.9 13.9 %all-to-all-start.1 = ((f32[32,16,128]{2,1,0:T(8,128)}), f32[32,16,128]{2,1,0:T(8,128)S(1)}, u32[]{:S(2)}, u32[]{:S(2)}) async-start(f32[32,16,128]{2,1,0:T(8,128)} %bitcast.2), calls=%async_computation.1 | async-start | bytes 524288 | tf_op jit(solution)/shard_map/all_to_all | solution.py:910
  33.6 5.2 %collective-permute-start.5 = (f32[4,40,128]{2,1,0:T(8,128)S(1)}, f32[4,40,128]{2,1,0:T(8,128)S(1)}, u32[]{:S(2)}, u32[]{:S(2)}) collective-permute-start(f32[4,40,128]{2,1,0:T(8,128)S(1)} %pad_maximum_fusion), channel_id=1, source_target_pairs={{0,16},{16,0},{1,17},{17,1},{2,18},{18,2},{3,19},{19,3},{4,20},{20... | collective-permute-start | bytes 245768 | tf_op jit(solution)/shard_map/ppermute | solution.py:931
  46.2 17.1 %all-to-all-start.2 = ((f32[32,1,2176]{2,1,0:T(1,128)}), f32[32,1,2176]{2,1,0:T(1,128)S(1)}, u32[]{:S(2)}, u32[]{:S(2)}) async-start(f32[32,1,2176]{2,1,0:T(1,128)} %gram.1), calls=%async_computation.2 | async-start | bytes 557056 | tf_op jit(solution)/shard_map/all_to_all | solution.py:934

commit v7 on v6

--- a/solution.py
+++ b/solution.py
@@ -563,6 +563,14 @@
     return slots
 
 
+def layer_slots(distance, half):
+    return range(distance - 3, half + 3 - distance)
+
+
+def layer_start(distance, half):
+    return sum(len(layer_slots(d, half)) for d in range(1, distance))
+
+
 def faces_kernel(rho_ref, zlo_ref, zhi_ref, first_ref, last_ref, x_ref):
     size_x, size_y, merged = rho_ref.shape
     half = merged // LANES
@@ -574,29 +582,32 @@
             return [jnp.where(upper, f, l) for f, l in zip(first, last)]
 
         slots = slots_with_halo(rows(rho_ref), rows(zlo_ref), rows(zhi_ref), 2)
-        for j in range(-2, half + 2):
-            first_ref[x, pl.ds((j + 2) * 3, 3), :] = slots[j][:3]
-            last_ref[x, pl.ds((j + 2) * 3, 3), :] = slots[j][5:]
+        for d in (1, 2, 3):
+            for n, j in enumerate(layer_slots(d, half)):
+                at = pl.ds(layer_start(d, half) + n, 1)
+                first_ref[x, at, :] = slots[j][d - 1 : d]
+                last_ref[x, at, :] = slots[j][8 - d : 9 - d]
 
     loop(size_x, pack, 4)
-    start = jnp.where(lax.axis_index("gx") == 0, size_x - 3, 0)
-    for i in range(3):
+    low = lax.axis_index("gx") == 0
+    for d in (1, 2, 3):
+        plane = jnp.where(low, size_x - d, d - 1)
         for y in range(0, size_y, 8):
             rows = pl.ds(y, 8)
-            natural, before, after = (lane_tiles(ref, start + i, rows) for ref in (rho_ref, zlo_ref, zhi_ref))
+            natural, before, after = (lane_tiles(ref, plane, rows) for ref in (rho_ref, zlo_ref, zhi_ref))
             slots = slots_with_halo(natural, before, after, 2)
-            for j in range(-2, half + 2):
-                x_ref[pl.ds((i * (half + 4) + (j + 2)) * size_y + y, 8), :] = slots[j]
+            for n, j in enumerate(layer_slots(d, half)):
+                x_ref[pl.ds((layer_start(d, half) + n) * size_y + y, 8), :] = slots[j]
 
 
 def faces(density, zlo, zhi):
     size_x, size_y, merged = density.shape
     half = merged // LANES
-    rows = -(-3 * (half + 4) // 8) * 8
+    rows = -(-layer_start(4, half) // 8) * 8
     shape = lambda *dims: jax.ShapeDtypeStruct(dims + (LANES,), jnp.float32)
     return pl.pallas_call(
         faces_kernel,
-        out_shape=(shape(size_x, rows), shape(size_x, rows), shape(3 * (half + 4) * size_y)),
+        out_shape=(shape(size_x, rows), shape(size_x, rows), shape(layer_start(4, half) * size_y)),
         in_specs=[pl.BlockSpec(memory_space=pltpu.VMEM)] * 3,
         out_specs=(pl.BlockSpec(memory_space=pltpu.VMEM),) * 3,
         compiler_params=pltpu.CompilerParams(vmem_limit_bytes=8 << 20),
@@ -633,28 +644,30 @@
             for j, value in slots_with_halo(natural, before, after, 3).items():
                 r_ref[pl.ds(r_row(x, j, y), 8), :] = value
 
+    def line(x, d, y):
+        return pl.ds(r_row(x, d - 3, y), len(layer_slots(d, half)), stride=PITCH)
+
     def place_y(x):
-        for j in range(-2, half + 2):
-            r_ref[pl.ds(r_row(x, j, -3), 3), :] = ylo_ref[x, pl.ds((j + 2) * 3, 3), :]
-            r_ref[pl.ds(r_row(x, j, size_y), 3), :] = yhi_ref[x, pl.ds((j + 2) * 3, 3), :]
+        for d in (1, 2, 3):
+            at = pl.ds(layer_start(d, half), len(layer_slots(d, half)))
+            r_ref[line(x, d, -d), :] = ylo_ref[x, at, :]
+            r_ref[line(x, d, size_y + d - 1), :] = yhi_ref[x, at, :]
 
     loop(size_x, place_y, 2)
 
-    def place_outer(i):
-        for j in range(-2, half + 2):
+    for d in (1, 2, 3):
+        for n, j in enumerate(layer_slots(d, half)):
             for y in range(0, size_y, 8):
-                value = x_ref[pl.ds((i * (half + 4) + (j + 2)) * size_y + y, 8), :]
-                r_ref[pl.ds(r_row(i - 3, j, y), 8), :] = value * flags[0]
-                r_ref[pl.ds(r_row(i + size_x, j, y), 8), :] = value * flags[1]
-
-    loop(3, place_outer)
-    for i in range(2):
-        for j in range(-2, half + 2):
-            low = edge_ref[i, pl.ds((j + 2) * 3 + 1, 2), :]
-            high = edge_ref[i + 2, pl.ds((j + 2) * 3, 2), :]
-            for x, scale in ((i - 2, flags[0]), (i + size_x, flags[1])):
-                r_ref[pl.ds(r_row(x, j, -2), 2), :] = low * scale
-                r_ref[pl.ds(r_row(x, j, size_y), 2), :] = high * scale
+                value = x_ref[pl.ds((layer_start(d, half) + n) * size_y + y, 8), :]
+                r_ref[pl.ds(r_row(-d, j, y), 8), :] = value * flags[0]
+                r_ref[pl.ds(r_row(size_x + d - 1, j, y), 8), :] = value * flags[1]
+    for dx in (1, 2):
+        for dy in range(1, 4 - dx):
+            at = pl.ds(layer_start(dy, half), len(layer_slots(dy, half)))
+            before, after = edge_ref[dx - 1, at, :], edge_ref[dx + 1, at, :]
+            for x, scale in ((-dx, flags[0]), (size_x + dx - 1, flags[1])):
+                r_ref[line(x, dy, -dy), :] = before * scale
+                r_ref[line(x, dy, size_y + dy - 1), :] = after * scale
 
     for part in range(FETCHES):
         arrive(part)
@@ -927,7 +940,10 @@
     answers = solve(received, devices, block, LEVELS - 1)
     correction = exchanged(answers)
     low = lax.axis_index("gx") == 0
-    edge = jnp.concatenate([jnp.where(low, a[-2:], a[:2]) for a in (ylo, yhi)], axis=0)
+    kept = -(-layer_start(3, merged // LANES) // 8) * 8
+    edge = jnp.concatenate(
+        [jnp.where(low, a[-d], a[d - 1])[None, :kept] for a in (ylo, yhi) for d in (1, 2)], axis=0
+    )
     edge = lax.ppermute(edge, "gx", swapped)
     psi = local_part(density, messages, (zlo, zhi, ylo, yhi, beside, edge))
     parts = gram(correction, psi, count)

time: 64.6 us -> 64.1 us (level)
    ppermute x1, waiting for transfers between devices: 3.79 us -> 2.03 us  [fast_local(): edge = lax.ppermute(edge, 'gx', swapped)]
    all_to_all x2, waiting for transfers between devices: 1.78 us -> 2.94 us  [exchanged(): lax.all_to_all(shaped, axes, 0, 0, tiled=True).reshape(messages.shape)]
  transfers between devices with their start and end apart: 9 -> 9, of which waited for: 3 -> 4; matrix products, arithmetic and copies ran while one was open for 0% -> 0% of each run, Pallas kernels for 25% -> 25%
where the time goes in v7:
time: 64.1 us; the launch traced here: 63.6 us
  starting transfers between devices  30.6 us (48%)
  Pallas kernels  18.1 us (28%)
  waiting for transfers between devices  13 us (20%)
  local copies, waits for them, and re-layouts  1.18 us (2%)
  between operations  0.8 us (1%)
    all_to_all x2, starting transfers between devices, exchanged(): lax.all_to_all(shaped, axes, 0, 0, tiled=True).reshape(messages.shape)  10.8 us
    ppermute x4, starting transfers between devices, shifted(): return (lax.ppermute(last, axis, up), lax.ppermute(first, axis, down))  10.8 us
    all_to_all x1, waiting for transfers between devices, fast_local(): parts = lax.all_to_all(parts, AXES, 0, 0, tiled=True)  7.98 us
    all_to_all x1, starting transfers between devices, fast_local(): parts = lax.all_to_all(parts, AXES, 0, 0, tiled=True)  6.26 us
    pallas_call x1, Pallas kernels, local_part(): pl.pallas_call(local_kernel, out_shape=jax.ShapeDtypeStruct((size_x * hal...  5.9 us
    pallas_call x1, Pallas kernels, solve(): pl.pallas_call(functools.partial(solve_kernel, devices, own, block), out_...  3.1 us
    all_to_all x2, waiting for transfers between devices, exchanged(): lax.all_to_all(shaped, axes, 0, 0, tiled=True).reshape(messages.shape)  2.94 us
    pallas_call x1, Pallas kernels, share(): pl.pallas_call(share_kernel, out_shape=jax.ShapeDtypeStruct((rows, LANES)...  2.7 us
  transfers between devices with their start and end apart: 9, of which 4 were waited for; matrix products, arithmetic and copies ran while one was open for 0% of the time, Pallas kernels for 25%

profile of v7, /device:TPU:1, one launch (start us, length us, event | category | flops | bytes accessed | tf_op | source)
XLA Modules:
  0.0 63.6 jit_solution(3262531742023295602)
XLA Ops:
  0.6 0.0 copy-start
  0.6 1.2 %fusion = (f32[16,16,256]{2,1,0:T(8,128)S(1)}, f32[16,16,256]{2,1,0:T(8,128)S(1)}) fusion(f32[16,16,1024]{2,1,0:T(8,128)} %rho_any.1), kind=kLoop, calls=%fused_computation.5 | loop fusion | bytes 1048576 | tf_op jit(solution)/shard_map/slice | solution.py:934
  1.8 4.0 %collective-permute-start = (f32[16,16,256]{2,1,0:T(8,128)S(1)}, f32[16,16,256]{2,1,0:T(8,128)S(1)}, u32[]{:S(2)}, u32[]{:S(2)}) collective-permute-start(f32[16,16,256]{2,1,0:T(8,128)S(1)} %get-tuple-element.9), channel_id=1, source_target_pairs={{0,1},{1,2},{2,3},{4,5},{5,6},{6,7},{8,9},{9,10},{10,11},{12,13},{... | collective-permute-start | bytes 786440 | tf_op jit(solution)/shard_map/ppermute | solution.py:914
  5.8 1.3 %collective-permute-start.1 = (f32[16,16,256]{2,1,0:T(8,128)S(1)}, f32[16,16,256]{2,1,0:T(8,128)S(1)}, u32[]{:S(2)}, u32[]{:S(2)}) collective-permute-start(f32[16,16,256]{2,1,0:T(8,128)S(1)} %get-tuple-element.8), channel_id=1, source_target_pairs={{1,0},{2,1},{3,2},{5,4},{6,5},{7,6},{9,8},{10,9},{11,10},{13,12},{... | collective-permute-start | bytes 786440 | tf_op jit(solution)/shard_map/ppermute | solution.py:914
  7.2 2.7 %share.1.sent_any = f32[512,128]{1,0:T(8,128)} custom-call(f32[16,16,1024]{2,1,0:T(8,128)S(1)} %copy-done), custom_call_target="tpu_custom_call" | custom-call | flops 20000000 | bytes 2000000 | tf_op jit(solution)/shard_map/share/pallas_call | solution.py:272
  9.9 7.6 %all-to-all-start = ((f32[32,16,128]{2,1,0:T(8,128)}), f32[32,16,128]{2,1,0:T(8,128)S(1)}, u32[]{:S(2)}, u32[]{:S(2)}) async-start(f32[32,16,128]{2,1,0:T(8,128)} %bitcast), calls=%async_computation | async-start | bytes 524288 | tf_op jit(solution)/shard_map/all_to_all | solution.py:923
  17.5 1.5 %faces.1 = (f32[16,32,128]{2,1,0:T(8,128)S(1)}, f32[16,32,128]{2,1,0:T(8,128)S(1)}, f32[480,128]{1,0:T(8,128)}) custom-call(f32[16,16,1024]{2,1,0:T(8,128)S(1)} %copy-done, f32[16,16,256]{2,1,0:T(8,128)S(1)} %collective-permute-done.zlo_ref, f32[16,16,256]{2,1,0:T(8,128)S(1)} %collective-permute-done.1.zhi_ref), custom_call_target="tpu_custom_call" | custom-call | flops 8000000 | bytes 2000000 | tf_op jit(solution)/shard_map/faces/pallas_call | solution.py:608
  19.0 3.5 %collective-permute-start.2 = (f32[16,32,128]{2,1,0:T(8,128)S(1)}, f32[16,32,128]{2,1,0:T(8,128)S(1)}, u32[]{:S(2)}, u32[]{:S(2)}) collective-permute-start(f32[16,32,128]{2,1,0:T(8,128)S(1)} %get-tuple-element.5), channel_id=1, source_target_pairs={{0,4},{4,8},{8,12},{1,5},{5,9},{9,13},{2,6},{6,10},{10,14},{3,7},{... | collective-permute-start | bytes 786440 | tf_op jit(solution)/shard_map/ppermute | solution.py:914
  22.5 1.9 %collective-permute-start.3 = (f32[16,32,128]{2,1,0:T(8,128)S(1)}, f32[16,32,128]{2,1,0:T(8,128)S(1)}, u32[]{:S(2)}, u32[]{:S(2)}) collective-permute-start(f32[16,32,128]{2,1,0:T(8,128)S(1)} %get-tuple-element.6), channel_id=1, source_target_pairs={{4,0},{8,4},{12,8},{5,1},{9,5},{13,9},{6,2},{10,6},{14,10},{7,3},{... | collective-permute-start | bytes 786440 | tf_op jit(solution)/shard_map/ppermute | solution.py:914
  24.5 1.2 %collective-permute-start.4 = (f32[480,128]{1,0:T(8,128)}, f32[480,128]{1,0:T(8,128)S(1)}, u32[]{:S(2)}, u32[]{:S(2)}) collective-permute-start(f32[480,128]{1,0:T(8,128)} %get-tuple-element.7), channel_id=1, source_target_pairs={{0,16},{16,0},{1,17},{17,1},{2,18},{18,2},{3,19},{19,3},{4,20},{20... | collective-permute-start | bytes 737288 | tf_op jit(solution)/shard_map/ppermute | solution.py:939
  25.7 2.1 %all-to-all-done = f32[32,16,128]{2,1,0:T(8,128)S(1)} async-done(((f32[32,16,128]{2,1,0:T(8,128)}), f32[32,16,128]{2,1,0:T(8,128)S(1)}, u32[]{:S(2)}, u32[]{:S(2)}) %all-to-all-start) | async-done | bytes 262176 | tf_op jit(solution)/shard_map/all_to_all | solution.py:923
  27.8 3.1 %solve.1 = f32[512,128]{1,0:T(8,128)} custom-call(f32[512,128]{1,0:T(8,128)S(1)} %bitcast.6, f32[256,256]{1,0:T(8,128)} %constant.10.clone.dense_any), custom_call_target="tpu_custom_call" | custom-call | flops 20000000 | bytes 2000000 | tf_op jit(solution)/shard_map/solve/pallas_call | solution.py:535
  30.9 3.2 %all-to-all-start.1 = ((f32[32,16,128]{2,1,0:T(8,128)}), f32[32,16,128]{2,1,0:T(8,128)S(1)}, u32[]{:S(2)}, u32[]{:S(2)}) async-start(f32[32,16,128]{2,1,0:T(8,128)} %bitcast.2), calls=%async_computation.1 | async-start | bytes 524288 | tf_op jit(solution)/shard_map/all_to_all | solution.py:923
  34.2 0.0 collective-permute-done.3.yhi_ref
  34.2 1.4 %collective-permute-start.5 = (f32[4,24,128]{2,1,0:T(8,128)S(1)}, f32[4,24,128]{2,1,0:T(8,128)S(1)}, u32[]{:S(2)}, u32[]{:S(2)}) collective-permute-start(f32[4,24,128]{2,1,0:T(8,128)S(1)} %pad_maximum_fusion), channel_id=1, source_target_pairs={{0,16},{16,0},{1,17},{17,1},{2,18},{18,2},{3,19},{19,3},{4,20},{20... | collective-permute-start | bytes 147464 | tf_op jit(solution)/shard_map/ppermute | solution.py:947
  35.7 0.0 collective-permute-done.4.x_ref
  35.7 2.0 %collective-permute-done.5.edge_ref = f32[4,24,128]{2,1,0:T(8,128)S(1)} collective-permute-done((f32[4,24,128]{2,1,0:T(8,128)S(1)}, f32[4,24,128]{2,1,0:T(8,128)S(1)}, u32[]{:S(2)}, u32[]{:S(2)}) %collective-permute-start.5) | collective-permute-done | bytes 49184 | tf_op jit(solution)/shard_map/ppermute | solution.py:947
  37.7 5.9 %local_part.1.psi_ref.local_ref = f32[2688,128]{1,0:T(8,128)S(1)} custom-call(f32[16,16,1024]{2,1,0:T(8,128)} %rho_any.1, f32[512,128]{1,0:T(8,128)} %share.1.sent_any, f32[16,16,256]{2,1,0:T(8,128)S(1)} %collective-permute-done.zlo_ref, f32[16,16,256]{2,1,0:T(8,128)S(1)} %collective-permute-done.1.zhi_ref, ...), custom_call_target="tpu_custom_call" | custom-call | flops 30000000 | bytes 4000000 | tf_op jit(solution)/shard_map/local_part/pallas_call | solution.py:729
  43.6 0.9 %all-to-all-done.1 = f32[32,16,128]{2,1,0:T(8,128)S(1)} async-done(((f32[32,16,128]{2,1,0:T(8,128)}), f32[32,16,128]{2,1,0:T(8,128)S(1)}, u32[]{:S(2)}, u32[]{:S(2)}) %all-to-all-start.1) | async-done | bytes 262176 | tf_op jit(solution)/shard_map/all_to_all | solution.py:923
  44.5 1.4 %gram.1 = f32[32,1,2176]{2,1,0:T(1,128)} custom-call(f32[512,128]{1,0:T(8,128)S(1)} %bitcast.4, f32[2688,128]{1,0:T(8,128)S(1)} %local_part.1.psi_ref.local_ref), custom_call_target="tpu_custom_call" | custom-call | tf_op jit(solution)/shard_map/gram/pallas_call | solution.py:778
  45.8 6.3 %all-to-all-start.2 = ((f32[32,1,2176]{2,1,0:T(1,128)}), f32[32,1,2176]{2,1,0:T(1,128)S(1)}, u32[]{:S(2)}, u32[]{:S(2)}) async-start(f32[32,1,2176]{2,1,0:T(1,128)} %gram.1), calls=%async_computation.2 | async-start | bytes 557056 | tf_op jit(solution)/shard_map/all_to_all | solution.py:950
  52.1 2.7 %correct.1 = f32[16,16,1024]{2,1,0:T(8,128)} custom-call(f32[512,128]{1,0:T(8,128)S(1)} %bitcast.5, f32[2688,128]{1,0:T(8,128)S(1)} %local_part.1.psi_ref.local_ref), custom_call_target="tpu_custom_call" | custom-call | flops 20000000 | bytes 2000000 | tf_op jit(solution)/shard_map/correct/pallas_call | solution.py:857
  54.8 8.0 %all-to-all-done.2.in_ref = f32[32,1,2176]{2,1,0:T(1,128)S(1)} async-done(((f32[32,1,2176]{2,1,0:T(1,128)}), f32[32,1,2176]{2,1,0:T(1,128)S(1)}, u32[]{:S(2)}, u32[]{:S(2)}) %all-to-all-start.2) | async-done | bytes 278560 | tf_op jit(solution)/shard_map/all_to_all | solution.py:950
  62.8 0.8 %total.1 = f32[64,64]{1,0:T(8,128)} custom-call(f32[32,1,2176]{2,1,0:T(1,128)S(1)} %all-to-all-done.2.in_ref), custom_call_target="tpu_custom_call" | custom-call | tf_op jit(solution)/shard_map/total/pallas_call | solution.py:897
  (9 shorter events, 0.0 us)
Async XLA Ops:
  0.6 6.5 %copy-start = (f32[16,16,1024]{2,1,0:T(8,128)S(1)}, f32[16,16,1024]{2,1,0:T(8,128)}, u32[]{:S(2)}) copy-start(f32[16,16,1024]{2,1,0:T(8,128)} %rho_any.1) | copy-start | bytes 3145732
  1.8 15.7 %collective-permute-start = (f32[16,16,256]{2,1,0:T(8,128)S(1)}, f32[16,16,256]{2,1,0:T(8,128)S(1)}, u32[]{:S(2)}, u32[]{:S(2)}) collective-permute-start(f32[16,16,256]{2,1,0:T(8,128)S(1)} %get-tuple-element.9), channel_id=1, source_target_pairs={{0,1},{1,2},{2,3},{4,5},{5,6},{6,7},{8,9},{9,10},{10,11},{12,13},{... | collective-permute-start | bytes 786440 | tf_op jit(solution)/shard_map/ppermute | solution.py:914
  5.8 11.6 %collective-permute-start.1 = (f32[16,16,256]{2,1,0:T(8,128)S(1)}, f32[16,16,256]{2,1,0:T(8,128)S(1)}, u32[]{:S(2)}, u32[]{:S(2)}) collective-permute-start(f32[16,16,256]{2,1,0:T(8,128)S(1)} %get-tuple-element.8), channel_id=1, source_target_pairs={{1,0},{2,1},{3,2},{5,4},{6,5},{7,6},{9,8},{10,9},{11,10},{13,12},{... | collective-permute-start | bytes 786440 | tf_op jit(solution)/shard_map/ppermute | solution.py:914
  9.9 17.9 %all-to-all-start = ((f32[32,16,128]{2,1,0:T(8,128)}), f32[32,16,128]{2,1,0:T(8,128)S(1)}, u32[]{:S(2)}, u32[]{:S(2)}) async-start(f32[32,16,128]{2,1,0:T(8,128)} %bitcast), calls=%async_computation | async-start | bytes 524288 | tf_op jit(solution)/shard_map/all_to_all | solution.py:923
  19.0 15.2 %collective-permute-start.2 = (f32[16,32,128]{2,1,0:T(8,128)S(1)}, f32[16,32,128]{2,1,0:T(8,128)S(1)}, u32[]{:S(2)}, u32[]{:S(2)}) collective-permute-start(f32[16,32,128]{2,1,0:T(8,128)S(1)} %get-tuple-element.5), channel_id=1, source_target_pairs={{0,4},{4,8},{8,12},{1,5},{5,9},{9,13},{2,6},{6,10},{10,14},{3,7},{... | collective-permute-start | bytes 786440 | tf_op jit(solution)/shard_map/ppermute | solution.py:914
  22.5 11.7 %collective-permute-start.3 = (f32[16,32,128]{2,1,0:T(8,128)S(1)}, f32[16,32,128]{2,1,0:T(8,128)S(1)}, u32[]{:S(2)}, u32[]{:S(2)}) collective-permute-start(f32[16,32,128]{2,1,0:T(8,128)S(1)} %get-tuple-element.6), channel_id=1, source_target_pairs={{4,0},{8,4},{12,8},{5,1},{9,5},{13,9},{6,2},{10,6},{14,10},{7,3},{... | collective-permute-start | bytes 786440 | tf_op jit(solution)/shard_map/ppermute | solution.py:914
  24.5 11.2 %collective-permute-start.4 = (f32[480,128]{1,0:T(8,128)}, f32[480,128]{1,0:T(8,128)S(1)}, u32[]{:S(2)}, u32[]{:S(2)}) collective-permute-start(f32[480,128]{1,0:T(8,128)} %get-tuple-element.7), channel_id=1, source_target_pairs={{0,16},{16,0},{1,17},{17,1},{2,18},{18,2},{3,19},{19,3},{4,20},{20... | collective-permute-start | bytes 737288 | tf_op jit(solution)/shard_map/ppermute | solution.py:939
  30.9 13.6 %all-to-all-start.1 = ((f32[32,16,128]{2,1,0:T(8,128)}), f32[32,16,128]{2,1,0:T(8,128)S(1)}, u32[]{:S(2)}, u32[]{:S(2)}) async-start(f32[32,16,128]{2,1,0:T(8,128)} %bitcast.2), calls=%async_computation.1 | async-start | bytes 524288 | tf_op jit(solution)/shard_map/all_to_all | solution.py:923
  34.2 3.5 %collective-permute-start.5 = (f32[4,24,128]{2,1,0:T(8,128)S(1)}, f32[4,24,128]{2,1,0:T(8,128)S(1)}, u32[]{:S(2)}, u32[]{:S(2)}) collective-permute-start(f32[4,24,128]{2,1,0:T(8,128)S(1)} %pad_maximum_fusion), channel_id=1, source_target_pairs={{0,16},{16,0},{1,17},{17,1},{2,18},{18,2},{3,19},{19,3},{4,20},{20... | collective-permute-start | bytes 147464 | tf_op jit(solution)/shard_map/ppermute | solution.py:947
  45.8 16.9 %all-to-all-start.2 = ((f32[32,1,2176]{2,1,0:T(1,128)}), f32[32,1,2176]{2,1,0:T(1,128)S(1)}, u32[]{:S(2)}, u32[]{:S(2)}) async-start(f32[32,1,2176]{2,1,0:T(1,128)} %gram.1), calls=%async_computation.2 | async-start | bytes 557056 | tf_op jit(solution)/shard_map/all_to_all | solution.py:950

commit v8 on v7

--- a/solution.py
+++ b/solution.py
@@ -158,16 +158,23 @@
     masks = [row_mask(-1 + 8 * i, 1, size_y, flags[2], flags[3]) for i in range(3)]
     z_first, z_last = edge_lanes(flags)
 
-    def smooth(x):
+    def smooth(step):
+        x = 2 * step
         for i in range(3):
             y = -1 + 8 * i
-            centre = column(r_ref, r_row, x, y, -2, half + 2)
+            first = column(r_ref, r_row, x, y, -2, half + 2)
+            second = column(r_ref, r_row, x + 1, y, -2, half + 2)
             mask = masks[i] * SIDE
             for j in range(-1, half + 1):
-                value = inside(weighted(r_ref, r_row, x, j, y, centre), mask, j, half, z_first, z_last)
-                t_ref[pl.ds(t_row(x, j, y), 8), :] = value
-
-    loop(size_x, smooth)
+                before = r_ref[pl.ds(r_row(x - 1, j, y), 8), :]
+                after = r_ref[pl.ds(r_row(x + 2, j, y), 8), :]
+                for at, centre, along_x in ((x, first, before + second[j]), (x + 1, second, first[j] + after)):
+                    around = (centre[j - 1] + centre[j + 1]) + RATIO * centre[j]
+                    beside = r_ref[pl.ds(r_row(at, j, y - 1), 8), :] + r_ref[pl.ds(r_row(at, j, y + 1), 8), :]
+                    value = inside(around + (beside + along_x), mask, j, half, z_first, z_last)
+                    t_ref[pl.ds(t_row(at, j, y), 8), :] = value
+
+    loop(size_x // 2, smooth)
     for x, near in ((-1, 0), (size_x, size_x - 1)):
         scale = plane_scale(flags, x, size_x)
         for i in range(3):
@@ -550,6 +557,16 @@
     return [ref[at, rows, pl.ds(LANES * k, LANES)] for k in range(ref.shape[2] // LANES)]
 
 
+def is_even(axis):
+    return lax.axis_index(axis) % 2 == 0
+
+
+def before_after(axis, first_swap, second_swap):
+    even = is_even(axis)
+    pairs = list(zip(first_swap, second_swap))
+    return [jnp.where(even, b, a) for a, b in pairs], [jnp.where(even, a, b) for a, b in pairs]
+
+
 def slots_with_halo(natural, before, after, reach):
     packed = pack_tiles(natural)
     half = len(packed)
@@ -571,9 +588,10 @@
     return sum(len(layer_slots(d, half)) for d in range(1, distance))
 
 
-def faces_kernel(rho_ref, zlo_ref, zhi_ref, first_ref, last_ref, x_ref):
+def faces_kernel(rho_ref, za_ref, zb_ref, ya_ref, yb_ref, x_ref):
     size_x, size_y, merged = rho_ref.shape
     half = merged // LANES
+    even_y = is_even("gy")
 
     def pack(x):
         def rows(ref):
@@ -581,12 +599,13 @@
             upper = lax.broadcasted_iota(jnp.int32, (8, LANES), 0) < 4
             return [jnp.where(upper, f, l) for f, l in zip(first, last)]
 
-        slots = slots_with_halo(rows(rho_ref), rows(zlo_ref), rows(zhi_ref), 2)
+        slots = slots_with_halo(rows(rho_ref), *before_after("gz", rows(za_ref), rows(zb_ref)), 2)
         for d in (1, 2, 3):
             for n, j in enumerate(layer_slots(d, half)):
                 at = pl.ds(layer_start(d, half) + n, 1)
-                first_ref[x, at, :] = slots[j][d - 1 : d]
-                last_ref[x, at, :] = slots[j][8 - d : 9 - d]
+                first, last = slots[j][d - 1 : d], slots[j][8 - d : 9 - d]
+                ya_ref[x, at, :] = jnp.where(even_y, last, first)
+                yb_ref[x, at, :] = jnp.where(even_y, first, last)
 
     loop(size_x, pack, 4)
     low = lax.axis_index("gx") == 0
@@ -594,13 +613,13 @@
         plane = jnp.where(low, size_x - d, d - 1)
         for y in range(0, size_y, 8):
             rows = pl.ds(y, 8)
-            natural, before, after = (lane_tiles(ref, plane, rows) for ref in (rho_ref, zlo_ref, zhi_ref))
-            slots = slots_with_halo(natural, before, after, 2)
+            natural, first, second = (lane_tiles(ref, plane, rows) for ref in (rho_ref, za_ref, zb_ref))
+            slots = slots_with_halo(natural, *before_after("gz", first, second), 2)
             for n, j in enumerate(layer_slots(d, half)):
                 x_ref[pl.ds((layer_start(d, half) + n) * size_y + y, 8), :] = slots[j]
 
 
-def faces(density, zlo, zhi):
+def faces(density, za, zb):
     size_x, size_y, merged = density.shape
     half = merged // LANES
     rows = -(-layer_start(4, half) // 8) * 8
@@ -613,11 +632,34 @@
         compiler_params=pltpu.CompilerParams(vmem_limit_bytes=8 << 20),
         cost_estimate=pl.CostEstimate(flops=8_000_000, bytes_accessed=2_000_000, transcendentals=0),
         name="faces",
-    )(density, zlo, zhi)
+    )(density, za, zb)
+
+
+def edges_kernel(ya_ref, yb_ref, out_ref):
+    size_x = ya_ref.shape[0]
+    low = lax.axis_index("gx") == 0
+    for d in (1, 2):
+        plane = jnp.where(low, size_x - d, d - 1)
+        got = [[ref[plane, pl.ds(0, out_ref.shape[1]), :]] for ref in (ya_ref, yb_ref)]
+        before, after = before_after("gy", *got)
+        out_ref[d - 1] = before[0]
+        out_ref[d + 1] = after[0]
+
+
+def edges(ya, yb, half):
+    kept = -(-layer_start(3, half) // 8) * 8
+    return pl.pallas_call(
+        edges_kernel,
+        out_shape=jax.ShapeDtypeStruct((4, kept, LANES), jnp.float32),
+        in_specs=[pl.BlockSpec(memory_space=pltpu.VMEM)] * 2,
+        out_specs=pl.BlockSpec(memory_space=pltpu.VMEM),
+        compiler_params=pltpu.CompilerParams(vmem_limit_bytes=4 << 20),
+        name="edges",
+    )(ya, yb)
 
 
 def local_kernel(
-    rho_any, sent_any, zlo_ref, zhi_ref, ylo_ref, yhi_ref, x_ref, edge_ref, psi_ref,
+    rho_any, sent_any, za_ref, zb_ref, ya_ref, yb_ref, x_ref, edge_ref, psi_ref,
     rho_ref, r_ref, v_ref, p_ref, sems, sem
 ):
     arrive = fetch_planes(rho_any, rho_ref, sems)
@@ -640,8 +682,8 @@
 
     def place(x):
         for y in range(0, size_y, 8):
-            natural, before, after = (lane_tiles(ref, x, pl.ds(y, 8)) for ref in (rho_ref, zlo_ref, zhi_ref))
-            for j, value in slots_with_halo(natural, before, after, 3).items():
+            natural, first, second = (lane_tiles(ref, x, pl.ds(y, 8)) for ref in (rho_ref, za_ref, zb_ref))
+            for j, value in slots_with_halo(natural, *before_after("gz", first, second), 3).items():
                 r_ref[pl.ds(r_row(x, j, y), 8), :] = value
 
     def line(x, d, y):
@@ -650,8 +692,9 @@
     def place_y(x):
         for d in (1, 2, 3):
             at = pl.ds(layer_start(d, half), len(layer_slots(d, half)))
-            r_ref[line(x, d, -d), :] = ylo_ref[x, at, :]
-            r_ref[line(x, d, size_y + d - 1), :] = yhi_ref[x, at, :]
+            before, after = before_after("gy", [ya_ref[x, at, :]], [yb_ref[x, at, :]])
+            r_ref[line(x, d, -d), :] = before[0]
+            r_ref[line(x, d, size_y + d - 1), :] = after[0]
 
     loop(size_x, place_y, 2)
 
@@ -904,14 +947,9 @@
     )(parts)
 
 
-def along(size):
-    up = [(i, i + 1) for i in range(size - 1)]
-    return up, [(j, i) for i, j in up]
-
-
-def shifted(first, last, axis):
-    up, down = along(lax.axis_size(axis))
-    return lax.ppermute(last, axis, up), lax.ppermute(first, axis, down)
+def swaps(axis):
+    size = lax.axis_size(axis)
+    return [[(i + k, i + 1 - k) for i in range(start, size - 1, 2) for k in (0, 1)] for start in (0, 1)]
 
 
 def exchanged(messages, axes=AXES):
@@ -931,21 +969,23 @@
 
     deep = 4 * PAIRS
     swapped = [(0, 1), (1, 0)]
-    zlo, zhi = shifted(density[..., :deep], density[..., -deep:], "gz")
+    even = is_even("gz")
+    first, last = density[..., :deep], density[..., -deep:]
+    pairs_a, pairs_b = swaps("gz")
+    zb = lax.ppermute(jnp.where(even, first, last), "gz", pairs_b)
+    za = lax.ppermute(jnp.where(even, last, first), "gz", pairs_a)
     messages = share(density)
     received = exchanged(messages)
-    first, last, plane = faces(density, zlo, zhi)
-    ylo, yhi = shifted(first, last, "gy")
+    face_a, face_b, plane = faces(density, za, zb)
+    pairs_a, pairs_b = swaps("gy")
+    ya = lax.ppermute(face_a, "gy", pairs_a)
+    yb = lax.ppermute(face_b, "gy", pairs_b)
     beside = lax.ppermute(plane, "gx", swapped)
     answers = solve(received, devices, block, LEVELS - 1)
     correction = exchanged(answers)
-    low = lax.axis_index("gx") == 0
-    kept = -(-layer_start(3, merged // LANES) // 8) * 8
-    edge = jnp.concatenate(
-        [jnp.where(low, a[-d], a[d - 1])[None, :kept] for a in (ylo, yhi) for d in (1, 2)], axis=0
-    )
+    edge = edges(ya, yb, merged // LANES)
     edge = lax.ppermute(edge, "gx", swapped)
-    psi = local_part(density, messages, (zlo, zhi, ylo, yhi, beside, edge))
+    psi = local_part(density, messages, (za, zb, ya, yb, beside, edge))
     parts = gram(correction, psi, count)
     parts = lax.all_to_all(parts, AXES, 0, 0, tiled=True)
     potential = correct(correction, psi, density.shape)

time: 64.1 us -> 66 us (1.030)
  waiting for transfers between devices: 13 us -> 21.8 us
  starting transfers between devices: 30.6 us -> 24.3 us
  Pallas kernels: 18.1 us -> 17.3 us
    all_to_all x2, waiting for transfers between devices: 2.94 us -> 8.04 us  [exchanged(): lax.all_to_all(shaped, axes, 0, 0, tiled=True).reshape(messages.shape)]
    ppermute x4, starting transfers between devices: 10.8 us -> 5.79 us  [the longest x1 3.38 us: fast_local(): yb = lax.ppermute(face_b, 'gy', pairs_b)]
    ppermute x4, waiting for transfers between devices: 0.01 us -> 4.3 us  [the longest x1 4.29 us: fast_local(): yb = lax.ppermute(face_b, 'gy', pairs_b)]
    unnamed x2 -> x4, local copies, waits for them, and re-layouts: 0.01 us -> 1.22 us
    slice x3 -> x0, local copies, waits for them, and re-layouts: 1.17 us -> none  [the longest x1 1.15 us: fast_local(): zlo, zhi = shifted(density[..., :deep], density[..., -deep:], 'gz')]
    ppermute x1, waiting for transfers between devices: 2.03 us -> 0.89 us  [fast_local(): edge = lax.ppermute(edge, 'gx', swapped)]
    all_to_all x2, starting transfers between devices: 10.8 us -> 9.85 us  [exchanged(): lax.all_to_all(shaped, axes, 0, 0, tiled=True).reshape(messages.shape)]
    pallas_call x1, Pallas kernels: 1.49 us -> 0.83 us  [faces(): pl.pallas_call(faces_kernel, out_shape=(shape(size_x, rows), shape(size_x...]
  transfers between devices with their start and end apart: 9 -> 9, of which waited for: 4 -> 5; matrix products, arithmetic and copies ran while one was open for 0% -> 0% of each run, Pallas kernels for 25% -> 19%
where the time goes in v8:
time: 66 us; the launch traced here: 65.5 us
  starting transfers between devices  24.3 us (37%)
  waiting for transfers between devices  21.8 us (33%)
  Pallas kernels  17.3 us (26%)
  local copies, waits for them, and re-layouts  1.22 us (2%)
  between operations  0.76 us (1%)
    all_to_all x2, starting transfers between devices, exchanged(): lax.all_to_all(shaped, axes, 0, 0, tiled=True).reshape(messages.shape)  9.85 us
    all_to_all x2, waiting for transfers between devices, exchanged(): lax.all_to_all(shaped, axes, 0, 0, tiled=True).reshape(messages.shape)  8.04 us
    all_to_all x1, waiting for transfers between devices, fast_local(): parts = lax.all_to_all(parts, AXES, 0, 0, tiled=True)  7.98 us
    all_to_all x1, starting transfers between devices, fast_local(): parts = lax.all_to_all(parts, AXES, 0, 0, tiled=True)  5.94 us
    pallas_call x1, Pallas kernels, local_part(): pl.pallas_call(local_kernel, out_shape=jax.ShapeDtypeStruct((size_x * hal...  5.9 us
    ppermute x1, waiting for transfers between devices, fast_local(): yb = lax.ppermute(face_b, 'gy', pairs_b)  4.29 us
    ppermute x1, starting transfers between devices, fast_local(): yb = lax.ppermute(face_b, 'gy', pairs_b)  3.38 us
    pallas_call x1, Pallas kernels, solve(): pl.pallas_call(functools.partial(solve_kernel, devices, own, block), out_...  3.09 us
  transfers between devices with their start and end apart: 9, of which 5 were waited for; matrix products, arithmetic and copies ran while one was open for 0% of the time, Pallas kernels for 19%

profile of v8, /device:TPU:1, one launch (start us, length us, event | category | flops | bytes accessed | tf_op | source)
XLA Modules:
  0.0 65.5 jit_solution(18401124000470852529)
XLA Ops:
  0.6 0.0 copy-start
  0.6 1.2 %copy-done = f32[16,16,1024]{2,1,0:T(8,128)S(1)} copy-done((f32[16,16,1024]{2,1,0:T(8,128)S(1)}, f32[16,16,1024]{2,1,0:T(8,128)}, u32[]{:S(2)}) %copy-start) | copy-done | bytes 1048600
  1.9 2.6 %share.1.sent_any = f32[512,128]{1,0:T(8,128)} custom-call(f32[16,16,1024]{2,1,0:T(8,128)S(1)} %copy-done), custom_call_target="tpu_custom_call" | custom-call | flops 20000000 | bytes 2000000 | tf_op jit(solution)/shard_map/share/pallas_call | solution.py:279
  4.5 7.1 %all-to-all-start = ((f32[32,16,128]{2,1,0:T(8,128)}), f32[32,16,128]{2,1,0:T(8,128)S(1)}, u32[]{:S(2)}, u32[]{:S(2)}) async-start(f32[32,16,128]{2,1,0:T(8,128)} %bitcast), calls=%async_computation | async-start | bytes 524288 | tf_op jit(solution)/shard_map/all_to_all | solution.py:961
  11.6 0.1 slice_select_fusion
  11.7 1.4 %collective-permute-start = (f32[16,16,256]{2,1,0:T(8,128)S(1)}, f32[16,16,256]{2,1,0:T(8,128)S(1)}, u32[]{:S(2)}, u32[]{:S(2)}) collective-permute-start(f32[16,16,256]{2,1,0:T(8,128)S(1)} %get-tuple-element.9), channel_id=1, source_target_pairs={{0,1},{1,0},{2,3},{3,2},{4,5},{5,4},{6,7},{7,6},{8,9},{9,8},{10,11... | collective-permute-start | bytes 786440 | tf_op jit(solution)/shard_map/ppermute | solution.py:976
  13.1 0.7 %collective-permute-start.1 = (f32[16,16,256]{2,1,0:T(8,128)S(1)}, f32[16,16,256]{2,1,0:T(8,128)S(1)}, u32[]{:S(2)}, u32[]{:S(2)}) collective-permute-start(f32[16,16,256]{2,1,0:T(8,128)S(1)} %get-tuple-element.8), channel_id=1, source_target_pairs={{1,2},{2,1},{5,6},{6,5},{9,10},{10,9},{13,14},{14,13},{17,18},{18,... | collective-permute-start | bytes 786440 | tf_op jit(solution)/shard_map/ppermute | solution.py:975
  13.8 8.0 %all-to-all-done = f32[32,16,128]{2,1,0:T(8,128)S(1)} async-done(((f32[32,16,128]{2,1,0:T(8,128)}), f32[32,16,128]{2,1,0:T(8,128)S(1)}, u32[]{:S(2)}, u32[]{:S(2)}) %all-to-all-start) | async-done | bytes 262176 | tf_op jit(solution)/shard_map/all_to_all | solution.py:961
  21.8 3.1 %solve.1 = f32[512,128]{1,0:T(8,128)} custom-call(f32[512,128]{1,0:T(8,128)S(1)} %bitcast.6, f32[256,256]{1,0:T(8,128)} %constant.20.clone.dense_any), custom_call_target="tpu_custom_call" | custom-call | flops 20000000 | bytes 2000000 | tf_op jit(solution)/shard_map/solve/pallas_call | solution.py:542
  24.9 2.8 %all-to-all-start.1 = ((f32[32,16,128]{2,1,0:T(8,128)}), f32[32,16,128]{2,1,0:T(8,128)S(1)}, u32[]{:S(2)}, u32[]{:S(2)}) async-start(f32[32,16,128]{2,1,0:T(8,128)} %bitcast.2), calls=%async_computation.1 | async-start | bytes 524288 | tf_op jit(solution)/shard_map/all_to_all | solution.py:961
  27.7 0.8 %faces.1 = (f32[16,32,128]{2,1,0:T(8,128)S(1)}, f32[16,32,128]{2,1,0:T(8,128)S(1)}, f32[480,128]{1,0:T(8,128)S(1)}) custom-call(f32[16,16,1024]{2,1,0:T(8,128)S(1)} %copy-done.1, f32[16,16,256]{2,1,0:T(8,128)S(1)} %collective-permute-done.za_ref, f32[16,16,256]{2,1,0:T(8,128)S(1)} %collective-permute-done.1.zb_ref), custom_call_target="tpu_custom_call" | custom-call | flops 8000000 | bytes 2000000 | tf_op jit(solution)/shard_map/faces/pallas_call | solution.py:627
  28.5 0.3 collective-permute-start.2
  28.9 3.4 %collective-permute-start.3 = (f32[16,32,128]{2,1,0:T(8,128)S(1)}, f32[16,32,128]{2,1,0:T(8,128)S(1)}, u32[]{:S(2)}, u32[]{:S(2)}) collective-permute-start(f32[16,32,128]{2,1,0:T(8,128)S(1)} %get-tuple-element.6), channel_id=1, source_target_pairs={{4,8},{8,4},{5,9},{9,5},{6,10},{10,6},{7,11},{11,7},{20,24},{24,20... | collective-permute-start | bytes 786440 | tf_op jit(solution)/shard_map/ppermute | solution.py:982
  32.2 1.2 %collective-permute-start.4 = (f32[480,128]{1,0:T(8,128)S(1)}, f32[480,128]{1,0:T(8,128)S(1)}, u32[]{:S(2)}, u32[]{:S(2)}) collective-permute-start(f32[480,128]{1,0:T(8,128)S(1)} %get-tuple-element.7), channel_id=1, source_target_pairs={{0,16},{16,0},{1,17},{17,1},{2,18},{18,2},{3,19},{19,3},{4,20},{20... | collective-permute-start | bytes 737288 | tf_op jit(solution)/shard_map/ppermute | solution.py:983
  33.5 4.3 %collective-permute-done.3.yb_ref = f32[16,32,128]{2,1,0:T(8,128)S(1)} collective-permute-done((f32[16,32,128]{2,1,0:T(8,128)S(1)}, f32[16,32,128]{2,1,0:T(8,128)S(1)}, u32[]{:S(2)}, u32[]{:S(2)}) %collective-permute-start.3) | collective-permute-done | bytes 262176 | tf_op jit(solution)/shard_map/ppermute | solution.py:982
  37.8 1.5 %collective-permute-start.5 = (f32[4,24,128]{2,1,0:T(8,128)S(1)}, f32[4,24,128]{2,1,0:T(8,128)S(1)}, u32[]{:S(2)}, u32[]{:S(2)}) collective-permute-start(f32[4,24,128]{2,1,0:T(8,128)S(1)} %edges.1), channel_id=1, source_target_pairs={{0,16},{16,0},{1,17},{17,1},{2,18},{18,2},{3,19},{19,3},{4,20},{20... | collective-permute-start | bytes 147464 | tf_op jit(solution)/shard_map/ppermute | solution.py:987
  39.3 0.6 collective-permute-done.4.x_ref
  39.9 0.9 %collective-permute-done.5.edge_ref = f32[4,24,128]{2,1,0:T(8,128)S(1)} collective-permute-done((f32[4,24,128]{2,1,0:T(8,128)S(1)}, f32[4,24,128]{2,1,0:T(8,128)S(1)}, u32[]{:S(2)}, u32[]{:S(2)}) %collective-permute-start.5) | collective-permute-done | bytes 49184 | tf_op jit(solution)/shard_map/ppermute | solution.py:987
  40.8 5.9 %local_part.1.psi_ref.local_ref = f32[2688,128]{1,0:T(8,128)S(1)} custom-call(f32[16,16,1024]{2,1,0:T(8,128)} %rho_any.1, f32[512,128]{1,0:T(8,128)} %share.1.sent_any, f32[16,16,256]{2,1,0:T(8,128)S(1)} %collective-permute-done.za_ref, f32[16,16,256]{2,1,0:T(8,128)S(1)} %collective-permute-done.1.zb_ref, f32[16,32,128]{2,1,0:T(8,128)S(1)} %collective-permute-done.2.ya_ref, ...), custom_call_target="tpu_custom_call" | custom-call | flops 30000000 | bytes 4000000 | tf_op jit(solution)/shard_map/local_part/pallas_call | solution.py:772
  46.7 1.4 %gram.1 = f32[32,1,2176]{2,1,0:T(1,128)} custom-call(f32[512,128]{1,0:T(8,128)S(1)} %bitcast.4, f32[2688,128]{1,0:T(8,128)S(1)} %local_part.1.psi_ref.local_ref), custom_call_target="tpu_custom_call" | custom-call | tf_op jit(solution)/shard_map/gram/pallas_call | solution.py:821
  48.1 5.9 %all-to-all-start.2 = ((f32[32,1,2176]{2,1,0:T(1,128)}), f32[32,1,2176]{2,1,0:T(1,128)S(1)}, u32[]{:S(2)}, u32[]{:S(2)}) async-start(f32[32,1,2176]{2,1,0:T(1,128)} %gram.1), calls=%async_computation.2 | async-start | bytes 557056 | tf_op jit(solution)/shard_map/all_to_all | solution.py:990
  54.0 2.7 %correct.1 = f32[16,16,1024]{2,1,0:T(8,128)} custom-call(f32[512,128]{1,0:T(8,128)S(1)} %bitcast.5, f32[2688,128]{1,0:T(8,128)S(1)} %local_part.1.psi_ref.local_ref), custom_call_target="tpu_custom_call" | custom-call | flops 20000000 | bytes 2000000 | tf_op jit(solution)/shard_map/correct/pallas_call | solution.py:900
  56.7 8.0 %all-to-all-done.2.in_ref = f32[32,1,2176]{2,1,0:T(1,128)S(1)} async-done(((f32[32,1,2176]{2,1,0:T(1,128)}), f32[32,1,2176]{2,1,0:T(1,128)S(1)}, u32[]{:S(2)}, u32[]{:S(2)}) %all-to-all-start.2) | async-done | bytes 278560 | tf_op jit(solution)/shard_map/all_to_all | solution.py:990
  64.7 0.8 %total.1 = f32[64,64]{1,0:T(8,128)} custom-call(f32[32,1,2176]{2,1,0:T(1,128)S(1)} %all-to-all-done.2.in_ref), custom_call_target="tpu_custom_call" | custom-call | tf_op jit(solution)/shard_map/total/pallas_call | solution.py:940
  (7 shorter events, 0.0 us)
Async XLA Ops:
  0.6 1.2 %copy-start = (f32[16,16,1024]{2,1,0:T(8,128)S(1)}, f32[16,16,1024]{2,1,0:T(8,128)}, u32[]{:S(2)}) copy-start(f32[16,16,1024]{2,1,0:T(8,128)} %rho_any.1) | copy-start | bytes 3145732
  1.9 9.7 %copy-start.1 = (f32[16,16,1024]{2,1,0:T(8,128)S(1)}, f32[16,16,1024]{2,1,0:T(8,128)}, u32[]{:S(2)}) copy-start(f32[16,16,1024]{2,1,0:T(8,128)} %rho_any.1) | copy-start | bytes 3145732
  4.5 17.3 %all-to-all-start = ((f32[32,16,128]{2,1,0:T(8,128)}), f32[32,16,128]{2,1,0:T(8,128)S(1)}, u32[]{:S(2)}, u32[]{:S(2)}) async-start(f32[32,16,128]{2,1,0:T(8,128)} %bitcast), calls=%async_computation | async-start | bytes 524288 | tf_op jit(solution)/shard_map/all_to_all | solution.py:961
  11.7 16.0 %collective-permute-start = (f32[16,16,256]{2,1,0:T(8,128)S(1)}, f32[16,16,256]{2,1,0:T(8,128)S(1)}, u32[]{:S(2)}, u32[]{:S(2)}) collective-permute-start(f32[16,16,256]{2,1,0:T(8,128)S(1)} %get-tuple-element.9), channel_id=1, source_target_pairs={{0,1},{1,0},{2,3},{3,2},{4,5},{5,4},{6,7},{7,6},{8,9},{9,8},{10,11... | collective-permute-start | bytes 786440 | tf_op jit(solution)/shard_map/ppermute | solution.py:976
  13.1 14.6 %collective-permute-start.1 = (f32[16,16,256]{2,1,0:T(8,128)S(1)}, f32[16,16,256]{2,1,0:T(8,128)S(1)}, u32[]{:S(2)}, u32[]{:S(2)}) collective-permute-start(f32[16,16,256]{2,1,0:T(8,128)S(1)} %get-tuple-element.8), channel_id=1, source_target_pairs={{1,2},{2,1},{5,6},{6,5},{9,10},{10,9},{13,14},{14,13},{17,18},{18,... | collective-permute-start | bytes 786440 | tf_op jit(solution)/shard_map/ppermute | solution.py:975
  24.9 21.8 %all-to-all-start.1 = ((f32[32,16,128]{2,1,0:T(8,128)}), f32[32,16,128]{2,1,0:T(8,128)S(1)}, u32[]{:S(2)}, u32[]{:S(2)}) async-start(f32[32,16,128]{2,1,0:T(8,128)} %bitcast.2), calls=%async_computation.1 | async-start | bytes 524288 | tf_op jit(solution)/shard_map/all_to_all | solution.py:961
  28.5 5.0 %collective-permute-start.2 = (f32[16,32,128]{2,1,0:T(8,128)S(1)}, f32[16,32,128]{2,1,0:T(8,128)S(1)}, u32[]{:S(2)}, u32[]{:S(2)}) collective-permute-start(f32[16,32,128]{2,1,0:T(8,128)S(1)} %get-tuple-element.5), channel_id=1, source_target_pairs={{0,4},{4,0},{8,12},{12,8},{1,5},{5,1},{9,13},{13,9},{2,6},{6,2},{1... | collective-permute-start | bytes 786440 | tf_op jit(solution)/shard_map/ppermute | solution.py:981
  28.9 8.9 %collective-permute-start.3 = (f32[16,32,128]{2,1,0:T(8,128)S(1)}, f32[16,32,128]{2,1,0:T(8,128)S(1)}, u32[]{:S(2)}, u32[]{:S(2)}) collective-permute-start(f32[16,32,128]{2,1,0:T(8,128)S(1)} %get-tuple-element.6), channel_id=1, source_target_pairs={{4,8},{8,4},{5,9},{9,5},{6,10},{10,6},{7,11},{11,7},{20,24},{24,20... | collective-permute-start | bytes 786440 | tf_op jit(solution)/shard_map/ppermute | solution.py:982
  32.2 7.7 %collective-permute-start.4 = (f32[480,128]{1,0:T(8,128)S(1)}, f32[480,128]{1,0:T(8,128)S(1)}, u32[]{:S(2)}, u32[]{:S(2)}) collective-permute-start(f32[480,128]{1,0:T(8,128)S(1)} %get-tuple-element.7), channel_id=1, source_target_pairs={{0,16},{16,0},{1,17},{17,1},{2,18},{18,2},{3,19},{19,3},{4,20},{20... | collective-permute-start | bytes 737288 | tf_op jit(solution)/shard_map/ppermute | solution.py:983
  37.8 3.0 %collective-permute-start.5 = (f32[4,24,128]{2,1,0:T(8,128)S(1)}, f32[4,24,128]{2,1,0:T(8,128)S(1)}, u32[]{:S(2)}, u32[]{:S(2)}) collective-permute-start(f32[4,24,128]{2,1,0:T(8,128)S(1)} %edges.1), channel_id=1, source_target_pairs={{0,16},{16,0},{1,17},{17,1},{2,18},{18,2},{3,19},{19,3},{4,20},{20... | collective-permute-start | bytes 147464 | tf_op jit(solution)/shard_map/ppermute | solution.py:987
  48.1 16.6 %all-to-all-start.2 = ((f32[32,1,2176]{2,1,0:T(1,128)}), f32[32,1,2176]{2,1,0:T(1,128)S(1)}, u32[]{:S(2)}, u32[]{:S(2)}) async-start(f32[32,1,2176]{2,1,0:T(1,128)} %gram.1), calls=%async_computation.2 | async-start | bytes 557056 | tf_op jit(solution)/shard_map/all_to_all | solution.py:990

commit v9 on v8

--- a/solution.py
+++ b/solution.py
@@ -174,7 +174,7 @@
                     value = inside(around + (beside + along_x), mask, j, half, z_first, z_last)
                     t_ref[pl.ds(t_row(at, j, y), 8), :] = value
 
-    loop(size_x // 2, smooth)
+    loop(size_x // 2, smooth, 2)
     for x, near in ((-1, 0), (size_x, size_x - 1)):
         scale = plane_scale(flags, x, size_x)
         for i in range(3):
@@ -219,7 +219,7 @@
                 q_ref[pl.ds(at, 8), :] = w * (RATIO + 3.0) + f
 
     coarsen(0, (-1,), (0,))
-    loop(size_x // 2, lambda i: coarsen(i + 1, (2 * i, 2 * i + 1), (2 * i - 1, 2 * i + 2)))
+    loop(size_x // 2, lambda i: coarsen(i + 1, (2 * i, 2 * i + 1), (2 * i - 1, 2 * i + 2)), 2)
     coarsen(coarse_x - 1, (size_x,), (size_x - 1,))
 
     def along_y(step):
@@ -231,7 +231,7 @@
                 value = value + (a_ref[pl.ds(base, count, stride=2), :] + a_ref[pl.ds(base + 3, count, stride=2), :])
                 c_ref[pl.ds((step * coarse_k + k) * coarse_y + start, count), :] = value * (SIDE / 8.0)
 
-    loop(coarse_x, along_y, 2)
+    loop(coarse_x, along_y, 5)
     used = coarse_x * coarse_k * coarse_y
     c_ref[pl.ds(used, c_ref.shape[0] - used), :] = jnp.zeros((c_ref.shape[0] - used, LANES), jnp.float32)
     to_messages(c_ref, out_ref)
@@ -978,8 +978,8 @@
     received = exchanged(messages)
     face_a, face_b, plane = faces(density, za, zb)
     pairs_a, pairs_b = swaps("gy")
+    yb = lax.ppermute(face_b, "gy", pairs_b)
     ya = lax.ppermute(face_a, "gy", pairs_a)
-    yb = lax.ppermute(face_b, "gy", pairs_b)
     beside = lax.ppermute(plane, "gx", swapped)
     answers = solve(received, devices, block, LEVELS - 1)
     correction = exchanged(answers)

time: 66 us -> 66 us (level)
  no operation moved by 1% of the time
where the time goes in v9:
time: 66 us; the launch traced here: 65.5 us
  starting transfers between devices  24.3 us (37%)
  waiting for transfers between devices  21.8 us (33%)
  Pallas kernels  17.3 us (26%)
  local copies, waits for them, and re-layouts  1.22 us (2%)
  between operations  0.76 us (1%)
    all_to_all x2, starting transfers between devices, exchanged(): lax.all_to_all(shaped, axes, 0, 0, tiled=True).reshape(messages.shape)  9.85 us
    all_to_all x2, waiting for transfers between devices, exchanged(): lax.all_to_all(shaped, axes, 0, 0, tiled=True).reshape(messages.shape)  8.04 us
    all_to_all x1, waiting for transfers between devices, fast_local(): parts = lax.all_to_all(parts, AXES, 0, 0, tiled=True)  7.98 us
    all_to_all x1, starting transfers between devices, fast_local(): parts = lax.all_to_all(parts, AXES, 0, 0, tiled=True)  5.94 us
    pallas_call x1, Pallas kernels, local_part(): pl.pallas_call(local_kernel, out_shape=jax.ShapeDtypeStruct((size_x * hal...  5.9 us
    ppermute x1, waiting for transfers between devices, fast_local(): yb = lax.ppermute(face_b, 'gy', pairs_b)  4.29 us
    ppermute x1, starting transfers between devices, fast_local(): yb = lax.ppermute(face_b, 'gy', pairs_b)  3.38 us
    pallas_call x1, Pallas kernels, solve(): pl.pallas_call(functools.partial(solve_kernel, devices, own, block), out_...  3.09 us
  transfers between devices with their start and end apart: 9, of which 5 were waited for; matrix products, arithmetic and copies ran while one was open for 0% of the time, Pallas kernels for 19%

profile of v9, /device:TPU:1, one launch (start us, length us, event | category | flops | bytes accessed | tf_op | source)
XLA Modules:
  0.0 65.5 jit_solution(8427062614571129301)
XLA Ops:
  0.6 0.0 copy-start
  0.6 1.2 %copy-done = f32[16,16,1024]{2,1,0:T(8,128)S(1)} copy-done((f32[16,16,1024]{2,1,0:T(8,128)S(1)}, f32[16,16,1024]{2,1,0:T(8,128)}, u32[]{:S(2)}) %copy-start) | copy-done | bytes 1048600
  1.9 2.6 %share.1.sent_any = f32[512,128]{1,0:T(8,128)} custom-call(f32[16,16,1024]{2,1,0:T(8,128)S(1)} %copy-done), custom_call_target="tpu_custom_call" | custom-call | flops 20000000 | bytes 2000000 | tf_op jit(solution)/shard_map/share/pallas_call | solution.py:279
  4.4 7.1 %all-to-all-start = ((f32[32,16,128]{2,1,0:T(8,128)}), f32[32,16,128]{2,1,0:T(8,128)S(1)}, u32[]{:S(2)}, u32[]{:S(2)}) async-start(f32[32,16,128]{2,1,0:T(8,128)} %bitcast), calls=%async_computation | async-start | bytes 524288 | tf_op jit(solution)/shard_map/all_to_all | solution.py:961
  11.5 0.1 slice_select_fusion
  11.6 1.4 %collective-permute-start = (f32[16,16,256]{2,1,0:T(8,128)S(1)}, f32[16,16,256]{2,1,0:T(8,128)S(1)}, u32[]{:S(2)}, u32[]{:S(2)}) collective-permute-start(f32[16,16,256]{2,1,0:T(8,128)S(1)} %get-tuple-element.9), channel_id=1, source_target_pairs={{0,1},{1,0},{2,3},{3,2},{4,5},{5,4},{6,7},{7,6},{8,9},{9,8},{10,11... | collective-permute-start | bytes 786440 | tf_op jit(solution)/shard_map/ppermute | solution.py:976
  13.0 0.7 %collective-permute-start.1 = (f32[16,16,256]{2,1,0:T(8,128)S(1)}, f32[16,16,256]{2,1,0:T(8,128)S(1)}, u32[]{:S(2)}, u32[]{:S(2)}) collective-permute-start(f32[16,16,256]{2,1,0:T(8,128)S(1)} %get-tuple-element.8), channel_id=1, source_target_pairs={{1,2},{2,1},{5,6},{6,5},{9,10},{10,9},{13,14},{14,13},{17,18},{18,... | collective-permute-start | bytes 786440 | tf_op jit(solution)/shard_map/ppermute | solution.py:975
  13.7 8.0 %all-to-all-done = f32[32,16,128]{2,1,0:T(8,128)S(1)} async-done(((f32[32,16,128]{2,1,0:T(8,128)}), f32[32,16,128]{2,1,0:T(8,128)S(1)}, u32[]{:S(2)}, u32[]{:S(2)}) %all-to-all-start) | async-done | bytes 262176 | tf_op jit(solution)/shard_map/all_to_all | solution.py:961
  21.7 3.1 %solve.1 = f32[512,128]{1,0:T(8,128)} custom-call(f32[512,128]{1,0:T(8,128)S(1)} %bitcast.6, f32[256,256]{1,0:T(8,128)} %constant.20.clone.dense_any), custom_call_target="tpu_custom_call" | custom-call | flops 20000000 | bytes 2000000 | tf_op jit(solution)/shard_map/solve/pallas_call | solution.py:542
  24.8 2.8 %all-to-all-start.1 = ((f32[32,16,128]{2,1,0:T(8,128)}), f32[32,16,128]{2,1,0:T(8,128)S(1)}, u32[]{:S(2)}, u32[]{:S(2)}) async-start(f32[32,16,128]{2,1,0:T(8,128)} %bitcast.2), calls=%async_computation.1 | async-start | bytes 524288 | tf_op jit(solution)/shard_map/all_to_all | solution.py:961
  27.6 0.8 %faces.1 = (f32[16,32,128]{2,1,0:T(8,128)S(1)}, f32[16,32,128]{2,1,0:T(8,128)S(1)}, f32[480,128]{1,0:T(8,128)S(1)}) custom-call(f32[16,16,1024]{2,1,0:T(8,128)S(1)} %copy-done.1, f32[16,16,256]{2,1,0:T(8,128)S(1)} %collective-permute-done.za_ref, f32[16,16,256]{2,1,0:T(8,128)S(1)} %collective-permute-done.1.zb_ref), custom_call_target="tpu_custom_call" | custom-call | flops 8000000 | bytes 2000000 | tf_op jit(solution)/shard_map/faces/pallas_call | solution.py:627
  28.5 0.3 collective-permute-start.2
  28.8 3.4 %collective-permute-start.3 = (f32[16,32,128]{2,1,0:T(8,128)S(1)}, f32[16,32,128]{2,1,0:T(8,128)S(1)}, u32[]{:S(2)}, u32[]{:S(2)}) collective-permute-start(f32[16,32,128]{2,1,0:T(8,128)S(1)} %get-tuple-element.6), channel_id=1, source_target_pairs={{4,8},{8,4},{5,9},{9,5},{6,10},{10,6},{7,11},{11,7},{20,24},{24,20... | collective-permute-start | bytes 786440 | tf_op jit(solution)/shard_map/ppermute | solution.py:981
  32.2 1.2 %collective-permute-start.4 = (f32[480,128]{1,0:T(8,128)S(1)}, f32[480,128]{1,0:T(8,128)S(1)}, u32[]{:S(2)}, u32[]{:S(2)}) collective-permute-start(f32[480,128]{1,0:T(8,128)S(1)} %get-tuple-element.7), channel_id=1, source_target_pairs={{0,16},{16,0},{1,17},{17,1},{2,18},{18,2},{3,19},{19,3},{4,20},{20... | collective-permute-start | bytes 737288 | tf_op jit(solution)/shard_map/ppermute | solution.py:983
  33.4 4.3 %collective-permute-done.3.yb_ref = f32[16,32,128]{2,1,0:T(8,128)S(1)} collective-permute-done((f32[16,32,128]{2,1,0:T(8,128)S(1)}, f32[16,32,128]{2,1,0:T(8,128)S(1)}, u32[]{:S(2)}, u32[]{:S(2)}) %collective-permute-start.3) | collective-permute-done | bytes 262176 | tf_op jit(solution)/shard_map/ppermute | solution.py:981
  37.7 1.5 %collective-permute-start.5 = (f32[4,24,128]{2,1,0:T(8,128)S(1)}, f32[4,24,128]{2,1,0:T(8,128)S(1)}, u32[]{:S(2)}, u32[]{:S(2)}) collective-permute-start(f32[4,24,128]{2,1,0:T(8,128)S(1)} %edges.1), channel_id=1, source_target_pairs={{0,16},{16,0},{1,17},{17,1},{2,18},{18,2},{3,19},{19,3},{4,20},{20... | collective-permute-start | bytes 147464 | tf_op jit(solution)/shard_map/ppermute | solution.py:987
  39.2 0.6 collective-permute-done.4.x_ref
  39.8 0.9 %collective-permute-done.5.edge_ref = f32[4,24,128]{2,1,0:T(8,128)S(1)} collective-permute-done((f32[4,24,128]{2,1,0:T(8,128)S(1)}, f32[4,24,128]{2,1,0:T(8,128)S(1)}, u32[]{:S(2)}, u32[]{:S(2)}) %collective-permute-start.5) | collective-permute-done | bytes 49184 | tf_op jit(solution)/shard_map/ppermute | solution.py:987
  40.7 5.9 %local_part.1.psi_ref.local_ref = f32[2688,128]{1,0:T(8,128)S(1)} custom-call(f32[16,16,1024]{2,1,0:T(8,128)} %rho_any.1, f32[512,128]{1,0:T(8,128)} %share.1.sent_any, f32[16,16,256]{2,1,0:T(8,128)S(1)} %collective-permute-done.za_ref, f32[16,16,256]{2,1,0:T(8,128)S(1)} %collective-permute-done.1.zb_ref, f32[16,32,128]{2,1,0:T(8,128)S(1)} %collective-permute-done.2.ya_ref, ...), custom_call_target="tpu_custom_call" | custom-call | flops 30000000 | bytes 4000000 | tf_op jit(solution)/shard_map/local_part/pallas_call | solution.py:772
  46.7 1.4 %gram.1 = f32[32,1,2176]{2,1,0:T(1,128)} custom-call(f32[512,128]{1,0:T(8,128)S(1)} %bitcast.4, f32[2688,128]{1,0:T(8,128)S(1)} %local_part.1.psi_ref.local_ref), custom_call_target="tpu_custom_call" | custom-call | tf_op jit(solution)/shard_map/gram/pallas_call | solution.py:821
  48.0 5.9 %all-to-all-start.2 = ((f32[32,1,2176]{2,1,0:T(1,128)}), f32[32,1,2176]{2,1,0:T(1,128)S(1)}, u32[]{:S(2)}, u32[]{:S(2)}) async-start(f32[32,1,2176]{2,1,0:T(1,128)} %gram.1), calls=%async_computation.2 | async-start | bytes 557056 | tf_op jit(solution)/shard_map/all_to_all | solution.py:990
  54.0 2.7 %correct.1 = f32[16,16,1024]{2,1,0:T(8,128)} custom-call(f32[512,128]{1,0:T(8,128)S(1)} %bitcast.5, f32[2688,128]{1,0:T(8,128)S(1)} %local_part.1.psi_ref.local_ref), custom_call_target="tpu_custom_call" | custom-call | flops 20000000 | bytes 2000000 | tf_op jit(solution)/shard_map/correct/pallas_call | solution.py:900
  56.6 8.0 %all-to-all-done.2.in_ref = f32[32,1,2176]{2,1,0:T(1,128)S(1)} async-done(((f32[32,1,2176]{2,1,0:T(1,128)}), f32[32,1,2176]{2,1,0:T(1,128)S(1)}, u32[]{:S(2)}, u32[]{:S(2)}) %all-to-all-start.2) | async-done | bytes 278560 | tf_op jit(solution)/shard_map/all_to_all | solution.py:990
  64.6 0.8 %total.1 = f32[64,64]{1,0:T(8,128)} custom-call(f32[32,1,2176]{2,1,0:T(1,128)S(1)} %all-to-all-done.2.in_ref), custom_call_target="tpu_custom_call" | custom-call | tf_op jit(solution)/shard_map/total/pallas_call | solution.py:940
  (7 shorter events, 0.0 us)
Async XLA Ops:
  0.6 1.2 %copy-start = (f32[16,16,1024]{2,1,0:T(8,128)S(1)}, f32[16,16,1024]{2,1,0:T(8,128)}, u32[]{:S(2)}) copy-start(f32[16,16,1024]{2,1,0:T(8,128)} %rho_any.1) | copy-start | bytes 3145732
  1.9 9.7 %copy-start.1 = (f32[16,16,1024]{2,1,0:T(8,128)S(1)}, f32[16,16,1024]{2,1,0:T(8,128)}, u32[]{:S(2)}) copy-start(f32[16,16,1024]{2,1,0:T(8,128)} %rho_any.1) | copy-start | bytes 3145732
  4.4 17.3 %all-to-all-start = ((f32[32,16,128]{2,1,0:T(8,128)}), f32[32,16,128]{2,1,0:T(8,128)S(1)}, u32[]{:S(2)}, u32[]{:S(2)}) async-start(f32[32,16,128]{2,1,0:T(8,128)} %bitcast), calls=%async_computation | async-start | bytes 524288 | tf_op jit(solution)/shard_map/all_to_all | solution.py:961
  11.6 16.0 %collective-permute-start = (f32[16,16,256]{2,1,0:T(8,128)S(1)}, f32[16,16,256]{2,1,0:T(8,128)S(1)}, u32[]{:S(2)}, u32[]{:S(2)}) collective-permute-start(f32[16,16,256]{2,1,0:T(8,128)S(1)} %get-tuple-element.9), channel_id=1, source_target_pairs={{0,1},{1,0},{2,3},{3,2},{4,5},{5,4},{6,7},{7,6},{8,9},{9,8},{10,11... | collective-permute-start | bytes 786440 | tf_op jit(solution)/shard_map/ppermute | solution.py:976
  13.0 14.6 %collective-permute-start.1 = (f32[16,16,256]{2,1,0:T(8,128)S(1)}, f32[16,16,256]{2,1,0:T(8,128)S(1)}, u32[]{:S(2)}, u32[]{:S(2)}) collective-permute-start(f32[16,16,256]{2,1,0:T(8,128)S(1)} %get-tuple-element.8), channel_id=1, source_target_pairs={{1,2},{2,1},{5,6},{6,5},{9,10},{10,9},{13,14},{14,13},{17,18},{18,... | collective-permute-start | bytes 786440 | tf_op jit(solution)/shard_map/ppermute | solution.py:975
  24.8 21.8 %all-to-all-start.1 = ((f32[32,16,128]{2,1,0:T(8,128)}), f32[32,16,128]{2,1,0:T(8,128)S(1)}, u32[]{:S(2)}, u32[]{:S(2)}) async-start(f32[32,16,128]{2,1,0:T(8,128)} %bitcast.2), calls=%async_computation.1 | async-start | bytes 524288 | tf_op jit(solution)/shard_map/all_to_all | solution.py:961
  28.5 5.0 %collective-permute-start.2 = (f32[16,32,128]{2,1,0:T(8,128)S(1)}, f32[16,32,128]{2,1,0:T(8,128)S(1)}, u32[]{:S(2)}, u32[]{:S(2)}) collective-permute-start(f32[16,32,128]{2,1,0:T(8,128)S(1)} %get-tuple-element.5), channel_id=1, source_target_pairs={{0,4},{4,0},{8,12},{12,8},{1,5},{5,1},{9,13},{13,9},{2,6},{6,2},{1... | collective-permute-start | bytes 786440 | tf_op jit(solution)/shard_map/ppermute | solution.py:982
  28.8 8.9 %collective-permute-start.3 = (f32[16,32,128]{2,1,0:T(8,128)S(1)}, f32[16,32,128]{2,1,0:T(8,128)S(1)}, u32[]{:S(2)}, u32[]{:S(2)}) collective-permute-start(f32[16,32,128]{2,1,0:T(8,128)S(1)} %get-tuple-element.6), channel_id=1, source_target_pairs={{4,8},{8,4},{5,9},{9,5},{6,10},{10,6},{7,11},{11,7},{20,24},{24,20... | collective-permute-start | bytes 786440 | tf_op jit(solution)/shard_map/ppermute | solution.py:981
  32.2 7.7 %collective-permute-start.4 = (f32[480,128]{1,0:T(8,128)S(1)}, f32[480,128]{1,0:T(8,128)S(1)}, u32[]{:S(2)}, u32[]{:S(2)}) collective-permute-start(f32[480,128]{1,0:T(8,128)S(1)} %get-tuple-element.7), channel_id=1, source_target_pairs={{0,16},{16,0},{1,17},{17,1},{2,18},{18,2},{3,19},{19,3},{4,20},{20... | collective-permute-start | bytes 737288 | tf_op jit(solution)/shard_map/ppermute | solution.py:983
  37.7 3.0 %collective-permute-start.5 = (f32[4,24,128]{2,1,0:T(8,128)S(1)}, f32[4,24,128]{2,1,0:T(8,128)S(1)}, u32[]{:S(2)}, u32[]{:S(2)}) collective-permute-start(f32[4,24,128]{2,1,0:T(8,128)S(1)} %edges.1), channel_id=1, source_target_pairs={{0,16},{16,0},{1,17},{17,1},{2,18},{18,2},{3,19},{19,3},{4,20},{20... | collective-permute-start | bytes 147464 | tf_op jit(solution)/shard_map/ppermute | solution.py:987
  48.0 16.6 %all-to-all-start.2 = ((f32[32,1,2176]{2,1,0:T(1,128)}), f32[32,1,2176]{2,1,0:T(1,128)S(1)}, u32[]{:S(2)}, u32[]{:S(2)}) async-start(f32[32,1,2176]{2,1,0:T(1,128)} %gram.1), calls=%async_computation.2 | async-start | bytes 557056 | tf_op jit(solution)/shard_map/all_to_all | solution.py:990

commit v10 on v8

--- a/solution.py
+++ b/solution.py
@@ -914,12 +914,11 @@
 
 
 def total_kernel(scale, in_ref, out_ref):
-    copies, _, width = in_ref.shape
-    terms = [in_ref[i] for i in range(copies)]
-    while len(terms) > 1:
-        terms = [terms[i] + terms[i + 1] for i in range(0, len(terms) - 1, 2)] + terms[len(terms) & ~1 :]
-    line = terms[0] * scale
-    lines = [line[:, r * LANES : (r + 1) * LANES] for r in range(width // LANES)]
+    _, _, width = in_ref.shape
+    lines = []
+    for r in range(width // LANES):
+        column = in_ref[:, 0, pl.ds(r * LANES, LANES)]
+        lines.append(jnp.sum(column, axis=0, keepdims=True) * scale)
     flat = jnp.concatenate(lines[:-1], axis=0)
     diagonal = lines[-1]
     quarter = PAIRS // 2

time: 66 us -> 66.1 us (level)
  no operation moved by 1% of the time
where the time goes in v10:
time: 66.1 us; the launch traced here: 65.6 us
  starting transfers between devices  24.3 us (37%)
  waiting for transfers between devices  21.8 us (33%)
  Pallas kernels  17.4 us (26%)
  local copies, waits for them, and re-layouts  1.22 us (2%)
  between operations  0.76 us (1%)
    all_to_all x2, starting transfers between devices, exchanged(): lax.all_to_all(shaped, axes, 0, 0, tiled=True).reshape(messages.shape)  9.85 us
    all_to_all x2, waiting for transfers between devices, exchanged(): lax.all_to_all(shaped, axes, 0, 0, tiled=True).reshape(messages.shape)  8.04 us
    all_to_all x1, waiting for transfers between devices, fast_local(): parts = lax.all_to_all(parts, AXES, 0, 0, tiled=True)  7.98 us
    all_to_all x1, starting transfers between devices, fast_local(): parts = lax.all_to_all(parts, AXES, 0, 0, tiled=True)  5.94 us
    pallas_call x1, Pallas kernels, local_part(): pl.pallas_call(local_kernel, out_shape=jax.ShapeDtypeStruct((size_x * hal...  5.9 us
    ppermute x1, waiting for transfers between devices, fast_local(): yb = lax.ppermute(face_b, 'gy', pairs_b)  4.29 us
    ppermute x1, starting transfers between devices, fast_local(): yb = lax.ppermute(face_b, 'gy', pairs_b)  3.38 us
    pallas_call x1, Pallas kernels, solve(): pl.pallas_call(functools.partial(solve_kernel, devices, own, block), out_...  3.09 us
  transfers between devices with their start and end apart: 9, of which 5 were waited for; matrix products, arithmetic and copies ran while one was open for 0% of the time, Pallas kernels for 19%

profile of v10, /device:TPU:1, one launch (start us, length us, event | category | flops | bytes accessed | tf_op | source)
XLA Modules:
  0.0 65.6 jit_solution(1858559478348396872)
XLA Ops:
  0.6 0.0 copy-start
  0.6 1.2 %copy-done = f32[16,16,1024]{2,1,0:T(8,128)S(1)} copy-done((f32[16,16,1024]{2,1,0:T(8,128)S(1)}, f32[16,16,1024]{2,1,0:T(8,128)}, u32[]{:S(2)}) %copy-start) | copy-done | bytes 1048600
  1.9 2.6 %share.1.sent_any = f32[512,128]{1,0:T(8,128)} custom-call(f32[16,16,1024]{2,1,0:T(8,128)S(1)} %copy-done), custom_call_target="tpu_custom_call" | custom-call | flops 20000000 | bytes 2000000 | tf_op jit(solution)/shard_map/share/pallas_call | solution.py:279
  4.5 7.1 %all-to-all-start = ((f32[32,16,128]{2,1,0:T(8,128)}), f32[32,16,128]{2,1,0:T(8,128)S(1)}, u32[]{:S(2)}, u32[]{:S(2)}) async-start(f32[32,16,128]{2,1,0:T(8,128)} %bitcast), calls=%async_computation | async-start | bytes 524288 | tf_op jit(solution)/shard_map/all_to_all | solution.py:960
  11.6 0.1 slice_select_fusion
  11.7 1.4 %collective-permute-start = (f32[16,16,256]{2,1,0:T(8,128)S(1)}, f32[16,16,256]{2,1,0:T(8,128)S(1)}, u32[]{:S(2)}, u32[]{:S(2)}) collective-permute-start(f32[16,16,256]{2,1,0:T(8,128)S(1)} %get-tuple-element.9), channel_id=1, source_target_pairs={{0,1},{1,0},{2,3},{3,2},{4,5},{5,4},{6,7},{7,6},{8,9},{9,8},{10,11... | collective-permute-start | bytes 786440 | tf_op jit(solution)/shard_map/ppermute | solution.py:975
  13.1 0.7 %collective-permute-start.1 = (f32[16,16,256]{2,1,0:T(8,128)S(1)}, f32[16,16,256]{2,1,0:T(8,128)S(1)}, u32[]{:S(2)}, u32[]{:S(2)}) collective-permute-start(f32[16,16,256]{2,1,0:T(8,128)S(1)} %get-tuple-element.8), channel_id=1, source_target_pairs={{1,2},{2,1},{5,6},{6,5},{9,10},{10,9},{13,14},{14,13},{17,18},{18,... | collective-permute-start | bytes 786440 | tf_op jit(solution)/shard_map/ppermute | solution.py:974
  13.8 8.0 %all-to-all-done = f32[32,16,128]{2,1,0:T(8,128)S(1)} async-done(((f32[32,16,128]{2,1,0:T(8,128)}), f32[32,16,128]{2,1,0:T(8,128)S(1)}, u32[]{:S(2)}, u32[]{:S(2)}) %all-to-all-start) | async-done | bytes 262176 | tf_op jit(solution)/shard_map/all_to_all | solution.py:960
  21.8 3.1 %solve.1 = f32[512,128]{1,0:T(8,128)} custom-call(f32[512,128]{1,0:T(8,128)S(1)} %bitcast.6, f32[256,256]{1,0:T(8,128)} %constant.20.clone.dense_any), custom_call_target="tpu_custom_call" | custom-call | flops 20000000 | bytes 2000000 | tf_op jit(solution)/shard_map/solve/pallas_call | solution.py:542
  24.9 2.8 %all-to-all-start.1 = ((f32[32,16,128]{2,1,0:T(8,128)}), f32[32,16,128]{2,1,0:T(8,128)S(1)}, u32[]{:S(2)}, u32[]{:S(2)}) async-start(f32[32,16,128]{2,1,0:T(8,128)} %bitcast.2), calls=%async_computation.1 | async-start | bytes 524288 | tf_op jit(solution)/shard_map/all_to_all | solution.py:960
  27.7 0.8 %faces.1 = (f32[16,32,128]{2,1,0:T(8,128)S(1)}, f32[16,32,128]{2,1,0:T(8,128)S(1)}, f32[480,128]{1,0:T(8,128)S(1)}) custom-call(f32[16,16,1024]{2,1,0:T(8,128)S(1)} %copy-done.1, f32[16,16,256]{2,1,0:T(8,128)S(1)} %collective-permute-done.za_ref, f32[16,16,256]{2,1,0:T(8,128)S(1)} %collective-permute-done.1.zb_ref), custom_call_target="tpu_custom_call" | custom-call | flops 8000000 | bytes 2000000 | tf_op jit(solution)/shard_map/faces/pallas_call | solution.py:627
  28.5 0.3 collective-permute-start.2
  28.9 3.4 %collective-permute-start.3 = (f32[16,32,128]{2,1,0:T(8,128)S(1)}, f32[16,32,128]{2,1,0:T(8,128)S(1)}, u32[]{:S(2)}, u32[]{:S(2)}) collective-permute-start(f32[16,32,128]{2,1,0:T(8,128)S(1)} %get-tuple-element.6), channel_id=1, source_target_pairs={{4,8},{8,4},{5,9},{9,5},{6,10},{10,6},{7,11},{11,7},{20,24},{24,20... | collective-permute-start | bytes 786440 | tf_op jit(solution)/shard_map/ppermute | solution.py:981
  32.2 1.2 %collective-permute-start.4 = (f32[480,128]{1,0:T(8,128)S(1)}, f32[480,128]{1,0:T(8,128)S(1)}, u32[]{:S(2)}, u32[]{:S(2)}) collective-permute-start(f32[480,128]{1,0:T(8,128)S(1)} %get-tuple-element.7), channel_id=1, source_target_pairs={{0,16},{16,0},{1,17},{17,1},{2,18},{18,2},{3,19},{19,3},{4,20},{20... | collective-permute-start | bytes 737288 | tf_op jit(solution)/shard_map/ppermute | solution.py:982
  33.5 4.3 %collective-permute-done.3.yb_ref = f32[16,32,128]{2,1,0:T(8,128)S(1)} collective-permute-done((f32[16,32,128]{2,1,0:T(8,128)S(1)}, f32[16,32,128]{2,1,0:T(8,128)S(1)}, u32[]{:S(2)}, u32[]{:S(2)}) %collective-permute-start.3) | collective-permute-done | bytes 262176 | tf_op jit(solution)/shard_map/ppermute | solution.py:981
  37.8 1.5 %collective-permute-start.5 = (f32[4,24,128]{2,1,0:T(8,128)S(1)}, f32[4,24,128]{2,1,0:T(8,128)S(1)}, u32[]{:S(2)}, u32[]{:S(2)}) collective-permute-start(f32[4,24,128]{2,1,0:T(8,128)S(1)} %edges.1), channel_id=1, source_target_pairs={{0,16},{16,0},{1,17},{17,1},{2,18},{18,2},{3,19},{19,3},{4,20},{20... | collective-permute-start | bytes 147464 | tf_op jit(solution)/shard_map/ppermute | solution.py:986
  39.3 0.6 collective-permute-done.4.x_ref
  39.9 0.9 %collective-permute-done.5.edge_ref = f32[4,24,128]{2,1,0:T(8,128)S(1)} collective-permute-done((f32[4,24,128]{2,1,0:T(8,128)S(1)}, f32[4,24,128]{2,1,0:T(8,128)S(1)}, u32[]{:S(2)}, u32[]{:S(2)}) %collective-permute-start.5) | collective-permute-done | bytes 49184 | tf_op jit(solution)/shard_map/ppermute | solution.py:986
  40.8 5.9 %local_part.1.psi_ref.local_ref = f32[2688,128]{1,0:T(8,128)S(1)} custom-call(f32[16,16,1024]{2,1,0:T(8,128)} %rho_any.1, f32[512,128]{1,0:T(8,128)} %share.1.sent_any, f32[16,16,256]{2,1,0:T(8,128)S(1)} %collective-permute-done.za_ref, f32[16,16,256]{2,1,0:T(8,128)S(1)} %collective-permute-done.1.zb_ref, f32[16,32,128]{2,1,0:T(8,128)S(1)} %collective-permute-done.2.ya_ref, ...), custom_call_target="tpu_custom_call" | custom-call | flops 30000000 | bytes 4000000 | tf_op jit(solution)/shard_map/local_part/pallas_call | solution.py:772
  46.7 1.4 %gram.1 = f32[32,1,2176]{2,1,0:T(1,128)} custom-call(f32[512,128]{1,0:T(8,128)S(1)} %bitcast.4, f32[2688,128]{1,0:T(8,128)S(1)} %local_part.1.psi_ref.local_ref), custom_call_target="tpu_custom_call" | custom-call | tf_op jit(solution)/shard_map/gram/pallas_call | solution.py:821
  48.1 5.9 %all-to-all-start.2 = ((f32[32,1,2176]{2,1,0:T(1,128)}), f32[32,1,2176]{2,1,0:T(1,128)S(1)}, u32[]{:S(2)}, u32[]{:S(2)}) async-start(f32[32,1,2176]{2,1,0:T(1,128)} %gram.1), calls=%async_computation.2 | async-start | bytes 557056 | tf_op jit(solution)/shard_map/all_to_all | solution.py:989
  54.0 2.7 %correct.1 = f32[16,16,1024]{2,1,0:T(8,128)} custom-call(f32[512,128]{1,0:T(8,128)S(1)} %bitcast.5, f32[2688,128]{1,0:T(8,128)S(1)} %local_part.1.psi_ref.local_ref), custom_call_target="tpu_custom_call" | custom-call | flops 20000000 | bytes 2000000 | tf_op jit(solution)/shard_map/correct/pallas_call | solution.py:900
  56.7 8.0 %all-to-all-done.2.in_ref = f32[32,1,2176]{2,1,0:T(1,128)S(1)} async-done(((f32[32,1,2176]{2,1,0:T(1,128)}), f32[32,1,2176]{2,1,0:T(1,128)S(1)}, u32[]{:S(2)}, u32[]{:S(2)}) %all-to-all-start.2) | async-done | bytes 278560 | tf_op jit(solution)/shard_map/all_to_all | solution.py:989
  64.7 0.9 %total.1 = f32[64,64]{1,0:T(8,128)} custom-call(f32[32,1,2176]{2,1,0:T(1,128)S(1)} %all-to-all-done.2.in_ref), custom_call_target="tpu_custom_call" | custom-call | tf_op jit(solution)/shard_map/total/pallas_call | solution.py:939
  (7 shorter events, 0.0 us)
Async XLA Ops:
  0.6 1.2 %copy-start = (f32[16,16,1024]{2,1,0:T(8,128)S(1)}, f32[16,16,1024]{2,1,0:T(8,128)}, u32[]{:S(2)}) copy-start(f32[16,16,1024]{2,1,0:T(8,128)} %rho_any.1) | copy-start | bytes 3145732
  1.9 9.7 %copy-start.1 = (f32[16,16,1024]{2,1,0:T(8,128)S(1)}, f32[16,16,1024]{2,1,0:T(8,128)}, u32[]{:S(2)}) copy-start(f32[16,16,1024]{2,1,0:T(8,128)} %rho_any.1) | copy-start | bytes 3145732
  4.5 17.3 %all-to-all-start = ((f32[32,16,128]{2,1,0:T(8,128)}), f32[32,16,128]{2,1,0:T(8,128)S(1)}, u32[]{:S(2)}, u32[]{:S(2)}) async-start(f32[32,16,128]{2,1,0:T(8,128)} %bitcast), calls=%async_computation | async-start | bytes 524288 | tf_op jit(solution)/shard_map/all_to_all | solution.py:960
  11.7 16.0 %collective-permute-start = (f32[16,16,256]{2,1,0:T(8,128)S(1)}, f32[16,16,256]{2,1,0:T(8,128)S(1)}, u32[]{:S(2)}, u32[]{:S(2)}) collective-permute-start(f32[16,16,256]{2,1,0:T(8,128)S(1)} %get-tuple-element.9), channel_id=1, source_target_pairs={{0,1},{1,0},{2,3},{3,2},{4,5},{5,4},{6,7},{7,6},{8,9},{9,8},{10,11... | collective-permute-start | bytes 786440 | tf_op jit(solution)/shard_map/ppermute | solution.py:975
  13.1 14.6 %collective-permute-start.1 = (f32[16,16,256]{2,1,0:T(8,128)S(1)}, f32[16,16,256]{2,1,0:T(8,128)S(1)}, u32[]{:S(2)}, u32[]{:S(2)}) collective-permute-start(f32[16,16,256]{2,1,0:T(8,128)S(1)} %get-tuple-element.8), channel_id=1, source_target_pairs={{1,2},{2,1},{5,6},{6,5},{9,10},{10,9},{13,14},{14,13},{17,18},{18,... | collective-permute-start | bytes 786440 | tf_op jit(solution)/shard_map/ppermute | solution.py:974
  24.9 21.8 %all-to-all-start.1 = ((f32[32,16,128]{2,1,0:T(8,128)}), f32[32,16,128]{2,1,0:T(8,128)S(1)}, u32[]{:S(2)}, u32[]{:S(2)}) async-start(f32[32,16,128]{2,1,0:T(8,128)} %bitcast.2), calls=%async_computation.1 | async-start | bytes 524288 | tf_op jit(solution)/shard_map/all_to_all | solution.py:960
  28.5 5.0 %collective-permute-start.2 = (f32[16,32,128]{2,1,0:T(8,128)S(1)}, f32[16,32,128]{2,1,0:T(8,128)S(1)}, u32[]{:S(2)}, u32[]{:S(2)}) collective-permute-start(f32[16,32,128]{2,1,0:T(8,128)S(1)} %get-tuple-element.5), channel_id=1, source_target_pairs={{0,4},{4,0},{8,12},{12,8},{1,5},{5,1},{9,13},{13,9},{2,6},{6,2},{1... | collective-permute-start | bytes 786440 | tf_op jit(solution)/shard_map/ppermute | solution.py:980
  28.9 8.9 %collective-permute-start.3 = (f32[16,32,128]{2,1,0:T(8,128)S(1)}, f32[16,32,128]{2,1,0:T(8,128)S(1)}, u32[]{:S(2)}, u32[]{:S(2)}) collective-permute-start(f32[16,32,128]{2,1,0:T(8,128)S(1)} %get-tuple-element.6), channel_id=1, source_target_pairs={{4,8},{8,4},{5,9},{9,5},{6,10},{10,6},{7,11},{11,7},{20,24},{24,20... | collective-permute-start | bytes 786440 | tf_op jit(solution)/shard_map/ppermute | solution.py:981
  32.2 7.7 %collective-permute-start.4 = (f32[480,128]{1,0:T(8,128)S(1)}, f32[480,128]{1,0:T(8,128)S(1)}, u32[]{:S(2)}, u32[]{:S(2)}) collective-permute-start(f32[480,128]{1,0:T(8,128)S(1)} %get-tuple-element.7), channel_id=1, source_target_pairs={{0,16},{16,0},{1,17},{17,1},{2,18},{18,2},{3,19},{19,3},{4,20},{20... | collective-permute-start | bytes 737288 | tf_op jit(solution)/shard_map/ppermute | solution.py:982
  37.8 3.0 %collective-permute-start.5 = (f32[4,24,128]{2,1,0:T(8,128)S(1)}, f32[4,24,128]{2,1,0:T(8,128)S(1)}, u32[]{:S(2)}, u32[]{:S(2)}) collective-permute-start(f32[4,24,128]{2,1,0:T(8,128)S(1)} %edges.1), channel_id=1, source_target_pairs={{0,16},{16,0},{1,17},{17,1},{2,18},{18,2},{3,19},{19,3},{4,20},{20... | collective-permute-start | bytes 147464 | tf_op jit(solution)/shard_map/ppermute | solution.py:986
  48.1 16.6 %all-to-all-start.2 = ((f32[32,1,2176]{2,1,0:T(1,128)}), f32[32,1,2176]{2,1,0:T(1,128)S(1)}, u32[]{:S(2)}, u32[]{:S(2)}) async-start(f32[32,1,2176]{2,1,0:T(1,128)} %gram.1), calls=%async_computation.2 | async-start | bytes 557056 | tf_op jit(solution)/shard_map/all_to_all | solution.py:989
